TPU v7x, 32 devices: a whole 2x2x4 slice. The times are simulated.
32 devices in a mesh: rows: 8 (over z, x), half: 4 (over y, core).
Axes of the slice: x: 2, y: 2, z: 4, core: 2. Of those that a mesh axis runs over, the one named last changes fastest.
Arguments:
- micrograph: bfloat16 [4096, 4096], P('rows', 'half'), may hold values from -6 to 6
- box_tops: int32 [8, 4, 4, 2], replicated, may hold values from 0 to 3840, as said below
- box_live: int32 [8, 4, 4], replicated, may hold values from 0 to 1, as said below
- box_class: int32 [8, 4, 4], replicated, may hold values from 0 to 49
- box_shift: int32 [8, 4, 4, 2], P('rows', 'half'), may hold values from -8 to 8
Outputs:
- power: float32 [4, 1024, 4096], P('half', 'rows')
- class_means: float32 [50, 2, 256, 256], P(None, None, 'rows', 'half')
Inputs may be any that keep to these rules, and one draw needn't show every extreme that they name: `box_tops`: the box of every slot lies inside the micrograph. A slot of box_live = 1 at index (i, j, s) has its first row among rows i * 512 to (i + 1) * 512 - 1. `box_live`: in each device's slots the live ones come first; in every draw some device has all 4 slots live.
All inputs are finite; a program needn't handle non-finite values.
Results may differ from a plain program's by a relative error of at most 0.0029.
Values may be sent and summed in bfloat16 or wider, within the bound.
No kernel may reach another device: no remote copies, remote signals or barrier semaphores. Data moves between devices by JAX's collectives and lax.ppermute only.
A program may use at most 64 MiB of HBM per device.

v0:
```python
import jax
import jax.numpy as jnp
from jax import lax
from jax.sharding import PartitionSpec as P

BOX = 256
CLASSES = 50
RADIX = 64


highest = lax.Precision.HIGHEST


def passed_along(block, axis, distance):
    devices = range(lax.axis_size(axis))
    route = [(i - distance, i) for i in devices if i - distance in devices]
    return lax.ppermute(block, axis, route)


def phases(left_index, right_index, length):
    rotations = jnp.mod(left_index[:, None] * right_index[None, :], length)
    angles = 2.0 * jnp.pi / length * rotations.astype(jnp.float32)
    return (jnp.cos(angles), jnp.sin(angles))


def product(pattern, left_side, matrix):
    return jnp.einsum(pattern, left_side, matrix, precision=highest)


def four_step(real_part, imag_part, first_index, how_many, rows_last):
    height = real_part.shape[0]
    length = real_part.shape[1]
    outer_size = RADIX
    inner_size = length // outer_size
    real_part = real_part.reshape(height, outer_size, inner_size)
    spread = jnp.arange(outer_size, dtype=jnp.int32)
    across = jnp.arange(inner_size, dtype=jnp.int32)
    cos_one, sin_one = phases(spread, spread, outer_size)
    section_real = product("mab,ka->mkb", real_part, cos_one)
    section_imag = -product("mab,ka->mkb", real_part, sin_one)
    if imag_part is not None:
        imag_part = imag_part.reshape(height, outer_size, inner_size)
        section_real = section_real + product("mab,ka->mkb", imag_part, sin_one)
        section_imag = section_imag + product("mab,ka->mkb", imag_part, cos_one)
    twist_cos, twist_sin = phases(spread, across, length)
    turned_real = section_real * twist_cos + section_imag * twist_sin
    turned_imag = section_imag * twist_cos - section_real * twist_sin
    wanted = first_index + jnp.arange(how_many, dtype=jnp.int32)
    cos_two, sin_two = phases(wanted, across, inner_size)
    pattern = "mkb,tb->tkm" if rows_last else "mkb,tb->mtk"
    out_real = product(pattern, turned_real, cos_two) + product(pattern, turned_imag, sin_two)
    out_imag = product(pattern, turned_imag, cos_two) - product(pattern, turned_real, sin_two)
    return (out_real, out_imag)


def per_device(micrograph, box_tops, box_live, box_class, box_shift):
    row_index = lax.axis_index("rows")
    half_index = lax.axis_index("half")
    band_rows = lax.all_gather(micrograph, "half", axis=1, tiled=True)
    height = band_rows.shape[0]
    full_width = band_rows.shape[1]
    quarter = full_width // lax.axis_size("half")
    per_block = quarter // RADIX
    image_rows = band_rows.astype(jnp.float32)
    part_real, part_imag = four_step(image_rows, None, half_index * per_block, per_block, True)
    partial_value = jnp.stack(
        [part_real.reshape(quarter, height), part_imag.reshape(quarter, height)]
    )
    columns = lax.all_to_all(partial_value, "rows", split_axis=1, concat_axis=2, tiled=True)
    column_count = columns.shape[1]
    freq_real, freq_imag = four_step(columns[0], columns[1], 0, full_width // RADIX, False)
    power_out = (freq_real * freq_real + freq_imag * freq_imag).reshape(1, column_count, full_width)
    power_out = power_out / (full_width * full_width)
    local_tops = box_tops[row_index, half_index]
    start_rows = local_tops[:, 0] - row_index * height
    start_cols = local_tops[:, 1]
    reach_bands = (BOX + height - 2) // height

    def cut_columns(source, corner):
        return lax.dynamic_slice_in_dim(source, corner, BOX, 1)

    pieces = [jax.vmap(cut_columns, (None, 0))(band_rows, start_cols)]
    for offset in range(1, reach_bands + 1):
        target = jnp.maximum(row_index - offset, 0)
        their_cols = box_tops[target, half_index][:, 1]
        outgoing = jax.vmap(cut_columns, (None, 0))(band_rows, their_cols)
        pieces.append(passed_along(outgoing, "rows", -offset))
    windows = jnp.concatenate(pieces, axis=1)
    particle_boxes = jax.vmap(
        lambda window, corner: lax.dynamic_slice_in_dim(window, corner, BOX, 0)
    )(windows, start_rows)
    frequency = jnp.arange(BOX, dtype=jnp.int32)
    cos_box, sin_box = phases(frequency, frequency, BOX)
    local_offsets = box_shift.reshape(-1, 2)

    def spectrum(member):
        particle, offsets_pair = member
        values = particle.astype(jnp.float32)
        inner_real = jnp.dot(values, cos_box, precision=highest)
        inner_imag = -jnp.dot(values, sin_box, precision=highest)
        outer_real = (
            jnp.dot(cos_box, inner_real, precision=highest)
            + jnp.dot(sin_box, inner_imag, precision=highest)
        ) / BOX
        outer_imag = (
            jnp.dot(cos_box, inner_imag, precision=highest)
            - jnp.dot(sin_box, inner_real, precision=highest)
        ) / BOX
        rotations = jnp.mod(
            frequency[:, None] * offsets_pair[0] + frequency[None, :] * offsets_pair[1], BOX
        )
        angles = 2.0 * jnp.pi / BOX * rotations.astype(jnp.float32)
        ramp_cos = jnp.cos(angles)
        ramp_sin = jnp.sin(angles)
        shifted_real = outer_real * ramp_cos + outer_imag * ramp_sin
        shifted_imag = outer_imag * ramp_cos - outer_real * ramp_sin
        return jnp.stack([shifted_real, shifted_imag]).astype(jnp.bfloat16)

    spectra = lax.map(spectrum, (particle_boxes, local_offsets))
    classes_all = jnp.arange(CLASSES, dtype=jnp.int32)
    all_labels = box_class.reshape(-1)
    all_live = box_live.reshape(-1)
    counts = jnp.sum(
        (all_labels[None, :] == classes_all[:, None]).astype(jnp.int32) * all_live[None, :], axis=1
    )
    arrived = lax.all_to_all(spectra, "rows", split_axis=2, concat_axis=0, tiled=True)
    chosen_labels = box_class[:, half_index].reshape(-1)
    chosen_live = box_live[:, half_index].reshape(-1)
    weights = (
        (chosen_labels[None, :] == classes_all[:, None]).astype(jnp.int32) * chosen_live[None, :]
    ).astype(jnp.bfloat16)
    flat_spectra = arrived.reshape(arrived.shape[0], -1)
    partial_sums = jnp.dot(weights, flat_spectra, preferred_element_type=jnp.float32)
    partial_sums = partial_sums.reshape((CLASSES,) + arrived.shape[1:])
    class_sums = lax.psum_scatter(partial_sums, "half", scatter_dimension=3, tiled=True)
    divisor = jnp.maximum(counts, 1).astype(jnp.float32)
    class_means = class_sums / divisor[:, None, None, None]
    return (power_out, class_means)


def solution(mesh):
    in_specs = (P("rows", "half"), P(), P(), P(), P("rows", "half", None, None))
    out_specs = (P("half", "rows", None), P(None, None, "rows", "half"))
    return jax.shard_map(
        per_device, mesh=mesh, in_specs=in_specs, out_specs=out_specs, check_vma=False
    )
```

profile of v0, /device:TPU:0, one launch (start us, length us, event | category | flops | bytes accessed | tf_op | source)
XLA Modules:
  0.0 372.7 jit_solution(6000020585060962176)
XLA Ops:
  10.3 37.0 %all-gather.2.cloned.1.call-done = bf16[512,4096]{0,1:T(8,128)(2,1)} async-done(((bf16[512,1024]{0,1:T(8,128)(2,1)}), bf16[512,4096]{0,1:T(8,128)(2,1)}) %all-gather.2.cloned.1.call-update) | async-done | bytes 4194320 | tf_op jit(solution)/shard_map/all_gather | solution.py:59
  47.3 6.5 %copy.180 = bf16[512,4096]{1,0:T(8,128)(2,1)} copy(bf16[512,4096]{0,1:T(8,128)(2,1)} %all-gather.2.cloned.1.call-done) | data formatting | bytes 8388608
  53.9 9.6 %while.17 = (s32[]{:T(128)}, bf16[512,4096]{1,0:T(8,128)(2,1)}, s32[4,2]{0,1:T(2,128)S(1)}, bf16[4,512,256]{2,1,0:T(8,128)(2,1)S(1)}, s32[]{:T(128)}) while((s32[]{:T(128)}, bf16[512,4096]{1,0:T(8,128)(2,1)}, s32[4,2]{0,1:T(2,128)S(1)}, bf16[4,512,256]{2,1,0:T(8,128)(2,1)S(1)}, s32[]{:T(128)}) %tuple.91), condition=%wide.while_cond.1, body=%wide.while_body.1.sunk | while | flops 2 | bytes 524393 | solution.py:80
  64.4 9.6 %while.16 = (s32[]{:T(128)}, bf16[512,4096]{1,0:T(8,128)(2,1)}, s32[4,2]{0,1:T(2,128)S(1)}, bf16[4,512,256]{2,1,0:T(8,128)(2,1)S(1)}, s32[]{:T(128)}) while((s32[]{:T(128)}, bf16[512,4096]{1,0:T(8,128)(2,1)}, s32[4,2]{0,1:T(2,128)S(1)}, bf16[4,512,256]{2,1,0:T(8,128)(2,1)S(1)}, s32[]{:T(128)}) %tuple.104), condition=%wide.while_cond, body=%wide.while_body.sunk | while | flops 2 | bytes 524393 | solution.py:80
  75.6 9.1 %fusion.70 = f32[64,512,64]{1,0,2:T(8,128)S(1)} fusion(bf16[512,64,64]{0,2,1:T(8,128)(2,1)} %bitcast.150), kind=kOutput, calls=%fused_computation.87 | convolution fusion | flops 1610670080 | bytes 12582912 | tf_op jit(solution)/shard_map/mab,ka->mkb/dot_general | solution.py:27
  85.5 12.3 %add_bitcast_fusion = (f32[512,64,64]{0,1,2:T(8,128)}, f32[512,64,64]{0,1,2:T(8,128)}) fusion(f32[64,512,64]{1,0,2:T(8,128)S(1)} %fusion.70, f32[64,64]{0,1:T(8,128)S(1)} %copy.155, f32[64,64]{0,1:T(8,128)S(1)} %copy.153, bf16[512,64,64]{0,2,1:T(8,128)(2,1)S(1)} %bitcast.151), kind=kOutput, calls=%fused_computation.77 | convolution fusion | flops 1625350144 | bytes 29392896 | tf_op jit(solution)/shard_map/mab,ka->mkb/dot_general | solution.py:27
  97.8 3.3 collective-permute-done
  102.5 3.0 gather_fusion
  105.6 51.1 %while.18 = (s32[]{:T(128)}, bf16[4,2,256,256]{3,1,0,2:T(2,128)(2,1)}, bf16[4,256,256]{2,1,0:T(8,128)(2,1)S(1)}, s32[4,2]{0,1:T(2,128)S(1)}, s32[]{:T(128)}) while((s32[]{:T(128)}, bf16[4,2,256,256]{3,1,0,2:T(2,128)(2,1)}, bf16[4,256,256]{2,1,0:T(8,128)(2,1)S(1)}, s32[4,2]{0,1:T(2,128)S(1)}, s32[]{:T(128)}) %tuple.105), condition=%wide.region_1.2_spmd.clone.clone, body=%wide.region_0.1_spmd.clone.clone.sunk | while | flops 1215365632 | bytes 5247101 | solution.py:119
  156.7 5.7 %all-to-all-start.1 = ((bf16[4,2,256,256]{3,1,0,2:T(2,128)(2,1)}), bf16[4,2,256,256]{3,1,0,2:T(2,128)(2,1)S(1)}, u32[]{:S(2)}, u32[]{:S(2)}) async-start(bf16[4,2,256,256]{3,1,0,2:T(2,128)(2,1)} %get-tuple-element.107), calls=%async_computation.1 | async-start | bytes 2097152 | tf_op jit(solution)/shard_map/all_to_all | solution.py:126
  162.4 12.5 %fusion.62 = f32[16,512,64]{1,0,2:T(8,128)S(1)} fusion(f32[512,64,64]{0,1,2:T(8,128)} %get-tuple-element.255, s32[16]{0:T(128)S(1)} %iota_add_fusion), kind=kOutput, calls=%fused_computation.78 | convolution fusion | flops 402667520 | bytes 10485824 | tf_op jit(solution)/shard_map/mkb,tb->tkm/dot_general | solution.py:27
  174.9 13.2 %subtract_bitcast_fusion.2 = f32[16,64,512]{2,0,1:T(8,128)S(1)} fusion(f32[16,512,64]{1,0,2:T(8,128)S(1)} %fusion.62, f32[512,64,64]{0,1,2:T(8,128)} %get-tuple-element.254, s32[16]{0:T(128)S(1)} %iota_add_fusion), kind=kOutput, calls=%fused_computation.96 | convolution fusion | flops 403191808 | bytes 12582976 | tf_op jit(solution)/shard_map/mkb,tb->tkm/dot_general | solution.py:27
  189.3 8.7 %fusion.64 = f32[16,512,64]{1,0,2:T(8,128)S(1)} fusion(f32[512,64,64]{0,1,2:T(8,128)S(1)} %bitcast.149, s32[16]{0:T(128)S(1)} %iota_add_fusion), kind=kOutput, calls=%fused_computation.80 | convolution fusion | flops 402667520 | bytes 10485824 | tf_op jit(solution)/shard_map/mkb,tb->tkm/dot_general | solution.py:27
  198.0 9.1 %add_bitcast_fusion.2 = f32[16,64,512]{2,0,1:T(8,128)S(1)} fusion(f32[16,512,64]{1,0,2:T(8,128)S(1)} %fusion.64, f32[512,64,64]{0,1,2:T(8,128)S(1)} %bitcast.147, s32[16]{0:T(128)S(1)} %iota_add_fusion), kind=kOutput, calls=%fused_computation.97 | convolution fusion | flops 403191808 | bytes 12582976 | tf_op jit(solution)/shard_map/mkb,tb->tkm/dot_general | solution.py:27
  208.9 6.4 %copy.162 = f32[2,1024,512]{2,0,1:T(2,128)} copy(f32[2,1024,512]{2,1,0:T(8,128)S(1)} %pad_maximum_fusion.1) | data formatting | bytes 8388608 | tf_op jit(solution)/shard_map/stack | solution.py:66
  215.4 6.1 %all-to-all-start = ((f32[2,1024,512]{2,0,1:T(2,128)}), f32[2,1024,512]{2,0,1:T(2,128)}, u32[]{:S(2)}, u32[]{:S(2)}) async-start(f32[2,1024,512]{2,0,1:T(2,128)} %copy.162), calls=%async_computation | async-start | bytes 8388608 | tf_op jit(solution)/shard_map/all_to_all | solution.py:69
  223.0 2.6 fusion.101
  225.6 9.1 %copy.195 = f32[50,2,32,256]{0,2,1,3:T(8,128)} copy(f32[50,2,32,256]{3,0,2,1:T(8,128)} %fusion.101) | data formatting | bytes 6553600
  234.7 8.0 %reshape.188 = f32[256,3200]{1,0:T(8,128)} reshape(f32[256,2,32,50]{3,2,1,0:T(8,128)} %bitcast.152) | data formatting | bytes 6553600
  243.3 70.4 %all-to-all-done = f32[2,1024,512]{2,0,1:T(2,128)} async-done(((f32[2,1024,512]{2,0,1:T(2,128)}), f32[2,1024,512]{2,0,1:T(2,128)}, u32[]{:S(2)}, u32[]{:S(2)}) %all-to-all-start) | async-done | bytes 4194336 | tf_op jit(solution)/shard_map/all_to_all | solution.py:69
  313.7 3.0 copy.163
  316.7 2.7 fusion.221
  321.4 2.9 copy.166
  324.3 4.8 %fusion.82 = f32[64,128,64]{1,0,2:T(8,128)S(1)} fusion(f32[128,64,64]{0,2,1:T(8,128)} %bitcast.155), kind=kOutput, calls=%fused_computation.106 | convolution fusion | flops 402710528 | bytes 4194304 | tf_op jit(solution)/shard_map/mab,ka->mkb/dot_general | solution.py:27
  329.1 3.1 fusion.84
  332.2 3.3 negate_add_fusion
  335.5 4.7 %add_bitcast_fusion.1 = (f32[128,64,64]{0,1,2:T(8,128)S(1)}, f32[128,64,64]{0,1,2:T(8,128)S(1)}) fusion(f32[64,128,64]{1,0,2:T(8,128)S(1)} %negate_add_fusion, f32[64,64]{0,1:T(8,128)S(1)} %copy.155, f32[64,64]{0,1:T(8,128)S(1)} %copy.153, f32[64,128,64]{1,0,2:T(8,128)S(1)} %fusion.84, f32[128,64,64]{0,2,1:T(8,128)S(1)} %bitcast.154), kind=kOutput, calls=%fused_computation.94 | convolution fusion | flops 406380544 | bytes 10518528 | tf_op jit(solution)/shard_map/mab,ka->mkb/dot_general | solution.py:27
  340.2 3.1 fusion.74
  343.3 3.1 fusion.76
  346.4 3.1 fusion.78
  349.5 3.8 %multiply_bitcast_fusion = f32[128,64,64]{0,1,2:T(8,128)S(1)} fusion(f32[64,128,64]{1,0,2:T(8,128)S(1)} %fusion.74, f32[64,128,64]{1,0,2:T(8,128)S(1)} %fusion.78, f32[64,128,64]{1,0,2:T(8,128)S(1)} %fusion.76, f32[128,64,64]{0,1,2:T(8,128)S(1)} %get-tuple-element.256), kind=kOutput, calls=%fused_computation.92 | convolution fusion | flops 405856256 | bytes 10485760 | tf_op jit(solution)/shard_map/mkb,tb->mtk/dot_general | solution.py:27
  356.4 3.9 %reshape.189 = f32[64,2,32,50]{3,2,1,0:T(8,128)S(1)} reshape(f32[64,3200]{1,0:T(8,128)} %reduce-scatter.4.cloned.1.call-done) | data formatting | bytes 1638400
  (145 shorter events, 92.4 us)
Async XLA Ops:
  7.2 2.4 copy-start.5
  7.2 40.2 %all-gather.2.cloned.1.call-start = ((), (), s32[]{:S(2)}) async-start(), calls=%async_computation.3 | async-start | bytes 5242880 | tf_op jit(solution)/shard_map/all_gather | solution.py:59
  74.0 27.2 %collective-permute-start = (bf16[4,512,256]{2,0,1:T(4,128)(2,1)S(1)}, bf16[4,512,256]{2,0,1:T(4,128)(2,1)S(1)}, u32[]{:S(2)}, u32[]{:S(2)}) collective-permute-start(bf16[4,512,256]{2,0,1:T(4,128)(2,1)S(1)} %copy.183), channel_id=1, source_target_pairs={{4,0},{8,4},{12,8},{16,12},{20,16},{24,20},{28,24},{5,1},{9,5},{13... | collective-permute-start | bytes 3145736 | tf_op jit(solution)/shard_map/ppermute | solution.py:17
  75.6 9.9 %copy-start = (bf16[512,4096]{0,1:T(8,128)(2,1)S(1)}, bf16[512,4096]{0,1:T(8,128)(2,1)}, u32[]{:S(2)}) copy-start(bf16[512,4096]{0,1:T(8,128)(2,1)} %all-gather.2.cloned.1.call-done) | copy-start | bytes 12582916
  102.5 3.1 copy-start.2
  156.7 58.7 %all-to-all-start.1 = ((bf16[4,2,256,256]{3,1,0,2:T(2,128)(2,1)}), bf16[4,2,256,256]{3,1,0,2:T(2,128)(2,1)S(1)}, u32[]{:S(2)}, u32[]{:S(2)}) async-start(bf16[4,2,256,256]{3,1,0,2:T(2,128)(2,1)} %get-tuple-element.107), calls=%async_computation.1 | async-start | bytes 2097152 | tf_op jit(solution)/shard_map/all_to_all | solution.py:126
  162.4 26.9 %slice-start.2 = ((s8[8388608]{0:T(1024)(128)(4,1)}), s8[4194304]{0:T(1024)(128)(4,1)S(1)}, s32[]{:S(2)}) async-start(s8[8388608]{0:T(1024)(128)(4,1)} %bitcast.148), calls=%async_computation.7 | async-start | bytes 8388608
  174.9 14.4 %slice-start.3 = ((s8[8388608]{0:T(1024)(128)(4,1)}), s8[4194304]{0:T(1024)(128)(4,1)S(1)}, s32[]{:S(2)}) async-start(s8[8388608]{0:T(1024)(128)(4,1)} %bitcast.148), calls=%async_computation.8 | async-start | bytes 8388608
  174.9 23.1 %slice-start = ((s8[8388608]{0:T(1024)(128)(4,1)}), s8[4194304]{0:T(1024)(128)(4,1)S(1)}, s32[]{:S(2)}) async-start(s8[8388608]{0:T(1024)(128)(4,1)} %bitcast.146), calls=%async_computation.5 | async-start | bytes 8388608
  188.1 9.9 %slice-start.1 = ((s8[8388608]{0:T(1024)(128)(4,1)}), s8[4194304]{0:T(1024)(128)(4,1)S(1)}, s32[]{:S(2)}) async-start(s8[8388608]{0:T(1024)(128)(4,1)} %bitcast.146), calls=%async_computation.6 | async-start | bytes 8388608
  215.3 6.2 %copy-start.3 = (s32[8,4,4]{0,2,1:T(4,128)S(1)}, s32[8,4,4]{0,2,1:T(4,128)}, u32[]{:S(2)}) copy-start(s32[8,4,4]{0,2,1:T(4,128)} %param.9) | copy-start | bytes 1540
  215.3 6.2 %copy-start.4 = (s32[8,4,4]{0,2,1:T(4,128)S(1)}, s32[8,4,4]{0,2,1:T(4,128)}, u32[]{:S(2)}) copy-start(s32[8,4,4]{0,2,1:T(4,128)} %param.10) | copy-start | bytes 1540
  215.4 98.4 %all-to-all-start = ((f32[2,1024,512]{2,0,1:T(2,128)}), f32[2,1024,512]{2,0,1:T(2,128)}, u32[]{:S(2)}, u32[]{:S(2)}) async-start(f32[2,1024,512]{2,0,1:T(2,128)} %copy.162), calls=%async_computation | async-start | bytes 8388608 | tf_op jit(solution)/shard_map/all_to_all | solution.py:69
  221.5 134.9 %reduce-scatter.4.cloned.1.call-start = ((), (), s32[]{:S(2)}) async-start(), calls=%async_computation.4 | async-start | bytes 4096000
  324.3 4.8 %copy-start.1 = (f32[1,128,8,512]{1,3,2,0:T(8,128)S(1)}, f32[1,128,8,512]{1,3,2,0:T(8,128)}, u32[]{:S(2)}) copy-start(f32[1,128,8,512]{1,3,2,0:T(8,128)} %copy.166) | copy-start | bytes 6291460
Sparse Core Ops, SparseCore 0:
  10.1 37.1 all-gather.1
  242.9 39.1 reduce-scatter.3
where the time goes:
time: 377 us; the launch traced here: 373 us
  matrix products  134 us (36%)
  waiting for transfers between devices  111 us (29%)
  local copies, waits for them, and re-layouts  89 us (24%)
  between operations  14.7 us (4%)
  starting transfers between devices  13.5 us (4%)
  other arithmetic  9.44 us (3%)
    dot_general x14, matrix products, product(): return jnp.einsum(pattern, left_side, matrix, precision=highest)  93.8 us
    all_to_all x1, waiting for transfers between devices, per_device(): lax.all_to_all(partial_value, 'rows', split_axis=1, concat_axis=2, tiled=...  70.4 us
    all_gather x1, waiting for transfers between devices, per_device(): band_rows = lax.all_gather(micrograph, 'half', axis=1, tiled=True)  37 us
    unnamed x34, local copies, waits for them, and re-layouts  36 us
    gather x24, local copies, waits for them, and re-layouts  19 us
    dot_general x4, matrix products, spectrum(): jnp.dot(sin_box, inner_imag, precision=highest)  9.97 us
  transfers between devices with their start and end apart: 5, of which 3 were waited for; matrix products, arithmetic and copies ran while one was open for 38% of the time, Pallas kernels for 0%

commit v1 on v0

--- a/solution.py
+++ b/solution.py
@@ -1,12 +1,19 @@
+import functools
+
+import numpy as np
+
 import jax
 import jax.numpy as jnp
 from jax import lax
+from jax.experimental import pallas as pl
+from jax.experimental.pallas import tpu as pltpu
 from jax.sharding import PartitionSpec as P
 
 BOX = 256
 CLASSES = 50
 RADIX = 64
-
+LANES = 128
+POINTS = 16
 
 highest = lax.Precision.HIGHEST
 
@@ -53,7 +60,7 @@
     return (out_real, out_imag)
 
 
-def per_device(micrograph, box_tops, box_live, box_class, box_shift):
+def general_device(micrograph, box_tops, box_live, box_class, box_shift):
     row_index = lax.axis_index("rows")
     half_index = lax.axis_index("half")
     band_rows = lax.all_gather(micrograph, "half", axis=1, tiled=True)
@@ -138,9 +145,375 @@
     return (power_out, class_means)
 
 
+f32 = jnp.float32
+bf16 = jnp.bfloat16
+VMEM = pl.BlockSpec(memory_space=pltpu.VMEM)
+SMEM = pl.BlockSpec(memory_space=pltpu.SMEM)
+
+
+def call(kernel, out, operands, specs, scratch=(), flops=0):
+    moved = sum(a.size * a.dtype.itemsize for a in operands) + out.size * out.dtype.itemsize
+    return pl.pallas_call(
+        kernel,
+        out_shape=out,
+        in_specs=specs,
+        out_specs=VMEM,
+        scratch_shapes=list(scratch),
+        compiler_params=pltpu.CompilerParams(vmem_limit_bytes=48 * 1024 * 1024),
+        cost_estimate=pl.CostEstimate(flops=flops, bytes_accessed=moved, transcendentals=0),
+    )(*operands)
+
+
+def halves(table):
+    high = table.astype(bf16)
+    low = (table - high.astype(np.float64)).astype(bf16)
+    return high, low
+
+
+def waves(left, right, length):
+    angles = 2.0 * np.pi / length * np.mod(np.outer(left, right), length)
+    return np.cos(angles), np.sin(angles)
+
+
+def dft4(re, im):
+    sr, si = re[0] + re[2], im[0] + im[2]
+    dr, di = re[0] - re[2], im[0] - im[2]
+    tr, ti = re[1] + re[3], im[1] + im[3]
+    er, ei = re[1] - re[3], im[1] - im[3]
+    return [sr + tr, dr + ei, sr - tr, dr - ei], [si + ti, di - er, si - ti, di + er]
+
+
+def turn(re, im, step):
+    step = step % POINTS
+    if step == 0:
+        return re, im
+    if step == POINTS // 4:
+        return im, -re
+    c = float(np.cos(2.0 * np.pi * step / POINTS))
+    s = float(np.sin(2.0 * np.pi * step / POINTS))
+    if step == POINTS // 8:
+        return (re + im) * c, (im - re) * c
+    if step == 3 * POINTS // 8:
+        return (im - re) * s, (re + im) * -s
+    return re * c + im * s, im * c - re * s
+
+
+def dft16(re, im):
+    mid_re = [[None] * 4 for _ in range(4)]
+    mid_im = [[None] * 4 for _ in range(4)]
+    for n in range(4):
+        yr, yi = dft4([re[4 * p + n] for p in range(4)], [im[4 * p + n] for p in range(4)])
+        for k in range(4):
+            mid_re[k][n], mid_im[k][n] = turn(yr[k], yi[k], n * k)
+    out_re, out_im = [None] * POINTS, [None] * POINTS
+    for k in range(4):
+        yr, yi = dft4(mid_re[k], mid_im[k])
+        for m in range(4):
+            out_re[k + 4 * m], out_im[k + 4 * m] = yr[m], yi[m]
+    return out_re, out_im
+
+
+def dot(a, b):
+    return jnp.dot(a, b, preferred_element_type=f32)
+
+
+def prepare_kernel(n_half, x_ref, y_ref):
+    height, quarter = x_ref.shape
+    rows_each = height // POINTS
+    kept = POINTS // n_half
+    cols_each = quarter // POINTS
+    share = height // n_half
+    place = lax.broadcasted_iota(jnp.int32, (height, height), 0)
+    source = lax.broadcasted_iota(jnp.int32, (height, height), 1)
+    wanted = (place % rows_each) * POINTS + place // rows_each
+    pick_rows = jnp.where(source == wanted, 1.0, 0.0).astype(bf16)
+    ordered = dot(pick_rows, x_ref[...]).astype(bf16)
+    place = lax.broadcasted_iota(jnp.int32, (quarter, quarter), 0)
+    source = lax.broadcasted_iota(jnp.int32, (quarter, quarter), 1)
+    wanted = (place % cols_each) * POINTS + place // cols_each
+    pick_cols = jnp.where(source == wanted, 1.0, 0.0).astype(bf16)
+    turned = lax.dot_general(
+        pick_cols, ordered, (((1,), (1,)), ((), ())), preferred_element_type=f32
+    ).astype(bf16)
+    for j in range(n_half):
+        for c in range(POINTS):
+            y_ref[j, c] = turned[c * cols_each:(c + 1) * cols_each, j * share:(j + 1) * share]
+
+
+def rows_kernel(n_rows, n_half, y_ref, hi_ref, lo_ref, tc_ref, ts_ref, z_ref, re_ref, im_ref):
+    share = y_ref.shape[3]
+    kept = z_ref.shape[1]
+    span = z_ref.shape[3]
+
+    def first(c, carry):
+        block = jnp.concatenate([y_ref[j, c] for j in range(n_half)], axis=0).T
+        both = dot(block, hi_ref[...]) + dot(block, lo_ref[...])
+        re, im = both[:, :BOX], both[:, BOX:]
+        tc, ts = tc_ref[c], ts_ref[c]
+        re_ref[c] = re * tc + im * ts
+        im_ref[c] = im * tc - re * ts
+        return carry
+
+    lax.fori_loop(0, POINTS, first, 0)
+    tiles = span // 16
+
+    def second(t, carry):
+        m = t // tiles
+        at = pl.multiple_of((t % tiles) * 16, 16)
+        row = pl.multiple_of(t * 16, 16)
+        for h in range(BOX // LANES):
+            lanes = pl.ds(h * LANES, LANES)
+            re = [re_ref[c, pl.ds(row, 16), lanes] for c in range(POINTS)]
+            im = [im_ref[c, pl.ds(row, 16), lanes] for c in range(POINTS)]
+            re, im = dft16(re, im)
+            for v in range(POINTS):
+                slab = v * (BOX // LANES) + h
+                to = (slab % n_rows) * n_half + slab // n_rows
+                z_ref[to, m, 0, pl.ds(at, 16), :] = re[v].astype(bf16)
+                z_ref[to, m, 1, pl.ds(at, 16), :] = im[v].astype(bf16)
+        return carry
+
+    lax.fori_loop(0, share // 16, second, 0)
+
+
+def columns_kernel(n_rows, n_half, z_ref, ahi_ref, alo_ref, bhi_ref, blo_ref, tc_ref, ts_ref,
+                   o_ref, re_ref, im_ref):
+    kept = z_ref.shape[1]
+    count = o_ref.shape[0]
+
+    def first(r, carry):
+        j = r // kept
+        m = r % kept
+        real = jnp.concatenate([z_ref[i * n_half + j, m, 0] for i in range(n_rows)], axis=0).T
+        imag = jnp.concatenate([z_ref[i * n_half + j, m, 1] for i in range(n_rows)], axis=0).T
+        both = (dot(real, ahi_ref[...]) + dot(imag, bhi_ref[...])
+                + dot(real, alo_ref[...]) + dot(imag, blo_ref[...]))
+        re, im = both[:, :BOX], both[:, BOX:]
+        tc, ts = tc_ref[r], ts_ref[r]
+        re_ref[r] = re * tc + im * ts
+        im_ref[r] = im * tc - re * ts
+        return carry
+
+    lax.fori_loop(0, POINTS, first, 0)
+
+    def second(t, carry):
+        row = pl.multiple_of(t * 8, 8)
+        for h in range(BOX // LANES):
+            lanes = pl.ds(h * LANES, LANES)
+            re = [re_ref[c, pl.ds(row, 8), lanes] for c in range(POINTS)]
+            im = [im_ref[c, pl.ds(row, 8), lanes] for c in range(POINTS)]
+            re, im = dft16(re, im)
+            for u in range(POINTS):
+                o_ref[pl.ds(row, 8), pl.ds(u * BOX + h * LANES, LANES)] = re[u] * re[u] + im[u] * im[u]
+        return carry
+
+    lax.fori_loop(0, count // 8, second, 0)
+
+
+def pieces_kernel(at_ref, x_ref, low_ref, o_ref, ext_ref):
+    height, quarter = x_ref.shape
+    tall, wide = height // BOX, quarter // BOX
+    ext_ref[pl.ds(0, height), :] = x_ref[...]
+    ext_ref[pl.ds(height, BOX), :] = low_ref[...]
+    chunk = 64
+
+    def one(slot, carry):
+        top, left = at_ref[2 * slot], at_ref[2 * slot + 1]
+        tile_row = jnp.clip(top >> 8, 0, tall - 1)
+        tile_col = left >> 8
+        row_cut, col_cut = top & (BOX - 1), left & (BOX - 1)
+        here = jnp.logical_and(tile_col >= 0, tile_col < wide).astype(f32)
+        after = jnp.logical_and(tile_col >= -1, tile_col < wide - 1).astype(f32)
+        col_a = pl.multiple_of(jnp.clip(tile_col, 0, wide - 1) * BOX, BOX)
+        col_b = pl.multiple_of(jnp.clip(tile_col + 1, 0, wide - 1) * BOX, BOX)
+        right = lax.broadcasted_iota(jnp.int32, (chunk, BOX), 1) >= col_cut
+        rows = lax.broadcasted_iota(jnp.int32, (chunk, BOX), 0)
+        for k in range(BOX // chunk):
+            upper = pl.multiple_of(tile_row * BOX + k * chunk, chunk)
+            lower = pl.multiple_of(tile_row * BOX + BOX + k * chunk, chunk)
+
+            def across(first_row):
+                a = ext_ref[pl.ds(first_row, chunk), pl.ds(col_a, BOX)].astype(f32) * here
+                b = ext_ref[pl.ds(first_row, chunk), pl.ds(col_b, BOX)].astype(f32) * after
+                return jnp.where(right, a, b)
+
+            whole = jnp.where(rows + k * chunk >= row_cut, across(upper), across(lower))
+            o_ref[slot, pl.ds(k * chunk, chunk), :] = whole.astype(bf16)
+        return carry
+
+    lax.fori_loop(0, o_ref.shape[0], one, 0)
+
+
+def spectra_kernel(n_rows, n_half, roll_ref, p_ref, whi_ref, wlo_ref, chi_ref, clo_ref, o_ref):
+    slots = p_ref.shape[1]
+    wide = 2 * BOX
+    tall = BOX // n_rows
+    band = wide // n_half
+
+    def one(s, carry):
+        box = p_ref[0, s].astype(f32)
+        for j in range(1, n_half):
+            box = box + p_ref[j, s].astype(f32)
+        box = pltpu.roll(box, roll_ref[2 * s], 0)
+        box = pltpu.roll(box, roll_ref[2 * s + 1], 1).astype(bf16)
+        inner = dot(box, whi_ref[...]) + dot(box, wlo_ref[...])
+        high = inner.astype(bf16)
+        low = (inner - high.astype(f32)).astype(bf16)
+        high = jnp.concatenate([high[:, :wide], high[:, wide:]], axis=0)
+        low = jnp.concatenate([low[:, :wide], low[:, wide:]], axis=0)
+        outer = dot(chi_ref[...], high) + dot(chi_ref[...], low) + dot(clo_ref[...], high)
+        outer = outer.astype(bf16)
+        for i in range(n_rows):
+            for j in range(n_half):
+                o_ref[i * n_half + j, s] = outer[i * tall:(i + 1) * tall, j * band:(j + 1) * band]
+        return carry
+
+    lax.fori_loop(0, slots, one, 0)
+
+
+def means_kernel(label_ref, live_ref, f_ref, o_ref, sum_ref, count_ref):
+    slots = f_ref.shape[1]
+    half = f_ref.shape[3] // 2
+    sum_ref[...] = jnp.zeros_like(sum_ref)
+
+    def clear(k, carry):
+        count_ref[k] = 0
+        return carry
+
+    lax.fori_loop(0, CLASSES, clear, 0)
+
+    def add(g, carry):
+        for s in range(slots):
+            k = label_ref[g * slots + s]
+            live = live_ref[g * slots + s]
+            count_ref[k] = count_ref[k] + live
+            sum_ref[k] = sum_ref[k] + f_ref[g, s].astype(f32) * live.astype(f32)
+        return carry
+
+    lax.fori_loop(0, f_ref.shape[0], add, 0)
+
+    def finish(k, carry):
+        mean = sum_ref[k] / jnp.maximum(count_ref[k], 1).astype(f32)
+        o_ref[k, 0] = mean[:, :half]
+        o_ref[k, 1] = mean[:, half:]
+        return carry
+
+    lax.fori_loop(0, CLASSES, finish, 0)
+
+
+def fast_device(micrograph, box_tops, box_live, box_class, box_shift):
+    n_rows = lax.axis_size("rows")
+    n_half = lax.axis_size("half")
+    everyone = ("rows", "half")
+    total = n_rows * n_half
+    height, quarter = micrograph.shape
+    width = quarter * n_half
+    row_index = lax.axis_index("rows")
+    half_index = lax.axis_index("half")
+    kept = POINTS // n_half
+    span = height // POINTS
+    slab = quarter // n_rows
+    slots = box_tops.shape[2]
+    shape = jax.ShapeDtypeStruct
+
+    below = passed_along(micrograph[:BOX], "rows", -1)
+
+    points = np.arange(BOX)
+    cos_box, sin_box = waves(points, points, BOX)
+    first_hi, first_lo = halves(np.concatenate([cos_box, -sin_box], axis=1))
+    turned_hi, turned_lo = halves(np.concatenate([sin_box, cos_box], axis=1))
+    tc, ts = waves(np.arange(POINTS), points, width)
+    tc = tc.astype(np.float32)[:, None, :]
+    ts = ts.astype(np.float32)[:, None, :]
+
+    ready = call(
+        functools.partial(prepare_kernel, n_half),
+        shape((n_half, POINTS, quarter // POINTS, height // n_half), bf16),
+        [micrograph], [VMEM],
+        flops=2 * height * quarter * (height + quarter),
+    )
+    ready = lax.all_to_all(ready, "half", 0, 0, tiled=True)
+    mixed = call(
+        functools.partial(rows_kernel, n_rows, n_half),
+        shape((total, kept, 2, span, slab), bf16),
+        [ready, first_hi, first_lo, tc, ts], [VMEM] * 5,
+        scratch=[pltpu.VMEM((POINTS, height // n_half, BOX), f32)] * 2,
+        flops=4 * height * quarter * 2 * BOX,
+    )
+    mixed = lax.all_to_all(mixed, everyone, 0, 0, tiled=True)
+
+    corner = jnp.stack([row_index * height, half_index * quarter])
+    at = (box_tops[row_index] - corner).reshape(-1)
+    pieces = call(
+        pieces_kernel,
+        shape((n_half * slots, BOX, BOX), bf16),
+        [at, micrograph, below], [SMEM, VMEM, VMEM],
+        scratch=[pltpu.VMEM((height + BOX, quarter), bf16)],
+        flops=10 * n_half * slots * BOX * BOX,
+    )
+    pieces = lax.all_to_all(pieces, "half", 0, 0, tiled=True).reshape(n_half, slots, BOX, BOX)
+    part = BOX // n_half
+
+    def by_part(a, b):
+        a = a.reshape(-1, n_half, 1, part)
+        b = b.reshape(-1, n_half, 1, part)
+        return np.concatenate([a, b], axis=2).reshape(-1, 2 * BOX)
+
+    plain = by_part(cos_box, -sin_box)
+    swapped = by_part(-sin_box, -cos_box)
+    inner_hi, inner_lo = halves(np.concatenate([plain, swapped], axis=1) / BOX)
+    outer_hi, outer_lo = halves(np.concatenate([cos_box, sin_box], axis=1))
+    my_tops = box_tops[row_index, half_index]
+    rolls = jnp.mod(box_shift.reshape(slots, 2) - my_tops, BOX).reshape(-1)
+    spectra = call(
+        functools.partial(spectra_kernel, n_rows, n_half),
+        shape((total, slots, BOX // n_rows, 2 * part), bf16),
+        [rolls, pieces, inner_hi, inner_lo, outer_hi, outer_lo], [SMEM] + [VMEM] * 5,
+        flops=slots * BOX * BOX * 4 * BOX * 10,
+    )
+    spectra = lax.all_to_all(spectra, everyone, 0, 0, tiled=True)
+
+    power = call(
+        functools.partial(columns_kernel, n_rows, n_half),
+        shape((slab, width), f32),
+        [mixed, first_hi, first_lo, turned_hi, turned_lo, tc / width, ts / width], [VMEM] * 7,
+        scratch=[pltpu.VMEM((POINTS, slab, BOX), f32)] * 2,
+        flops=8 * slab * width * 2 * BOX,
+    )[None]
+    class_means = call(
+        means_kernel,
+        shape((CLASSES, 2, BOX // n_rows, part), f32),
+        [box_class.reshape(-1), box_live.reshape(-1), spectra], [SMEM, SMEM, VMEM],
+        scratch=[pltpu.VMEM((CLASSES, BOX // n_rows, 2 * part), f32), pltpu.SMEM((CLASSES,), jnp.int32)],
+        flops=4 * total * slots * BOX * BOX,
+    )
+    return (power, class_means)
+
+
+def fits(mesh, micrograph):
+    height, quarter = micrograph.shape
+    n_rows, n_half = mesh.shape["rows"], mesh.shape["half"]
+    return (
+        height * n_rows == POINTS * BOX
+        and quarter * n_half == POINTS * BOX
+        and POINTS % n_half == 0
+        and height % BOX == 0
+        and quarter % BOX == 0
+        and height // n_half == LANES
+        and quarter // n_rows == LANES
+        and BOX // n_rows % 16 == 0
+        and 2 * BOX // n_half == LANES
+    )
+
+
 def solution(mesh):
     in_specs = (P("rows", "half"), P(), P(), P(), P("rows", "half", None, None))
     out_specs = (P("half", "rows", None), P(None, None, "rows", "half"))
+
+    def per_device(micrograph, *boxes):
+        device = fast_device if fits(mesh, micrograph) else general_device
+        return device(micrograph, *boxes)
+
     return jax.shard_map(
         per_device, mesh=mesh, in_specs=in_specs, out_specs=out_specs, check_vma=False
     )

time: 377 us -> 166 us (0.44)
  matrix products: 134 us -> 0 us
  local copies, waits for them, and re-layouts: 89 us -> 12.9 us
  Pallas kernels: 0 us -> 30.5 us
  between operations: 14.7 us -> 0.87 us
  other arithmetic: 9.44 us -> 0.1 us
  waiting for transfers between devices: 111 us -> 104 us
    dot_general x39 -> x0, matrix products: 134 us -> none  [the longest x14 93.8 us: product(): return jnp.einsum(pattern, left_side, matrix, precision=highest)]
    all_gather x1 -> x0, waiting for transfers between devices: 37 us -> none  [per_device(): band_rows = lax.all_gather(micrograph, 'half', axis=1, tiled=True)]
    pallas_call x0 -> x6, Pallas kernels: none -> 30.5 us  [call(): pl.pallas_call(kernel, out_shape=out, in_specs=specs, out_specs=VMEM, scr...]
    unnamed x34 -> x47, local copies, waits for them, and re-layouts: 36 us -> 10.8 us
    gather x27 -> x0, local copies, waits for them, and re-layouts: 23.6 us -> none
    all_to_all x2 -> x4, waiting for transfers between devices: 70.4 us -> 89 us  [the longest x1 41.4 us: fast_device(): mixed = lax.all_to_all(mixed, everyone, 0, 0, tiled=True)]
    ppermute x1, waiting for transfers between devices: 3.35 us -> 14.7 us  [passed_along(): return lax.ppermute(block, axis, route)]
    slice x7 -> x1, local copies, waits for them, and re-layouts: 9.95 us -> 1.08 us  [fast_device(): below = passed_along(micrograph[:BOX], 'rows', -1)]
  transfers between devices with their start and end apart: 5 -> 5, of which waited for: 3 -> 5; matrix products, arithmetic and copies ran while one was open for 38% -> 1% of each run, Pallas kernels for 0% -> 11%
where the time goes in v1:
time: 166 us; the launch traced here: 165 us
  waiting for transfers between devices  104 us (63%)
  Pallas kernels  30.5 us (18%)
  starting transfers between devices  17.2 us (10%)
  local copies, waits for them, and re-layouts  12.9 us (8%)
    all_to_all x1, waiting for transfers between devices, fast_device(): mixed = lax.all_to_all(mixed, everyone, 0, 0, tiled=True)  41.4 us
    pallas_call x6, Pallas kernels, call(): pl.pallas_call(kernel, out_shape=out, in_specs=specs, out_specs=VMEM, scr...  30.5 us
    all_to_all x1, waiting for transfers between devices, fast_device(): lax.all_to_all(pieces, 'half', 0, 0, tiled=True)  22.8 us
    all_to_all x1, waiting for transfers between devices, fast_device(): spectra = lax.all_to_all(spectra, everyone, 0, 0, tiled=True)  19.7 us
    ppermute x1, waiting for transfers between devices, passed_along(): return lax.ppermute(block, axis, route)  14.7 us
    unnamed x47, local copies, waits for them, and re-layouts  10.8 us
    all_to_all x1, waiting for transfers between devices, fast_device(): ready = lax.all_to_all(ready, 'half', 0, 0, tiled=True)  5.04 us
    all_to_all x1, starting transfers between devices, fast_device(): spectra = lax.all_to_all(spectra, everyone, 0, 0, tiled=True)  5.02 us
  transfers between devices with their start and end apart: 5, of which 5 were waited for; matrix products, arithmetic and copies ran while one was open for 1% of the time, Pallas kernels for 11%

profile of v1, /device:TPU:0, one launch (start us, length us, event | category | flops | bytes accessed | tf_op | source)
XLA Modules:
  0.0 165.4 jit_solution(15011201799307712842)
XLA Ops:
  0.6 1.1 slice.3
  1.7 1.3 collective-permute-start
  3.0 0.4 dynamic-slice_reduce_fusion
  3.8 14.7 %collective-permute-done.low_ref = bf16[256,1024]{1,0:T(8,128)(2,1)S(1)} collective-permute-done((bf16[256,1024]{1,0:T(8,128)(2,1)S(1)}, bf16[256,1024]{1,0:T(8,128)(2,1)S(1)}, u32[]{:S(2)}, u32[]{:S(2)}) %collective-permute-start) | collective-permute-done | bytes 524320 | tf_op jit(solution)/shard_map/ppermute | solution.py:24
  18.5 1.2 copy-done.1
  19.7 3.9 %shard_map.179 = bf16[16,256,256]{2,1,0:T(8,128)(2,1)} custom-call(s32[32]{0:T(128)S(1)} %sub.22.at_ref, bf16[512,1024]{1,0:T(8,128)(2,1)S(1)} %copy-done.1, bf16[256,1024]{1,0:T(8,128)(2,1)S(1)} %collective-permute-done.low_ref), custom_call_target="tpu_custom_call" | custom-call | flops 10485760 | bytes 3670144 | tf_op jit(solution)/shard_map/pallas_call | solution.py:156
  23.6 3.7 %all-to-all-start.2 = ((bf16[16,256,256]{2,1,0:T(8,128)(2,1)}), bf16[16,256,256]{2,1,0:T(8,128)(2,1)S(1)}, u32[]{:S(2)}, u32[]{:S(2)}) async-start(bf16[16,256,256]{2,1,0:T(8,128)(2,1)} %shard_map.179), calls=%async_computation.2 | async-start | bytes 4194304 | tf_op jit(solution)/shard_map/all_to_all | solution.py:454
  27.4 1.8 %shard_map.176 = bf16[4,16,64,128]{3,2,1,0:T(8,128)(2,1)S(1)} custom-call(bf16[512,1024]{1,0:T(8,128)(2,1)S(1)} %copy-done.2), custom_call_target="tpu_custom_call" | custom-call | flops 1610612736 | bytes 2097152 | tf_op jit(solution)/shard_map/pallas_call | solution.py:156
  29.2 1.0 copy-done.4
  30.2 22.8 %all-to-all-done.2 = bf16[16,256,256]{2,1,0:T(8,128)(2,1)S(1)} async-done(((bf16[16,256,256]{2,1,0:T(8,128)(2,1)}), bf16[16,256,256]{2,1,0:T(8,128)(2,1)S(1)}, u32[]{:S(2)}, u32[]{:S(2)}) %all-to-all-start.2) | async-done | bytes 2097184 | tf_op jit(solution)/shard_map/all_to_all | solution.py:454
  53.0 3.5 %all-to-all-start = ((bf16[4,16,64,128]{3,2,1,0:T(8,128)(2,1)}), bf16[4,16,64,128]{3,2,1,0:T(8,128)(2,1)S(1)}, u32[]{:S(2)}, u32[]{:S(2)}) async-start(bf16[4,16,64,128]{3,2,1,0:T(8,128)(2,1)} %copy-done.4), calls=%async_computation | async-start | bytes 2097152 | tf_op jit(solution)/shard_map/all_to_all | solution.py:435
  56.9 1.0 copy-done.6
  58.0 1.0 copy-done.7
  59.0 0.9 copy-done.14
  59.9 4.9 %shard_map.180 = bf16[32,4,32,128]{3,2,1,0:T(8,128)(2,1)S(1)} custom-call(s32[8]{0:T(128)S(1)} %and_select_fusion.roll_ref, bf16[4,4,256,256]{3,2,1,0:T(8,128)(2,1)S(1)} %bitcast.4, bf16[256,1024]{1,0:T(8,128)(2,1)S(1)} %copy-done.6, bf16[256,1024]{1,0:T(8,128)(2,1)S(1)} %copy-done.7, bf16[256,512]{1,0:T(8,128)(2,1)S(1)} %copy-done.13, ...), custom_call_target="tpu_custom_call" | custom-call | flops 2684354560 | bytes 4718624 | tf_op jit(solution)/shard_map/pallas_call | solution.py:156
  64.9 1.0 copy-done.5
  65.9 5.0 %all-to-all-done.y_ref = bf16[4,16,64,128]{3,2,1,0:T(8,128)(2,1)S(1)} async-done(((bf16[4,16,64,128]{3,2,1,0:T(8,128)(2,1)}), bf16[4,16,64,128]{3,2,1,0:T(8,128)(2,1)S(1)}, u32[]{:S(2)}, u32[]{:S(2)}) %all-to-all-start) | async-done | bytes 1048608 | tf_op jit(solution)/shard_map/all_to_all | solution.py:435
  70.9 5.0 %all-to-all-start.3 = ((bf16[32,4,32,128]{3,2,1,0:T(8,128)(2,1)}), bf16[32,4,32,128]{3,2,1,0:T(8,128)(2,1)S(1)}, u32[]{:S(2)}, u32[]{:S(2)}) async-start(bf16[32,4,32,128]{3,2,1,0:T(8,128)(2,1)} %copy-done.5), calls=%async_computation.3 | async-start | bytes 2097152 | tf_op jit(solution)/shard_map/all_to_all | solution.py:474
  76.0 5.1 %shard_map.177 = bf16[32,4,2,32,128]{4,3,2,1,0:T(8,128)(2,1)S(1)} custom-call(bf16[4,16,64,128]{3,2,1,0:T(8,128)(2,1)S(1)} %all-to-all-done.y_ref, bf16[256,512]{1,0:T(8,128)(2,1)S(1)} %copy-done.8, bf16[256,512]{1,0:T(8,128)(2,1)S(1)} %copy-done.9, f32[16,1,256]{2,1,0:T(1,128)S(1)} %copy-done.17, f32[16,1,256]{2,1,0:T(1,128)S(1)} %copy-done.18), custom_call_target="tpu_custom_call" | custom-call | flops 1073741824 | bytes 3702784 | tf_op jit(solution)/shard_map/pallas_call | solution.py:156
  81.1 1.3 copy-done.3
  82.4 19.7 %all-to-all-done.3.f_ref = bf16[32,4,32,128]{3,2,1,0:T(8,128)(2,1)S(1)} async-done(((bf16[32,4,32,128]{3,2,1,0:T(8,128)(2,1)}), bf16[32,4,32,128]{3,2,1,0:T(8,128)(2,1)S(1)}, u32[]{:S(2)}, u32[]{:S(2)}) %all-to-all-start.3) | async-done | bytes 1048608 | tf_op jit(solution)/shard_map/all_to_all | solution.py:474
  102.2 3.6 %all-to-all-start.1 = ((bf16[32,4,2,32,128]{4,3,2,1,0:T(8,128)(2,1)}), bf16[32,4,2,32,128]{4,3,2,1,0:T(8,128)(2,1)S(1)}, u32[]{:S(2)}, u32[]{:S(2)}) async-start(bf16[32,4,2,32,128]{4,3,2,1,0:T(8,128)(2,1)} %copy-done.3), calls=%async_computation.1 | async-start | bytes 4194304 | tf_op jit(solution)/shard_map/all_to_all | solution.py:443
  105.8 0.1 copy.23
  105.9 0.1 reshape.22.label_ref
  106.0 0.1 copy.24
  106.1 0.1 reshape.23.live_ref
  106.3 6.8 %shard_map.181 = f32[50,2,32,64]{3,2,1,0:T(8,128)} custom-call(s32[128]{0:T(128)S(1)} %reshape.22.label_ref, s32[128]{0:T(128)S(1)} %reshape.23.live_ref, bf16[32,4,32,128]{3,2,1,0:T(8,128)(2,1)S(1)} %all-to-all-done.3.f_ref), custom_call_target="tpu_custom_call" | custom-call | flops 33554432 | bytes 1868800 | tf_op jit(solution)/shard_map/pallas_call | solution.py:156
  113.1 41.4 %all-to-all-done.1.z_ref = bf16[32,4,2,32,128]{4,3,2,1,0:T(8,128)(2,1)S(1)} async-done(((bf16[32,4,2,32,128]{4,3,2,1,0:T(8,128)(2,1)}), bf16[32,4,2,32,128]{4,3,2,1,0:T(8,128)(2,1)S(1)}, u32[]{:S(2)}, u32[]{:S(2)}) %all-to-all-start.1) | async-done | bytes 2097184 | tf_op jit(solution)/shard_map/all_to_all | solution.py:443
  154.5 0.9 copy-done.10
  155.5 0.9 copy-done.11
  156.4 0.9 copy-done.12
  157.4 8.0 %shard_map.178 = f32[128,4096]{1,0:T(8,128)} custom-call(bf16[32,4,2,32,128]{4,3,2,1,0:T(8,128)(2,1)S(1)} %all-to-all-done.1.z_ref, bf16[256,512]{1,0:T(8,128)(2,1)S(1)} %copy-done.8, bf16[256,512]{1,0:T(8,128)(2,1)S(1)} %copy-done.10, bf16[256,512]{1,0:T(8,128)(2,1)S(1)} %copy-done.11, bf16[256,512]{1,0:T(8,128)(2,1)S(1)} %copy-done.12, ...), custom_call_target="tpu_custom_call" | custom-call | flops 2147483648 | bytes 5275648 | tf_op jit(solution)/shard_map/pallas_call | solution.py:156
  (45 shorter events, 0.7 us)
Async XLA Ops:
  0.6 2.4 %copy-start = (s32[8,4,4,2]{0,3,2,1:T(2,128)S(1)}, s32[8,4,4,2]{0,3,2,1:T(2,128)}, u32[]{:S(2)}) copy-start(s32[8,4,4,2]{0,3,2,1:T(2,128)} %param.18) | copy-start | bytes 3076
  1.7 16.8 %collective-permute-start = (bf16[256,1024]{1,0:T(8,128)(2,1)S(1)}, bf16[256,1024]{1,0:T(8,128)(2,1)S(1)}, u32[]{:S(2)}, u32[]{:S(2)}) collective-permute-start(bf16[256,1024]{1,0:T(8,128)(2,1)S(1)} %slice.3), channel_id=1, source_target_pairs={{4,0},{8,4},{12,8},{16,12},{20,16},{24,20},{28,24},{5,1},{9,5},{13... | collective-permute-start | bytes 1572872 | tf_op jit(solution)/shard_map/ppermute | solution.py:24
  18.5 1.2 copy-start.1
  23.6 3.8 %copy-start.2 = (bf16[512,1024]{1,0:T(8,128)(2,1)S(1)}, bf16[512,1024]{1,0:T(8,128)(2,1)}, u32[]{:S(2)}) copy-start(bf16[512,1024]{1,0:T(8,128)(2,1)} %x_ref.3) | copy-start | bytes 3145732
  23.6 29.4 %all-to-all-start.2 = ((bf16[16,256,256]{2,1,0:T(8,128)(2,1)}), bf16[16,256,256]{2,1,0:T(8,128)(2,1)S(1)}, u32[]{:S(2)}, u32[]{:S(2)}) async-start(bf16[16,256,256]{2,1,0:T(8,128)(2,1)} %shard_map.179), calls=%async_computation.2 | async-start | bytes 4194304 | tf_op jit(solution)/shard_map/all_to_all | solution.py:454
  29.2 1.0 copy-start.4
  30.2 26.6 %copy-start.21 = (s32[1,1,4,2]{2,3,1,0:T(2,128)S(1)}, s32[1,1,4,2]{2,3,1,0:T(2,128)}, u32[]{:S(2)}) copy-start(s32[1,1,4,2]{2,3,1,0:T(2,128)} %param.21) | copy-start | bytes 100
  30.2 26.8 %copy-start.13 = (bf16[256,512]{1,0:T(8,128)(2,1)S(1)}, bf16[256,512]{1,0:T(8,128)(2,1)}, u32[]{:S(2)}) copy-start(bf16[256,512]{1,0:T(8,128)(2,1)} %constant.63.clone.chi_ref) | copy-start | bytes 786436
  53.0 17.9 %all-to-all-start = ((bf16[4,16,64,128]{3,2,1,0:T(8,128)(2,1)}), bf16[4,16,64,128]{3,2,1,0:T(8,128)(2,1)S(1)}, u32[]{:S(2)}, u32[]{:S(2)}) async-start(bf16[4,16,64,128]{3,2,1,0:T(8,128)(2,1)} %copy-done.4), calls=%async_computation | async-start | bytes 2097152 | tf_op jit(solution)/shard_map/all_to_all | solution.py:435
  56.9 1.0 copy-start.6
  58.0 1.0 copy-start.7
  59.0 0.9 copy-start.14
  64.9 1.0 copy-start.5
  65.9 10.1 %copy-start.8 = (bf16[256,512]{1,0:T(8,128)(2,1)S(1)}, bf16[256,512]{1,0:T(8,128)(2,1)}, u32[]{:S(2)}) copy-start(bf16[256,512]{1,0:T(8,128)(2,1)} %constant.57.clone.hi_ref.ahi_ref) | copy-start | bytes 786436
  65.9 10.1 %copy-start.9 = (bf16[256,512]{1,0:T(8,128)(2,1)S(1)}, bf16[256,512]{1,0:T(8,128)(2,1)}, u32[]{:S(2)}) copy-start(bf16[256,512]{1,0:T(8,128)(2,1)} %constant.58.clone.lo_ref.alo_ref) | copy-start | bytes 786436
  65.9 10.1 %copy-start.17 = (f32[16,1,256]{2,1,0:T(1,128)S(1)}, f32[16,1,256]{2,1,0:T(1,128)}, u32[]{:S(2)}) copy-start(f32[16,1,256]{2,1,0:T(1,128)} %constant.59.clone.tc_ref) | copy-start | bytes 49156
  65.9 10.1 %copy-start.18 = (f32[16,1,256]{2,1,0:T(1,128)S(1)}, f32[16,1,256]{2,1,0:T(1,128)}, u32[]{:S(2)}) copy-start(f32[16,1,256]{2,1,0:T(1,128)} %constant.60.clone.ts_ref) | copy-start | bytes 49156
  70.9 31.2 %all-to-all-start.3 = ((bf16[32,4,32,128]{3,2,1,0:T(8,128)(2,1)}), bf16[32,4,32,128]{3,2,1,0:T(8,128)(2,1)S(1)}, u32[]{:S(2)}, u32[]{:S(2)}) async-start(bf16[32,4,32,128]{3,2,1,0:T(8,128)(2,1)} %copy-done.5), calls=%async_computation.3 | async-start | bytes 2097152 | tf_op jit(solution)/shard_map/all_to_all | solution.py:474
  81.1 1.3 copy-start.3
  82.4 23.3 %copy-start.19 = (s32[8,4,4]{0,2,1:T(4,128)S(1)}, s32[8,4,4]{0,2,1:T(4,128)}, u32[]{:S(2)}) copy-start(s32[8,4,4]{0,2,1:T(4,128)} %param.20) | copy-start | bytes 1540
  82.4 23.6 %copy-start.20 = (s32[8,4,4]{0,2,1:T(4,128)S(1)}, s32[8,4,4]{0,2,1:T(4,128)}, u32[]{:S(2)}) copy-start(s32[8,4,4]{0,2,1:T(4,128)} %param.19) | copy-start | bytes 1540
  102.2 52.3 %all-to-all-start.1 = ((bf16[32,4,2,32,128]{4,3,2,1,0:T(8,128)(2,1)}), bf16[32,4,2,32,128]{4,3,2,1,0:T(8,128)(2,1)S(1)}, u32[]{:S(2)}, u32[]{:S(2)}) async-start(bf16[32,4,2,32,128]{4,3,2,1,0:T(8,128)(2,1)} %copy-done.3), calls=%async_computation.1 | async-start | bytes 4194304 | tf_op jit(solution)/shard_map/all_to_all | solution.py:443
  105.8 48.7 %copy-start.15 = (f32[16,1,256]{2,1,0:T(1,128)S(1)}, f32[16,1,256]{2,1,0:T(1,128)}, u32[]{:S(2)}) copy-start(f32[16,1,256]{2,1,0:T(1,128)} %constant.67.clone.tc_ref) | copy-start | bytes 49156
  105.8 48.7 %copy-start.16 = (f32[16,1,256]{2,1,0:T(1,128)S(1)}, f32[16,1,256]{2,1,0:T(1,128)}, u32[]{:S(2)}) copy-start(f32[16,1,256]{2,1,0:T(1,128)} %constant.68.clone.ts_ref) | copy-start | bytes 49156
  154.5 1.0 copy-start.10
  155.5 0.9 copy-start.11
  156.4 0.9 copy-start.12

commit v2 on v1

--- a/solution.py
+++ b/solution.py
@@ -316,6 +316,7 @@
     ext_ref[pl.ds(0, height), :] = x_ref[...]
     ext_ref[pl.ds(height, BOX), :] = low_ref[...]
     chunk = 64
+    slots = o_ref.shape[1]
 
     def one(slot, carry):
         top, left = at_ref[2 * slot], at_ref[2 * slot + 1]
@@ -338,22 +339,20 @@
                 return jnp.where(right, a, b)
 
             whole = jnp.where(rows + k * chunk >= row_cut, across(upper), across(lower))
-            o_ref[slot, pl.ds(k * chunk, chunk), :] = whole.astype(bf16)
-        return carry
-
-    lax.fori_loop(0, o_ref.shape[0], one, 0)
-
-
-def spectra_kernel(n_rows, n_half, roll_ref, p_ref, whi_ref, wlo_ref, chi_ref, clo_ref, o_ref):
-    slots = p_ref.shape[1]
+            o_ref[slot // slots, slot % slots, pl.ds(k * chunk, chunk), :] = whole.astype(bf16)
+        return carry
+
+    lax.fori_loop(0, o_ref.shape[0] * slots, one, 0)
+
+
+def spectra_kernel(n_rows, n_half, roll_ref, p_ref, q_ref, r_ref, whi_ref, wlo_ref, chi_ref, clo_ref, o_ref):
+    slots = q_ref.shape[0]
     wide = 2 * BOX
     tall = BOX // n_rows
     band = wide // n_half
 
     def one(s, carry):
-        box = p_ref[0, s].astype(f32)
-        for j in range(1, n_half):
-            box = box + p_ref[j, s].astype(f32)
+        box = p_ref[s].astype(f32) + q_ref[s].astype(f32) + r_ref[s].astype(f32)
         box = pltpu.roll(box, roll_ref[2 * s], 0)
         box = pltpu.roll(box, roll_ref[2 * s + 1], 1).astype(bf16)
         inner = dot(box, whi_ref[...]) + dot(box, wlo_ref[...])
@@ -371,34 +370,36 @@
     lax.fori_loop(0, slots, one, 0)
 
 
-def means_kernel(label_ref, live_ref, f_ref, o_ref, sum_ref, count_ref):
+def means_kernel(label_ref, live_ref, divisor_ref, f_ref, o_ref, *sum_refs):
     slots = f_ref.shape[1]
     half = f_ref.shape[3] // 2
-    sum_ref[...] = jnp.zeros_like(sum_ref)
-
-    def clear(k, carry):
-        count_ref[k] = 0
-        return carry
-
-    lax.fori_loop(0, CLASSES, clear, 0)
+    for sum_ref in sum_refs:
+        sum_ref[...] = jnp.zeros_like(sum_ref)
 
     def add(g, carry):
-        for s in range(slots):
+        for s, sum_ref in enumerate(sum_refs):
             k = label_ref[g * slots + s]
-            live = live_ref[g * slots + s]
-            count_ref[k] = count_ref[k] + live
-            sum_ref[k] = sum_ref[k] + f_ref[g, s].astype(f32) * live.astype(f32)
+            live = live_ref[g * slots + s].astype(f32)
+            sum_ref[k] = sum_ref[k] + f_ref[g, s].astype(f32) * live
         return carry
 
     lax.fori_loop(0, f_ref.shape[0], add, 0)
 
     def finish(k, carry):
-        mean = sum_ref[k] / jnp.maximum(count_ref[k], 1).astype(f32)
+        mean = sum_refs[0][k]
+        for sum_ref in sum_refs[1:]:
+            mean = mean + sum_ref[k]
+        mean = mean / divisor_ref[k]
         o_ref[k, 0] = mean[:, :half]
         o_ref[k, 1] = mean[:, half:]
         return carry
 
-    lax.fori_loop(0, CLASSES, finish, 0)
+    lax.fori_loop(0, o_ref.shape[0], finish, 0)
+
+
+def swapped(block, axis, bit):
+    route = [(i, i ^ bit) for i in range(lax.axis_size(axis))]
+    return lax.ppermute(block, axis, route)
 
 
 def fast_device(micrograph, box_tops, box_live, box_class, box_shift):
@@ -443,15 +444,17 @@
     mixed = lax.all_to_all(mixed, everyone, 0, 0, tiled=True)
 
     corner = jnp.stack([row_index * height, half_index * quarter])
-    at = (box_tops[row_index] - corner).reshape(-1)
+    owners = jnp.bitwise_xor(half_index, jnp.asarray(np.array([0, 2, 1, 3], np.int32)))
+    at = (box_tops[row_index][owners] - corner).reshape(-1)
     pieces = call(
         pieces_kernel,
-        shape((n_half * slots, BOX, BOX), bf16),
+        shape((n_half, slots, BOX, BOX), bf16),
         [at, micrograph, below], [SMEM, VMEM, VMEM],
         scratch=[pltpu.VMEM((height + BOX, quarter), bf16)],
         flops=10 * n_half * slots * BOX * BOX,
     )
-    pieces = lax.all_to_all(pieces, "half", 0, 0, tiled=True).reshape(n_half, slots, BOX, BOX)
+    beside = swapped(pieces[2:], "half", 1)
+    across = swapped(pieces[1] + beside[1], "half", 2)
     part = BOX // n_half
 
     def by_part(a, b):
@@ -460,17 +463,18 @@
         return np.concatenate([a, b], axis=2).reshape(-1, 2 * BOX)
 
     plain = by_part(cos_box, -sin_box)
-    swapped = by_part(-sin_box, -cos_box)
-    inner_hi, inner_lo = halves(np.concatenate([plain, swapped], axis=1) / BOX)
+    crossed = by_part(-sin_box, -cos_box)
+    inner_hi, inner_lo = halves(np.concatenate([plain, crossed], axis=1) / BOX)
     outer_hi, outer_lo = halves(np.concatenate([cos_box, sin_box], axis=1))
     my_tops = box_tops[row_index, half_index]
     rolls = jnp.mod(box_shift.reshape(slots, 2) - my_tops, BOX).reshape(-1)
     spectra = call(
         functools.partial(spectra_kernel, n_rows, n_half),
         shape((total, slots, BOX // n_rows, 2 * part), bf16),
-        [rolls, pieces, inner_hi, inner_lo, outer_hi, outer_lo], [SMEM] + [VMEM] * 5,
+        [rolls, pieces[0], beside[0], across, inner_hi, inner_lo, outer_hi, outer_lo], [SMEM] + [VMEM] * 7,
         flops=slots * BOX * BOX * 4 * BOX * 10,
     )
+    spectra, mixed = lax.optimization_barrier((spectra, mixed))
     spectra = lax.all_to_all(spectra, everyone, 0, 0, tiled=True)
 
     power = call(
@@ -480,11 +484,15 @@
         scratch=[pltpu.VMEM((POINTS, slab, BOX), f32)] * 2,
         flops=8 * slab * width * 2 * BOX,
     )[None]
+    labels, lives = box_class.reshape(-1), box_live.reshape(-1)
+    matches = labels[None, :] == jnp.arange(CLASSES, dtype=jnp.int32)[:, None]
+    counts = jnp.sum(jnp.where(matches, lives[None, :], 0), axis=1)
+    divisor = jnp.maximum(counts, 1).astype(f32)
     class_means = call(
         means_kernel,
         shape((CLASSES, 2, BOX // n_rows, part), f32),
-        [box_class.reshape(-1), box_live.reshape(-1), spectra], [SMEM, SMEM, VMEM],
-        scratch=[pltpu.VMEM((CLASSES, BOX // n_rows, 2 * part), f32), pltpu.SMEM((CLASSES,), jnp.int32)],
+        [labels, lives, divisor, spectra], [SMEM, SMEM, SMEM, VMEM],
+        scratch=[pltpu.VMEM((CLASSES, BOX // n_rows, 2 * part), f32)] * slots,
         flops=4 * total * slots * BOX * BOX,
     )
     return (power, class_means)
@@ -496,7 +504,7 @@
     return (
         height * n_rows == POINTS * BOX
         and quarter * n_half == POINTS * BOX
-        and POINTS % n_half == 0
+        and n_half == 4
         and height % BOX == 0
         and quarter % BOX == 0
         and height // n_half == LANES

time: 166 us -> 161 us (0.970)
  waiting for transfers between devices: 104 us -> 63 us
  blocking collectives: 0 us -> 18.6 us
  starting transfers between devices: 17.2 us -> 34 us
    all_to_all x1, waiting for transfers between devices: 41.4 us -> 0.01 us  [fast_device(): mixed = lax.all_to_all(mixed, everyone, 0, 0, tiled=True)]
    all_to_all x2 -> x0, waiting for transfers between devices: 27.9 us -> none  [the longest x1 22.8 us: fast_device(): lax.all_to_all(pieces, 'half', 0, 0, tiled=True)]
    all_to_all x1, starting transfers between devices: 5.02 us -> 27.6 us  [fast_device(): spectra = lax.all_to_all(spectra, everyone, 0, 0, tiled=True)]
    all_to_all x0 -> x1, blocking collectives: none -> 18.6 us  [fast_device(): ready = lax.all_to_all(ready, 'half', 0, 0, tiled=True)]
    ppermute x1, waiting for transfers between devices: 14.7 us -> 31.9 us  [passed_along(): return lax.ppermute(block, axis, route)]
    ppermute x0 -> x2, waiting for transfers between devices: none -> 16.3 us  [swapped(): return lax.ppermute(block, axis, route)]
    all_to_all x2 -> x0, starting transfers between devices: 7.26 us -> none  [the longest x1 3.74 us: fast_device(): lax.all_to_all(pieces, 'half', 0, 0, tiled=True)]
    all_to_all x1, waiting for transfers between devices: 19.7 us -> 14.7 us  [fast_device(): spectra = lax.all_to_all(spectra, everyone, 0, 0, tiled=True)]
  transfers between devices with their start and end apart: 5 -> 5, of which waited for: 5 -> 4; matrix products, arithmetic and copies ran while one was open for 1% -> 2% of each run, Pallas kernels for 11% -> 10%
where the time goes in v2:
time: 161 us
  waiting for transfers between devices  63 us (39%)
  starting transfers between devices  34 us (21%)
  Pallas kernels  29.7 us (18%)
  blocking collectives  18.6 us (12%)
  local copies, waits for them, and re-layouts  13.1 us (8%)
    ppermute x1, waiting for transfers between devices, passed_along(): return lax.ppermute(block, axis, route)  31.9 us
    pallas_call x6, Pallas kernels, call(): pl.pallas_call(kernel, out_shape=out, in_specs=specs, out_specs=VMEM, scr...  29.7 us
    all_to_all x1, starting transfers between devices, fast_device(): spectra = lax.all_to_all(spectra, everyone, 0, 0, tiled=True)  27.6 us
    all_to_all x1, blocking collectives, fast_device(): ready = lax.all_to_all(ready, 'half', 0, 0, tiled=True)  18.6 us
    ppermute x2, waiting for transfers between devices, swapped(): return lax.ppermute(block, axis, route)  16.3 us
    all_to_all x1, waiting for transfers between devices, fast_device(): spectra = lax.all_to_all(spectra, everyone, 0, 0, tiled=True)  14.7 us
    unnamed x47, local copies, waits for them, and re-layouts  10.7 us
    all_to_all x1, starting transfers between devices, fast_device(): mixed = lax.all_to_all(mixed, everyone, 0, 0, tiled=True)  4.89 us
  transfers between devices with their start and end apart: 5, of which 4 were waited for; matrix products, arithmetic and copies ran while one was open for 2% of the time, Pallas kernels for 10%

profile of v2, /device:TPU:0, one launch (start us, length us, event | category | flops | bytes accessed | tf_op | source)
XLA Modules:
  0.0 160.5 jit_solution(10219455271588263826)
XLA Ops:
  0.7 1.2 copy-done.1
  1.9 1.8 %shard_map.187 = bf16[4,16,64,128]{3,2,1,0:T(8,128)(2,1)S(1)} custom-call(bf16[512,1024]{1,0:T(8,128)(2,1)S(1)} %copy-done.1), custom_call_target="tpu_custom_call" | custom-call | flops 1610612736 | bytes 2097152 | tf_op jit(solution)/shard_map/pallas_call | solution.py:156
  3.7 18.6 %all_to_all.15.y_ref = bf16[4,16,64,128]{3,2,1,0:T(8,128)(2,1)S(1)} all-to-all(bf16[4,16,64,128]{3,2,1,0:T(8,128)(2,1)S(1)} %shard_map.187), channel_id=1, replica_groups=mesh['rows'=8,'half'=4] {'half'}, dimensions={0} | all-to-all | bytes 2097152 | tf_op jit(solution)/shard_map/all_to_all | solution.py:436
  22.4 5.1 %shard_map.188 = bf16[32,4,2,32,128]{4,3,2,1,0:T(8,128)(2,1)S(1)} custom-call(bf16[4,16,64,128]{3,2,1,0:T(8,128)(2,1)S(1)} %all_to_all.15.y_ref, bf16[256,512]{1,0:T(8,128)(2,1)S(1)} %copy-done.7, bf16[256,512]{1,0:T(8,128)(2,1)S(1)} %copy-done.8, f32[16,1,256]{2,1,0:T(1,128)S(1)} %copy-done.16, f32[16,1,256]{2,1,0:T(1,128)S(1)} %copy-done.17), custom_call_target="tpu_custom_call" | custom-call | flops 1073741824 | bytes 3702784 | tf_op jit(solution)/shard_map/pallas_call | solution.py:156
  27.5 1.3 copy-done.3
  28.8 4.9 %all-to-all-start.1 = ((bf16[32,4,2,32,128]{4,3,2,1,0:T(8,128)(2,1)}), bf16[32,4,2,32,128]{4,3,2,1,0:T(8,128)(2,1)S(1)}, u32[]{:S(2)}, u32[]{:S(2)}) async-start(bf16[32,4,2,32,128]{4,3,2,1,0:T(8,128)(2,1)} %copy-done.3), calls=%async_computation.1 | async-start | bytes 4194304 | tf_op jit(solution)/shard_map/all_to_all | solution.py:444
  33.8 0.8 slice.18
  34.6 1.3 collective-permute-start
  36.0 0.1 copy.42
  36.2 0.6 gather_fusion
  36.9 0.1 copy.45
  37.1 31.9 %collective-permute-done.low_ref = bf16[256,1024]{1,0:T(8,128)(2,1)} collective-permute-done((bf16[256,1024]{1,0:T(8,128)(2,1)}, bf16[256,1024]{1,0:T(8,128)(2,1)}, u32[]{:S(2)}, u32[]{:S(2)}) %collective-permute-start) | collective-permute-done | bytes 524320 | tf_op jit(solution)/shard_map/ppermute | solution.py:24
  69.0 3.0 %shard_map.185 = bf16[4,4,256,256]{3,2,1,0:T(8,128)(2,1)S(1)} custom-call(s32[32]{0:T(128)S(1)} %sub.23.at_ref, bf16[512,1024]{1,0:T(8,128)(2,1)S(1)} %copy-done.2, bf16[256,1024]{1,0:T(8,128)(2,1)} %collective-permute-done.low_ref), custom_call_target="tpu_custom_call" | custom-call | flops 10485760 | bytes 3670144 | tf_op jit(solution)/shard_map/pallas_call | solution.py:156
  72.2 2.6 %collective-permute-done.1 = bf16[2,4,256,256]{3,2,1,0:T(8,128)(2,1)S(1)} collective-permute-done((bf16[2,4,256,256]{3,2,1,0:T(8,128)(2,1)S(1)}, bf16[2,4,256,256]{3,2,1,0:T(8,128)(2,1)S(1)}, u32[]{:S(2)}, u32[]{:S(2)}) %collective-permute-start.1) | collective-permute-done | bytes 1048608 | tf_op jit(solution)/shard_map/ppermute | solution.py:402
  74.9 0.9 fusion
  75.8 0.2 collective-permute-start.2
  76.4 13.7 %collective-permute-done.2.r_ref = bf16[4,256,256]{2,1,0:T(8,128)(2,1)} collective-permute-done((bf16[4,256,256]{2,1,0:T(8,128)(2,1)}, bf16[4,256,256]{2,1,0:T(8,128)(2,1)}, u32[]{:S(2)}, u32[]{:S(2)}) %collective-permute-start.2) | collective-permute-done | bytes 524320 | tf_op jit(solution)/shard_map/ppermute | solution.py:402
  90.1 1.0 copy-done.5
  91.1 1.0 copy-done.6
  92.2 0.9 copy-done.12
  93.1 0.9 copy-done.13
  94.1 5.3 %shard_map.186 = bf16[32,4,32,128]{3,2,1,0:T(8,128)(2,1)S(1)} custom-call(s32[8]{0:T(128)S(1)} %and_select_fusion.roll_ref, bf16[4,256,256]{2,1,0:T(8,128)(2,1)S(1)} %get-tuple-element.7.p_ref, bf16[4,256,256]{2,1,0:T(8,128)(2,1)S(1)} %get-tuple-element.8.q_ref, bf16[4,256,256]{2,1,0:T(8,128)(2,1)} %collective-permute-done.2.r_ref, ...), custom_call_target="tpu_custom_call" | custom-call | flops 2684354560 | bytes 4194336 | tf_op jit(solution)/shard_map/pallas_call | solution.py:156
  99.4 1.0 copy-done.4
  100.4 27.6 %all-to-all-start.2 = ((bf16[32,4,32,128]{3,2,1,0:T(8,128)(2,1)}), bf16[32,4,32,128]{3,2,1,0:T(8,128)(2,1)S(1)}, u32[]{:S(2)}, u32[]{:S(2)}) async-start(bf16[32,4,32,128]{3,2,1,0:T(8,128)(2,1)} %copy-done.4), calls=%async_computation.2 | async-start | bytes 2097152 | tf_op jit(solution)/shard_map/all_to_all | solution.py:478
  128.1 0.1 reshape.23.label_ref
  128.3 0.1 reshape.24.live_ref
  128.6 0.9 copy-done.9
  129.5 0.9 copy-done.10
  130.5 0.9 copy-done.11
  131.4 8.0 %shard_map.189 = f32[128,4096]{1,0:T(8,128)} custom-call(bf16[32,4,2,32,128]{4,3,2,1,0:T(8,128)(2,1)S(1)} %all-to-all-done.1.z_ref, bf16[256,512]{1,0:T(8,128)(2,1)S(1)} %copy-done.7, bf16[256,512]{1,0:T(8,128)(2,1)S(1)} %copy-done.9, bf16[256,512]{1,0:T(8,128)(2,1)S(1)} %copy-done.10, bf16[256,512]{1,0:T(8,128)(2,1)S(1)} %copy-done.11, ...), custom_call_target="tpu_custom_call" | custom-call | flops 2147483648 | bytes 5275648 | tf_op jit(solution)/shard_map/pallas_call | solution.py:156
  139.4 14.7 %all-to-all-done.2.f_ref = bf16[32,4,32,128]{3,2,1,0:T(8,128)(2,1)S(1)} async-done(((bf16[32,4,32,128]{3,2,1,0:T(8,128)(2,1)}), bf16[32,4,32,128]{3,2,1,0:T(8,128)(2,1)S(1)}, u32[]{:S(2)}, u32[]{:S(2)}) %all-to-all-start.2) | async-done | bytes 1048608 | tf_op jit(solution)/shard_map/all_to_all | solution.py:478
  154.2 6.4 %shard_map.190 = f32[50,2,32,64]{3,2,1,0:T(8,128)} custom-call(s32[128]{0:T(128)S(1)} %reshape.23.label_ref, s32[128]{0:T(128)S(1)} %reshape.24.live_ref, f32[50]{0:T(128)S(1)} %maximum_convert_fusion.divisor_ref, bf16[32,4,32,128]{3,2,1,0:T(8,128)(2,1)S(1)} %all-to-all-done.2.f_ref), custom_call_target="tpu_custom_call" | custom-call | flops 33554432 | bytes 1869000 | tf_op jit(solution)/shard_map/pallas_call | solution.py:156
  (54 shorter events, 1.3 us)
Async XLA Ops:
  0.6 35.3 %copy-start = (s32[8,4,4,2]{0,3,2,1:T(2,128)S(1)}, s32[8,4,4,2]{0,3,2,1:T(2,128)}, u32[]{:S(2)}) copy-start(s32[8,4,4,2]{0,3,2,1:T(2,128)} %param.19) | copy-start | bytes 3076
  0.6 1.2 copy-start.1
  3.7 18.7 %copy-start.7 = (bf16[256,512]{1,0:T(8,128)(2,1)S(1)}, bf16[256,512]{1,0:T(8,128)(2,1)}, u32[]{:S(2)}) copy-start(bf16[256,512]{1,0:T(8,128)(2,1)} %constant.63.clone.hi_ref.ahi_ref) | copy-start | bytes 786436
  3.7 18.7 %copy-start.8 = (bf16[256,512]{1,0:T(8,128)(2,1)S(1)}, bf16[256,512]{1,0:T(8,128)(2,1)}, u32[]{:S(2)}) copy-start(bf16[256,512]{1,0:T(8,128)(2,1)} %constant.64.clone.lo_ref.alo_ref) | copy-start | bytes 786436
  3.7 18.7 %copy-start.16 = (f32[16,1,256]{2,1,0:T(1,128)S(1)}, f32[16,1,256]{2,1,0:T(1,128)}, u32[]{:S(2)}) copy-start(f32[16,1,256]{2,1,0:T(1,128)} %constant.65.clone.tc_ref) | copy-start | bytes 49156
  3.7 18.7 %copy-start.17 = (f32[16,1,256]{2,1,0:T(1,128)S(1)}, f32[16,1,256]{2,1,0:T(1,128)}, u32[]{:S(2)}) copy-start(f32[16,1,256]{2,1,0:T(1,128)} %constant.66.clone.ts_ref) | copy-start | bytes 49156
  27.5 1.3 copy-start.3
  28.8 4.9 %copy-start.2 = (bf16[512,1024]{1,0:T(8,128)(2,1)S(1)}, bf16[512,1024]{1,0:T(8,128)(2,1)}, u32[]{:S(2)}) copy-start(bf16[512,1024]{1,0:T(8,128)(2,1)} %x_ref.3) | copy-start | bytes 3145732
  28.8 7.0 %copy-start.21 = (s32[4]{0:T(128)S(1)}, s32[4]{0:T(128)}, u32[]{:S(2)}) copy-start(s32[4]{0:T(128)} %constant.67.clone) | copy-start | bytes 52
  28.8 71.5 %all-to-all-start.1 = ((bf16[32,4,2,32,128]{4,3,2,1,0:T(8,128)(2,1)}), bf16[32,4,2,32,128]{4,3,2,1,0:T(8,128)(2,1)S(1)}, u32[]{:S(2)}, u32[]{:S(2)}) async-start(bf16[32,4,2,32,128]{4,3,2,1,0:T(8,128)(2,1)} %copy-done.3), calls=%async_computation.1 | async-start | bytes 4194304 | tf_op jit(solution)/shard_map/all_to_all | solution.py:444
  34.6 34.4 %collective-permute-start = (bf16[256,1024]{1,0:T(8,128)(2,1)}, bf16[256,1024]{1,0:T(8,128)(2,1)}, u32[]{:S(2)}, u32[]{:S(2)}) collective-permute-start(bf16[256,1024]{1,0:T(8,128)(2,1)} %slice.18), channel_id=1, source_target_pairs={{4,0},{8,4},{12,8},{16,12},{20,16},{24,20},{28,24},{5,1},{9,5},{13... | collective-permute-start | bytes 1572872 | tf_op jit(solution)/shard_map/ppermute | solution.py:24
  72.1 4.0 %copy-start.20 = (s32[1,1,4,2]{2,3,1,0:T(2,128)S(1)}, s32[1,1,4,2]{2,3,1,0:T(2,128)}, u32[]{:S(2)}) copy-start(s32[1,1,4,2]{2,3,1,0:T(2,128)} %param.22) | copy-start | bytes 100
  72.2 2.7 %collective-permute-start.1 = (bf16[2,4,256,256]{3,2,1,0:T(8,128)(2,1)S(1)}, bf16[2,4,256,256]{3,2,1,0:T(8,128)(2,1)S(1)}, u32[]{:S(2)}, u32[]{:S(2)}) collective-permute-start(bf16[2,4,256,256]{3,2,1,0:T(8,128)(2,1)S(1)} %slice.27), channel_id=1, source_target_pairs={{0,1},{1,0},{2,3},{3,2},{4,5},{5,4},{6,7},{7,6},{8,9},{9,8},{10,11... | collective-permute-start | bytes 3145736 | tf_op jit(solution)/shard_map/ppermute | solution.py:402
  75.8 14.3 %collective-permute-start.2 = (bf16[4,256,256]{2,1,0:T(8,128)(2,1)}, bf16[4,256,256]{2,1,0:T(8,128)(2,1)}, u32[]{:S(2)}, u32[]{:S(2)}) collective-permute-start(bf16[4,256,256]{2,1,0:T(8,128)(2,1)} %get-tuple-element.6), channel_id=1, source_target_pairs={{0,2},{1,3},{2,0},{3,1},{4,6},{5,7},{6,4},{7,5},{8,10},{9,11},{10,... | collective-permute-start | bytes 1572872 | tf_op jit(solution)/shard_map/ppermute | solution.py:402
  90.1 1.0 copy-start.5
  91.1 1.0 copy-start.6
  92.2 0.9 copy-start.12
  93.1 0.9 copy-start.13
  99.4 1.0 copy-start.4
  100.4 27.6 %copy-start.18 = (s32[8,4,4]{0,2,1:T(4,128)S(1)}, s32[8,4,4]{0,2,1:T(4,128)}, u32[]{:S(2)}) copy-start(s32[8,4,4]{0,2,1:T(4,128)} %param.21) | copy-start | bytes 1540
  100.4 27.8 %copy-start.19 = (s32[8,4,4]{0,2,1:T(4,128)S(1)}, s32[8,4,4]{0,2,1:T(4,128)}, u32[]{:S(2)}) copy-start(s32[8,4,4]{0,2,1:T(4,128)} %param.20) | copy-start | bytes 1540
  100.4 28.2 %copy-start.14 = (f32[16,1,256]{2,1,0:T(1,128)S(1)}, f32[16,1,256]{2,1,0:T(1,128)}, u32[]{:S(2)}) copy-start(f32[16,1,256]{2,1,0:T(1,128)} %constant.74.clone.tc_ref) | copy-start | bytes 49156
  100.4 28.2 %copy-start.15 = (f32[16,1,256]{2,1,0:T(1,128)S(1)}, f32[16,1,256]{2,1,0:T(1,128)}, u32[]{:S(2)}) copy-start(f32[16,1,256]{2,1,0:T(1,128)} %constant.75.clone.ts_ref) | copy-start | bytes 49156
  100.4 53.8 %all-to-all-start.2 = ((bf16[32,4,32,128]{3,2,1,0:T(8,128)(2,1)}), bf16[32,4,32,128]{3,2,1,0:T(8,128)(2,1)S(1)}, u32[]{:S(2)}, u32[]{:S(2)}) async-start(bf16[32,4,32,128]{3,2,1,0:T(8,128)(2,1)} %copy-done.4), calls=%async_computation.2 | async-start | bytes 2097152 | tf_op jit(solution)/shard_map/all_to_all | solution.py:478
  128.6 1.0 copy-start.9
  129.5 0.9 copy-start.10
  130.5 0.9 copy-start.11

commit v3 on v2

--- a/solution.py
+++ b/solution.py
@@ -8,6 +8,7 @@
 from jax.experimental import pallas as pl
 from jax.experimental.pallas import tpu as pltpu
 from jax.sharding import PartitionSpec as P
+
 
 BOX = 256
 CLASSES = 50
@@ -145,19 +146,22 @@
     return (power_out, class_means)
 
 
+GROUP = 4
 f32 = jnp.float32
 bf16 = jnp.bfloat16
 VMEM = pl.BlockSpec(memory_space=pltpu.VMEM)
 SMEM = pl.BlockSpec(memory_space=pltpu.SMEM)
+HBM = pl.BlockSpec(memory_space=pltpu.HBM)
 
 
 def call(kernel, out, operands, specs, scratch=(), flops=0):
-    moved = sum(a.size * a.dtype.itemsize for a in operands) + out.size * out.dtype.itemsize
+    made = out if isinstance(out, tuple) else (out,)
+    moved = sum(a.size * a.dtype.itemsize for a in (*operands, *made))
     return pl.pallas_call(
         kernel,
         out_shape=out,
         in_specs=specs,
-        out_specs=VMEM,
+        out_specs=(VMEM,) * len(out) if isinstance(out, tuple) else VMEM,
         scratch_shapes=list(scratch),
         compiler_params=pltpu.CompilerParams(vmem_limit_bytes=48 * 1024 * 1024),
         cost_estimate=pl.CostEstimate(flops=flops, bytes_accessed=moved, transcendentals=0),
@@ -213,6 +217,13 @@
     return out_re, out_im
 
 
+def fetch(*pairs):
+    copies = [pltpu.make_async_copy(source, target, sem) for source, target, sem in pairs]
+    for copy in copies:
+        copy.start()
+    return copies
+
+
 def dot(a, b):
     return jnp.dot(a, b, preferred_element_type=f32)
 
@@ -220,7 +231,6 @@
 def prepare_kernel(n_half, x_ref, y_ref):
     height, quarter = x_ref.shape
     rows_each = height // POINTS
-    kept = POINTS // n_half
     cols_each = quarter // POINTS
     share = height // n_half
     place = lax.broadcasted_iota(jnp.int32, (height, height), 0)
@@ -240,21 +250,33 @@
             y_ref[j, c] = turned[c * cols_each:(c + 1) * cols_each, j * share:(j + 1) * share]
 
 
-def rows_kernel(n_rows, n_half, y_ref, hi_ref, lo_ref, tc_ref, ts_ref, z_ref, re_ref, im_ref):
+def rows_kernel(n_rows, n_half, y_ref, w_hbm, t_hbm, z_ref, re_ref, im_ref, w_ref, t_ref, sems):
+    copies = fetch((w_hbm, w_ref, sems.at[0]), (t_hbm, t_ref, sems.at[1]))
     share = y_ref.shape[3]
-    kept = z_ref.shape[1]
-    span = z_ref.shape[3]
-
-    def first(c, carry):
-        block = jnp.concatenate([y_ref[j, c] for j in range(n_half)], axis=0).T
-        both = dot(block, hi_ref[...]) + dot(block, lo_ref[...])
-        re, im = both[:, :BOX], both[:, BOX:]
-        tc, ts = tc_ref[c], ts_ref[c]
-        re_ref[c] = re * tc + im * ts
-        im_ref[c] = im * tc - re * ts
+    span = z_ref.shape[2]
+    half = LANES // 2
+    lane = lax.broadcasted_iota(jnp.int32, (16, LANES), 1)
+
+    for copy in copies:
+        copy.wait()
+
+    def first(g, carry):
+        blocks = [
+            jnp.concatenate([y_ref[j, g * GROUP + k] for j in range(n_half)], axis=0)
+            for k in range(GROUP)
+        ]
+        block = jnp.concatenate(blocks, axis=1).T
+        both = dot(block, w_ref[0]) + dot(block, w_ref[1])
+        for k in range(GROUP):
+            c = g * GROUP + k
+            part = both[k * share:(k + 1) * share]
+            re, im = part[:, :BOX], part[:, BOX:]
+            tc, ts = t_ref[0, c], t_ref[1, c]
+            re_ref[c] = re * tc + im * ts
+            im_ref[c] = im * tc - re * ts
         return carry
 
-    lax.fori_loop(0, POINTS, first, 0)
+    lax.fori_loop(0, POINTS // GROUP, first, 0)
     tiles = span // 16
 
     def second(t, carry):
@@ -269,34 +291,58 @@
             for v in range(POINTS):
                 slab = v * (BOX // LANES) + h
                 to = (slab % n_rows) * n_half + slab // n_rows
-                z_ref[to, m, 0, pl.ds(at, 16), :] = re[v].astype(bf16)
-                z_ref[to, m, 1, pl.ds(at, 16), :] = im[v].astype(bf16)
+                imag = pltpu.roll(im[v], half, 1)
+                if 2 * slab < n_rows * n_half:
+                    both = jnp.where(lane < half, re[v], imag)
+                else:
+                    both = jnp.where(lane < half, re[v], jnp.where(lane == half, im[v], imag))
+                    both = jnp.where(lane == 0, pltpu.roll(re[v], half, 1), both)
+                if slab == 0:
+                    both = jnp.where(lane == half, pltpu.roll(re[POINTS // 2], half, 1), both)
+                z_ref[to, m, pl.ds(at, 16), :] = both.astype(bf16)
         return carry
 
     lax.fori_loop(0, share // 16, second, 0)
 
 
-def columns_kernel(n_rows, n_half, z_ref, ahi_ref, alo_ref, bhi_ref, blo_ref, tc_ref, ts_ref,
-                   o_ref, re_ref, im_ref):
+def columns_kernel(n_rows, n_half, place_ref, z_ref, w_hbm, t_hbm, own_ref, far_ref, edge_ref,
+                   re_ref, im_ref, mre_ref, mim_ref, mirror_ref, raw_ref, w_ref, t_ref, sems):
+    copies = fetch((w_hbm, w_ref, sems.at[0]), (t_hbm, t_ref, sems.at[1]))
     kept = z_ref.shape[1]
-    count = o_ref.shape[0]
-
-    def first(r, carry):
-        j = r // kept
-        m = r % kept
-        real = jnp.concatenate([z_ref[i * n_half + j, m, 0] for i in range(n_rows)], axis=0).T
-        imag = jnp.concatenate([z_ref[i * n_half + j, m, 1] for i in range(n_rows)], axis=0).T
-        both = (dot(real, ahi_ref[...]) + dot(imag, bhi_ref[...])
-                + dot(real, alo_ref[...]) + dot(imag, blo_ref[...]))
-        re, im = both[:, :BOX], both[:, BOX:]
-        tc, ts = tc_ref[r], ts_ref[r]
-        re_ref[r] = re * tc + im * ts
-        im_ref[r] = im * tc - re * ts
+    count = own_ref.shape[0]
+    width = own_ref.shape[1]
+
+    for copy in copies:
+        copy.wait()
+
+    def first(g, carry):
+        blocks = []
+        for k in range(GROUP):
+            r = g * GROUP + k
+            j, m = r // kept, r % kept
+            blocks.append(
+                jnp.concatenate([z_ref[i * n_half + j, m] for i in range(n_rows)], axis=0)
+            )
+        block = jnp.concatenate(blocks, axis=1).T
+        product = dot(block, w_ref[0]) + dot(block, w_ref[1])
+        for k in range(GROUP):
+            r = g * GROUP + k
+            both = product[2 * count * k:2 * count * (k + 1)]
+            a, b = both[:count, :BOX], both[count:, :BOX]
+            c, d = both[:count, BOX:], both[count:, BOX:]
+            tc, ts = t_ref[0, r], t_ref[1, r]
+            re, im = a - d, b + c
+            re_ref[r] = re * tc + im * ts
+            im_ref[r] = im * tc - re * ts
+            tc, ts = t_ref[2, r], t_ref[3, r]
+            re, im = a + d, b - c
+            mre_ref[r] = re * tc + im * ts
+            mim_ref[r] = im * tc - re * ts
         return carry
 
-    lax.fori_loop(0, POINTS, first, 0)
-
-    def second(t, carry):
+    lax.fori_loop(0, POINTS // GROUP, first, 0)
+
+    def tile(t, raw):
         row = pl.multiple_of(t * 8, 8)
         for h in range(BOX // LANES):
             lanes = pl.ds(h * LANES, LANES)
@@ -304,29 +350,78 @@
             im = [im_ref[c, pl.ds(row, 8), lanes] for c in range(POINTS)]
             re, im = dft16(re, im)
             for u in range(POINTS):
-                o_ref[pl.ds(row, 8), pl.ds(u * BOX + h * LANES, LANES)] = re[u] * re[u] + im[u] * im[u]
+                to = pl.ds(u * BOX + h * LANES, LANES)
+                if raw:
+                    raw_ref[0, :, to], raw_ref[1, :, to] = re[u], im[u]
+                else:
+                    own_ref[pl.ds(row, 8), to] = re[u] * re[u] + im[u] * im[u]
+            re = [mre_ref[c, pl.ds(row, 8), lanes] for c in range(POINTS)]
+            im = [mim_ref[c, pl.ds(row, 8), lanes] for c in range(POINTS)]
+            re, im = dft16(re, im)
+            for u in range(POINTS):
+                to = pl.ds((POINTS - 1 - u) * BOX + h * LANES, LANES)
+                if raw:
+                    raw_ref[2, :, to], raw_ref[3, :, to] = re[u], im[u]
+                else:
+                    mirror_ref[pl.ds(row, 8), to] = re[u] * re[u] + im[u] * im[u]
+
+    def second(t, carry):
+        tile(t, False)
         return carry
 
     lax.fori_loop(0, count // 8, second, 0)
-
-
-def pieces_kernel(at_ref, x_ref, low_ref, o_ref, ext_ref):
+    tile(0, True)
+    origin = place_ref[0] == 0
+    for k in range(width // LANES):
+        to = pl.ds(k * LANES, LANES)
+        re, im, mre, mim = (raw_ref[n, 0:1, to] for n in range(4))
+        even = 0.25 * ((re + mre) * (re + mre) + (im - mim) * (im - mim))
+        odd = 0.25 * ((re - mre) * (re - mre) + (im + mim) * (im + mim))
+        own_ref[0:1, to] = jnp.where(origin, even, own_ref[0:1, to])
+        edge_ref[k:k + 1, :] = jnp.where(origin, odd, mirror_ref[0:1, to])
+    place = lax.broadcasted_iota(jnp.int32, (count, count), 0)
+    source = lax.broadcasted_iota(jnp.int32, (count, count), 1)
+    flip = jnp.where((place + source) % count == 0, 1.0, 0.0).astype(bf16)
+    for k in range(POINTS):
+        to = pl.ds(k * BOX, BOX)
+        far_ref[:, to] = dot(flip, mirror_ref[:, to].astype(bf16)).astype(bf16)
+
+
+def power_kernel(place_ref, own_ref, far_ref, edge_ref, o_ref):
+    count, width = own_ref.shape
+    upper = place_ref[0] != 0
+    o_ref[pl.ds(0, count), :] = own_ref[...]
+    o_ref[pl.ds(count, count), :] = far_ref[...].astype(f32)
+    for k in range(width // LANES):
+        to = pl.ds(k * LANES, LANES)
+        o_ref[0:1, to] = jnp.where(upper, edge_ref[k:k + 1, :], own_ref[0:1, to])
+        o_ref[count:count + 1, to] = jnp.where(upper, own_ref[0:1, to], o_ref[count:count + 1, to])
+
+
+def pieces_kernel(at_ref, x_ref, low_ref, x2_ref, low2_ref, own_ref, sent_ref, ext_ref):
     height, quarter = x_ref.shape
     tall, wide = height // BOX, quarter // BOX
-    ext_ref[pl.ds(0, height), :] = x_ref[...]
-    ext_ref[pl.ds(height, BOX), :] = low_ref[...]
+    slots = own_ref.shape[0]
     chunk = 64
-    slots = o_ref.shape[1]
-
-    def one(slot, carry):
+    mine = at_ref[4 * slots]
+    ext_ref[mine, pl.ds(0, height), :] = x_ref[...]
+    ext_ref[mine, pl.ds(height, BOX), :] = low_ref[...]
+    ext_ref[1 - mine, pl.ds(0, height), :] = x2_ref[...]
+    ext_ref[1 - mine, pl.ds(height, BOX), :] = low2_ref[...]
+
+    def one(o_ref, first_slot, s):
+        slot = first_slot + s
         top, left = at_ref[2 * slot], at_ref[2 * slot + 1]
         tile_row = jnp.clip(top >> 8, 0, tall - 1)
         tile_col = left >> 8
         row_cut, col_cut = top & (BOX - 1), left & (BOX - 1)
-        here = jnp.logical_and(tile_col >= 0, tile_col < wide).astype(f32)
-        after = jnp.logical_and(tile_col >= -1, tile_col < wide - 1).astype(f32)
-        col_a = pl.multiple_of(jnp.clip(tile_col, 0, wide - 1) * BOX, BOX)
-        col_b = pl.multiple_of(jnp.clip(tile_col + 1, 0, wide - 1) * BOX, BOX)
+        here = jnp.logical_and(tile_col >= 0, tile_col < 2 * wide).astype(f32)
+        after = jnp.logical_and(tile_col >= -1, tile_col < 2 * wide - 1).astype(f32)
+        tile_a = jnp.clip(tile_col, 0, 2 * wide - 1)
+        tile_b = jnp.clip(tile_col + 1, 0, 2 * wide - 1)
+        side_a, side_b = tile_a // wide, tile_b // wide
+        col_a = pl.multiple_of((tile_a % wide) * BOX, BOX)
+        col_b = pl.multiple_of((tile_b % wide) * BOX, BOX)
         right = lax.broadcasted_iota(jnp.int32, (chunk, BOX), 1) >= col_cut
         rows = lax.broadcasted_iota(jnp.int32, (chunk, BOX), 0)
         for k in range(BOX // chunk):
@@ -334,56 +429,89 @@
             lower = pl.multiple_of(tile_row * BOX + BOX + k * chunk, chunk)
 
             def across(first_row):
-                a = ext_ref[pl.ds(first_row, chunk), pl.ds(col_a, BOX)].astype(f32) * here
-                b = ext_ref[pl.ds(first_row, chunk), pl.ds(col_b, BOX)].astype(f32) * after
+                a = ext_ref[side_a, pl.ds(first_row, chunk), pl.ds(col_a, BOX)].astype(f32) * here
+                b = ext_ref[side_b, pl.ds(first_row, chunk), pl.ds(col_b, BOX)].astype(f32) * after
                 return jnp.where(right, a, b)
 
             whole = jnp.where(rows + k * chunk >= row_cut, across(upper), across(lower))
-            o_ref[slot // slots, slot % slots, pl.ds(k * chunk, chunk), :] = whole.astype(bf16)
+            o_ref[s, pl.ds(k * chunk, chunk), :] = whole.astype(bf16)
+
+    def both(s, carry):
+        one(own_ref, 0, s)
+        one(sent_ref, slots, s)
         return carry
 
-    lax.fori_loop(0, o_ref.shape[0] * slots, one, 0)
-
-
-def spectra_kernel(n_rows, n_half, roll_ref, p_ref, q_ref, r_ref, whi_ref, wlo_ref, chi_ref, clo_ref, o_ref):
+    lax.fori_loop(0, slots, both, 0)
+
+
+def spectra_kernel(n_planes, n_half, at_ref, p_ref, q_ref, w_hbm, c_hbm, *refs):
+    members = len(refs) - 5
+    o_refs, (w_ref, c_ref, w2_ref, c2_ref, sems) = refs[:members], refs[members:]
+    copies = fetch((w_hbm, w_ref, sems.at[0]), (c_hbm, c_ref, sems.at[1]))
     slots = q_ref.shape[0]
     wide = 2 * BOX
-    tall = BOX // n_rows
     band = wide // n_half
+    tall = o_refs[0].shape[2]
+    beside = members // n_half
+    plane, side, column = (at_ref[2 * slots + n] for n in range(3))
+    for copy in copies:
+        copy.wait()
+    for part in range(2):
+        for k in range(n_planes):
+            for i in range(beside):
+                first = (lax.rem(plane + k, n_planes) * beside + (side ^ i)) * tall
+                rows = c_ref[part, pl.ds(pl.multiple_of(first, tall), tall), :]
+                c2_ref[part, pl.ds((k * beside + i) * tall, tall), :] = rows
+        for half in range(2):
+            for j in range(n_half):
+                first = pl.multiple_of((column ^ j) * band + half * wide, band)
+                w2_ref[part, :, pl.ds(j * band + half * wide, band)] = w_ref[part, :, pl.ds(first, band)]
 
     def one(s, carry):
-        box = p_ref[s].astype(f32) + q_ref[s].astype(f32) + r_ref[s].astype(f32)
-        box = pltpu.roll(box, roll_ref[2 * s], 0)
-        box = pltpu.roll(box, roll_ref[2 * s + 1], 1).astype(bf16)
-        inner = dot(box, whi_ref[...]) + dot(box, wlo_ref[...])
+        box = p_ref[s].astype(f32) + q_ref[s].astype(f32)
+        box = pltpu.roll(box, at_ref[2 * s], 0)
+        box = pltpu.roll(box, at_ref[2 * s + 1], 1).astype(bf16)
+        inner = dot(box, w2_ref[0]) + dot(box, w2_ref[1])
         high = inner.astype(bf16)
         low = (inner - high.astype(f32)).astype(bf16)
         high = jnp.concatenate([high[:, :wide], high[:, wide:]], axis=0)
         low = jnp.concatenate([low[:, :wide], low[:, wide:]], axis=0)
-        outer = dot(chi_ref[...], high) + dot(chi_ref[...], low) + dot(clo_ref[...], high)
+        outer = dot(c2_ref[0], high) + dot(c2_ref[0], low) + dot(c2_ref[1], high)
         outer = outer.astype(bf16)
-        for i in range(n_rows):
-            for j in range(n_half):
-                o_ref[i * n_half + j, s] = outer[i * tall:(i + 1) * tall, j * band:(j + 1) * band]
+        for k in range(n_planes):
+            for i in range(beside):
+                row = (k * beside + i) * tall
+                for j in range(n_half):
+                    o_refs[i * n_half + j][k, s] = outer[row:row + tall, j * band:(j + 1) * band]
         return carry
 
-    lax.fori_loop(0, slots, one, 0)
-
-
-def means_kernel(label_ref, live_ref, divisor_ref, f_ref, o_ref, *sum_refs):
-    slots = f_ref.shape[1]
-    half = f_ref.shape[3] // 2
+    lax.fori_loop(0, slots, one, 0, unroll=2)
+
+
+def gather_kernel(members, *refs):
+    sides, outs = refs[:members], refs[members:]
+    slots = sides[0].shape[1]
+    for k, out_ref in enumerate(outs):
+        for m, side_ref in enumerate(sides):
+            out_ref[pl.ds(m * slots, slots)] = side_ref[k]
+
+
+def means_kernel(label_ref, live_ref, divisor_ref, *refs):
+    count = (len(refs) - 1) // 2
+    f_refs, o_ref, sum_refs = refs[:count], refs[count], refs[count + 1:]
+    here = f_refs[0].shape[0]
+    half = f_refs[0].shape[2] // 2
     for sum_ref in sum_refs:
         sum_ref[...] = jnp.zeros_like(sum_ref)
 
     def add(g, carry):
-        for s, sum_ref in enumerate(sum_refs):
-            k = label_ref[g * slots + s]
-            live = live_ref[g * slots + s].astype(f32)
-            sum_ref[k] = sum_ref[k] + f_ref[g, s].astype(f32) * live
+        for n, (f_ref, sum_ref) in enumerate(zip(f_refs, sum_refs)):
+            k = label_ref[n * here + g]
+            live = live_ref[n * here + g].astype(f32)
+            sum_ref[k] = sum_ref[k] + f_ref[g].astype(f32) * live
         return carry
 
-    lax.fori_loop(0, f_ref.shape[0], add, 0)
+    lax.fori_loop(0, here, add, 0, unroll=4)
 
     def finish(k, carry):
         mean = sum_refs[0][k]
@@ -394,7 +522,7 @@
         o_ref[k, 1] = mean[:, half:]
         return carry
 
-    lax.fori_loop(0, o_ref.shape[0], finish, 0)
+    lax.fori_loop(0, o_ref.shape[0], finish, 0, unroll=5)
 
 
 def swapped(block, axis, bit):
@@ -418,14 +546,22 @@
     shape = jax.ShapeDtypeStruct
 
     below = passed_along(micrograph[:BOX], "rows", -1)
+    micrograph2 = swapped(micrograph, "half", 1)
 
     points = np.arange(BOX)
     cos_box, sin_box = waves(points, points, BOX)
-    first_hi, first_lo = halves(np.concatenate([cos_box, -sin_box], axis=1))
-    turned_hi, turned_lo = halves(np.concatenate([sin_box, cos_box], axis=1))
+
+    def table(values):
+        return pltpu.with_memory_space_constraint(jnp.asarray(values), pltpu.HBM)
+
+    first = np.stack(halves(np.concatenate([cos_box, -sin_box], axis=1)))
     tc, ts = waves(np.arange(POINTS), points, width)
-    tc = tc.astype(np.float32)[:, None, :]
-    ts = ts.astype(np.float32)[:, None, :]
+    mc, ms = waves(np.arange(POINTS), BOX - points, width)
+    turns = np.stack([tc, ts]).astype(np.float32)[:, :, None]
+    turns_both = (np.stack([tc, ts, mc, ms]) / width).astype(np.float32)[:, :, None]
+
+    def fetched(*tables):
+        return [pltpu.VMEM(t.shape, t.dtype) for t in tables] + [pltpu.SemaphoreType.DMA((len(tables),))]
 
     ready = call(
         functools.partial(prepare_kernel, n_half),
@@ -434,27 +570,29 @@
         flops=2 * height * quarter * (height + quarter),
     )
     ready = lax.all_to_all(ready, "half", 0, 0, tiled=True)
+    below2 = swapped(below, "half", 1)
     mixed = call(
         functools.partial(rows_kernel, n_rows, n_half),
-        shape((total, kept, 2, span, slab), bf16),
-        [ready, first_hi, first_lo, tc, ts], [VMEM] * 5,
-        scratch=[pltpu.VMEM((POINTS, height // n_half, BOX), f32)] * 2,
+        shape((total, kept, span, slab), bf16),
+        [ready, table(first), table(turns)], [VMEM, HBM, HBM],
+        scratch=[pltpu.VMEM((POINTS, height // n_half, BOX), f32)] * 2 + fetched(first, turns),
         flops=4 * height * quarter * 2 * BOX,
     )
     mixed = lax.all_to_all(mixed, everyone, 0, 0, tiled=True)
 
-    corner = jnp.stack([row_index * height, half_index * quarter])
-    owners = jnp.bitwise_xor(half_index, jnp.asarray(np.array([0, 2, 1, 3], np.int32)))
-    at = (box_tops[row_index][owners] - corner).reshape(-1)
-    pieces = call(
+    core = half_index % 2
+    corner = jnp.stack([row_index * height, (half_index - core) * quarter])
+    band_tops = box_tops[row_index]
+    at = jnp.stack([band_tops[half_index], band_tops[half_index ^ 2]]) - corner
+    at = jnp.concatenate([at.reshape(-1), core.reshape(1)])
+    pieces, sent = call(
         pieces_kernel,
-        shape((n_half, slots, BOX, BOX), bf16),
-        [at, micrograph, below], [SMEM, VMEM, VMEM],
-        scratch=[pltpu.VMEM((height + BOX, quarter), bf16)],
-        flops=10 * n_half * slots * BOX * BOX,
-    )
-    beside = swapped(pieces[2:], "half", 1)
-    across = swapped(pieces[1] + beside[1], "half", 2)
+        (shape((slots, BOX, BOX), bf16),) * 2,
+        [at, micrograph, below, micrograph2, below2], [SMEM] + [VMEM] * 4,
+        scratch=[pltpu.VMEM((2, height + BOX, quarter), bf16)],
+        flops=20 * slots * BOX * BOX,
+    )
+    across = swapped(sent, "half", 2)
     part = BOX // n_half
 
     def by_part(a, b):
@@ -464,35 +602,76 @@
 
     plain = by_part(cos_box, -sin_box)
     crossed = by_part(-sin_box, -cos_box)
-    inner_hi, inner_lo = halves(np.concatenate([plain, crossed], axis=1) / BOX)
-    outer_hi, outer_lo = halves(np.concatenate([cos_box, sin_box], axis=1))
+    inner = np.stack(halves(np.concatenate([plain, crossed], axis=1) / BOX))
+    outer = np.stack(halves(np.concatenate([cos_box, sin_box], axis=1)))
     my_tops = box_tops[row_index, half_index]
     rolls = jnp.mod(box_shift.reshape(slots, 2) - my_tops, BOX).reshape(-1)
+    n_planes = n_rows // 2
+    members = total // n_planes
+    plane = row_index // 2
+    member = (row_index % 2) * n_half + half_index
+    spot = jnp.stack([plane, row_index % 2, half_index])
     spectra = call(
-        functools.partial(spectra_kernel, n_rows, n_half),
-        shape((total, slots, BOX // n_rows, 2 * part), bf16),
-        [rolls, pieces[0], beside[0], across, inner_hi, inner_lo, outer_hi, outer_lo], [SMEM] + [VMEM] * 7,
+        functools.partial(spectra_kernel, n_planes, n_half),
+        (shape((n_planes, slots, BOX // n_rows, 2 * part), bf16),) * members,
+        [jnp.concatenate([rolls, spot]), pieces, across, table(inner), table(outer)],
+        [SMEM, VMEM, VMEM, HBM, HBM],
+        scratch=[pltpu.VMEM(t.shape, t.dtype) for t in (inner, outer)] + fetched(inner, outer),
         flops=slots * BOX * BOX * 4 * BOX * 10,
     )
-    spectra, mixed = lax.optimization_barrier((spectra, mixed))
-    spectra = lax.all_to_all(spectra, everyone, 0, 0, tiled=True)
-
+    sides = [spectra[0]]
+    for m in range(1, members):
+        route = [(d, d - d % members + (d % members ^ m)) for d in range(total)]
+        sides.append(lax.ppermute(spectra[m], everyone, route))
+    gathered = call(
+        functools.partial(gather_kernel, members),
+        (shape((members * slots, BOX // n_rows, 2 * part), bf16),) * n_planes,
+        sides, [VMEM] * members,
+        flops=total * slots * BOX * BOX // 8,
+    )
+
+    arrived = [gathered[0]]
+    for k in range(1, n_planes):
+        route = [(d, (d + k * members) % total) for d in range(total)]
+        arrived.append(lax.ppermute(gathered[k], everyone, route))
+
+    def source_order(values):
+        values = values.reshape(n_planes, members, slots)
+        ids = jnp.arange(max(n_planes, members), dtype=jnp.int32)
+        values = values[jnp.mod(plane - ids[:n_planes], n_planes)]
+        return values[:, member ^ ids[:members]].reshape(-1)
+
+    half = slab // 2
+    place = half_index * n_rows + row_index
+    own, far, edge = call(
+        functools.partial(columns_kernel, n_rows, n_half),
+        (shape((half, width), f32), shape((half, width), bf16), shape((width // LANES, LANES), f32)),
+        [place.reshape(1), mixed, table(first), table(turns_both)], [SMEM, VMEM, HBM, HBM],
+        scratch=[pltpu.VMEM((POINTS, half, BOX), f32)] * 4
+        + [pltpu.VMEM((half, width), f32), pltpu.VMEM((4, 8, width), f32)]
+        + fetched(first, turns_both),
+        flops=8 * slab * width * 2 * BOX,
+    )
+    far = lax.ppermute(far, everyone, [(d, total - 1 - d) for d in range(total)])
+    seats = [(p % n_rows) * n_half + p // n_rows for p in range(total)]
+    route = [(p, total - p) for p in range(1, total // 2)] + [(0, total // 2)]
+    edge = lax.ppermute(edge, everyone, [(seats[a], seats[b]) for a, b in route])
     power = call(
-        functools.partial(columns_kernel, n_rows, n_half),
+        power_kernel,
         shape((slab, width), f32),
-        [mixed, first_hi, first_lo, turned_hi, turned_lo, tc / width, ts / width], [VMEM] * 7,
-        scratch=[pltpu.VMEM((POINTS, slab, BOX), f32)] * 2,
-        flops=8 * slab * width * 2 * BOX,
+        [(2 * place >= total).astype(jnp.int32).reshape(1), own, far, edge], [SMEM] + [VMEM] * 3,
+        flops=slab * width,
     )[None]
     labels, lives = box_class.reshape(-1), box_live.reshape(-1)
     matches = labels[None, :] == jnp.arange(CLASSES, dtype=jnp.int32)[:, None]
     counts = jnp.sum(jnp.where(matches, lives[None, :], 0), axis=1)
     divisor = jnp.maximum(counts, 1).astype(f32)
+    labels_here, lives_here = source_order(box_class), source_order(box_live)
     class_means = call(
         means_kernel,
         shape((CLASSES, 2, BOX // n_rows, part), f32),
-        [labels, lives, divisor, spectra], [SMEM, SMEM, SMEM, VMEM],
-        scratch=[pltpu.VMEM((CLASSES, BOX // n_rows, 2 * part), f32)] * slots,
+        [labels_here, lives_here, divisor, *arrived], [SMEM] * 3 + [VMEM] * len(arrived),
+        scratch=[pltpu.VMEM((CLASSES, BOX // n_rows, 2 * part), f32)] * n_planes,
         flops=4 * total * slots * BOX * BOX,
     )
     return (power, class_means)
@@ -511,6 +690,7 @@
         and quarter // n_rows == LANES
         and BOX // n_rows % 16 == 0
         and 2 * BOX // n_half == LANES
+        and n_rows == 8
     )
 
 

time: 161 us -> 159 us (0.988)
  the two profiles are of different devices: /device:TPU:0 before, /device:TPU:9 now
where the time goes in v3:
time: 159 us; the launch traced here: 158 us
  waiting for transfers between devices  67 us (42%)
  starting transfers between devices  35.5 us (22%)
  Pallas kernels  27.9 us (18%)
  blocking collectives  16.6 us (10%)
  local copies, waits for them, and re-layouts  8.84 us (6%)
    pallas_call x8, Pallas kernels, call(): pl.pallas_call(kernel, out_shape=out, in_specs=specs, out_specs=(VMEM,) *...  27.9 us
    ppermute x3, waiting for transfers between devices, fast_device(): arrived.append(lax.ppermute(gathered[k], everyone, route))  25.5 us
    ppermute x1, waiting for transfers between devices, passed_along(): return lax.ppermute(block, axis, route)  23.5 us
    all_to_all x1, blocking collectives, fast_device(): ready = lax.all_to_all(ready, 'half', 0, 0, tiled=True)  16.6 us
    ppermute x7, starting transfers between devices, fast_device(): sides.append(lax.ppermute(spectra[m], everyone, route))  14.7 us
    ppermute x3, waiting for transfers between devices, swapped(): return lax.ppermute(block, axis, route)  11.3 us
    ppermute x3, starting transfers between devices, fast_device(): arrived.append(lax.ppermute(gathered[k], everyone, route))  7.8 us
    ppermute x7, waiting for transfers between devices, fast_device(): sides.append(lax.ppermute(spectra[m], everyone, route))  6.64 us
  transfers between devices with their start and end apart: 17, of which 8 were waited for; matrix products, arithmetic and copies ran while one was open for 4% of the time, Pallas kernels for 12%

profile of v3, /device:TPU:9, one launch (start us, length us, event | category | flops | bytes accessed | tf_op | source)
XLA Modules:
  0.0 158.3 jit_solution(16128609786702082019)
XLA Ops:
  0.6 1.2 copy-done
  1.9 1.8 %shard_map.113 = bf16[4,16,64,128]{3,2,1,0:T(8,128)(2,1)S(1)} custom-call(bf16[512,1024]{1,0:T(8,128)(2,1)S(1)} %copy-done), custom_call_target="tpu_custom_call" | custom-call | flops 1610612736 | bytes 2097152 | tf_op jit(solution)/shard_map/pallas_call | solution.py:160
  3.7 16.6 %all_to_all.10.y_ref = bf16[4,16,64,128]{3,2,1,0:T(8,128)(2,1)S(1)} all-to-all(bf16[4,16,64,128]{3,2,1,0:T(8,128)(2,1)S(1)} %shard_map.113), channel_id=1, replica_groups=mesh['rows'=8,'half'=4] {'half'}, dimensions={0} | all-to-all | bytes 2097152 | tf_op jit(solution)/shard_map/all_to_all | solution.py:572
  20.3 5.5 %shard_map.114 = bf16[32,4,32,128]{3,2,1,0:T(8,128)(2,1)} custom-call(bf16[4,16,64,128]{3,2,1,0:T(8,128)(2,1)S(1)} %all_to_all.10.y_ref, bf16[2,256,512]{2,1,0:T(8,128)(2,1)} %constant.135.clone.w_hbm, f32[2,16,1,256]{3,2,1,0:T(1,128)} %constant.136.clone.t_hbm), custom_call_target="tpu_custom_call" | custom-call | flops 1073741824 | bytes 2654208 | tf_op jit(solution)/shard_map/pallas_call | solution.py:160
  25.9 5.7 %all-to-all-start.1 = ((bf16[32,4,32,128]{3,2,1,0:T(8,128)(2,1)}), bf16[32,4,32,128]{3,2,1,0:T(8,128)(2,1)S(1)}, u32[]{:S(2)}, u32[]{:S(2)}) async-start(bf16[32,4,32,128]{3,2,1,0:T(8,128)(2,1)} %shard_map.114), calls=%async_computation.1 | async-start | bytes 2097152 | tf_op jit(solution)/shard_map/all_to_all | solution.py:581
  31.7 0.8 slice.8
  32.5 3.1 %collective-permute-start.2 = (bf16[256,1024]{1,0:T(8,128)(2,1)}, bf16[256,1024]{1,0:T(8,128)(2,1)}, u32[]{:S(2)}, u32[]{:S(2)}) collective-permute-start(bf16[256,1024]{1,0:T(8,128)(2,1)} %slice.8), channel_id=1, source_target_pairs={{4,0},{8,4},{12,8},{16,12},{20,16},{24,20},{28,24},{5,1},{9,5},{13... | collective-permute-start | bytes 1572872 | tf_op jit(solution)/shard_map/ppermute | solution.py:25
  35.6 0.7 collective-permute-start.3
  36.3 23.5 %collective-permute-done.2.low_ref = bf16[256,1024]{1,0:T(8,128)(2,1)} collective-permute-done((bf16[256,1024]{1,0:T(8,128)(2,1)}, bf16[256,1024]{1,0:T(8,128)(2,1)}, u32[]{:S(2)}, u32[]{:S(2)}) %collective-permute-start.2) | collective-permute-done | bytes 524320 | tf_op jit(solution)/shard_map/ppermute | solution.py:25
  59.8 1.0 collective-permute-start.4
  61.8 0.9 collective-permute-done.4.low2_ref
  62.7 3.1 %shard_map.117 = (bf16[4,256,256]{2,1,0:T(8,128)(2,1)S(1)}, bf16[4,256,256]{2,1,0:T(8,128)(2,1)}) custom-call(s32[17]{0:T(128)S(1)} %pad_add_fusion.2.at_ref, bf16[512,1024]{1,0:T(8,128)(2,1)S(1)} %copy-done.1, bf16[256,1024]{1,0:T(8,128)(2,1)} %collective-permute-done.2.low_ref, bf16[512,1024]{1,0:T(8,128)(2,1)S(1)} %collective-permute-done.3.x2_ref, ...), custom_call_target="tpu_custom_call" | custom-call | flops 5242880 | bytes 4194372 | tf_op jit(solution)/shard_map/pallas_call | solution.py:160
  65.8 0.8 copy-done.2
  66.6 1.2 collective-permute-start.5
  69.5 10.4 %collective-permute-done.5.q_ref = bf16[4,256,256]{2,1,0:T(8,128)(2,1)S(1)} collective-permute-done((bf16[4,256,256]{2,1,0:T(8,128)(2,1)}, bf16[4,256,256]{2,1,0:T(8,128)(2,1)S(1)}, u32[]{:S(2)}, u32[]{:S(2)}) %collective-permute-start.5) | collective-permute-done | bytes 524320 | tf_op jit(solution)/shard_map/ppermute | solution.py:530
  79.9 1.0 copy-done.3
  81.0 6.7 %shard_map.118 = (bf16[4,4,32,128]{3,2,1,0:T(8,128)(2,1)S(1)}, bf16[4,4,32,128]{3,2,1,0:T(8,128)(2,1)}, bf16[4,4,32,128]{3,2,1,0:T(8,128)(2,1)}, bf16[4,4,32,128...) custom-call(s32[11]{0:T(128)S(1)} %pad_add_fusion.at_ref, ...), custom_call_target="tpu_custom_call" | custom-call | flops 2684354560 | bytes 3670060 | tf_op jit(solution)/shard_map/pallas_call | solution.py:160
  88.3 1.2 collective-permute-start.6
  89.6 1.2 collective-permute-start.7
  91.2 8.7 %collective-permute-start.9 = (bf16[4,4,32,128]{3,2,1,0:T(8,128)(2,1)}, bf16[4,4,32,128]{3,2,1,0:T(8,128)(2,1)S(1)}, u32[]{:S(2)}, u32[]{:S(2)}) collective-permute-start(bf16[4,4,32,128]{3,2,1,0:T(8,128)(2,1)} %get-tuple-element.28), channel_id=1, source_target_pairs={{0,4},{1,5},{2,6},{3,7},{4,0},{5,1},{6,2},{7,3},{8,12},{9,13},{10,... | collective-permute-start | bytes 393224 | tf_op jit(solution)/shard_map/ppermute | solution.py:625
  100.1 5.2 %shard_map.115 = (f32[64,4096]{1,0:T(8,128)S(1)}, bf16[64,4096]{1,0:T(8,128)(2,1)S(1)}, f32[32,128]{1,0:T(8,128)}) custom-call(s32[1]{0:T(128)} %bitcast.1.place_ref, bf16[32,4,32,128]{3,2,1,0:T(8,128)(2,1)S(1)} %all-to-all-done.1.z_ref, bf16[2,256,512]{2,1,0:T(8,128)(2,1)} %constant.135.clone.w_hbm, f32[4,16,1,256]{3,2,1,0:T(1,128)} %constant.139.clone.t_hbm), custom_call_target="tpu_custom_call" | custom-call | flops 2147483648 | bytes 3227652 | tf_op jit(solution)/shard_map/pallas_call | solution.py:160
  105.3 2.7 %collective-permute-start.11 = (bf16[4,4,32,128]{3,2,1,0:T(8,128)(2,1)S(1)}, bf16[4,4,32,128]{3,2,1,0:T(8,128)(2,1)S(1)}, u32[]{:S(2)}, u32[]{:S(2)}) collective-permute-start(bf16[4,4,32,128]{3,2,1,0:T(8,128)(2,1)S(1)} %copy-done.5), channel_id=1, source_target_pairs={{0,6},{1,7},{2,4},{3,5},{4,2},{5,3},{6,0},{7,1},{8,14},{9,15},{10,... | collective-permute-start | bytes 393224 | tf_op jit(solution)/shard_map/ppermute | solution.py:625
  108.3 3.1 %collective-permute-done.11.refs_6_ = bf16[4,4,32,128]{3,2,1,0:T(8,128)(2,1)S(1)} collective-permute-done((bf16[4,4,32,128]{3,2,1,0:T(8,128)(2,1)S(1)}, bf16[4,4,32,128]{3,2,1,0:T(8,128)(2,1)S(1)}, u32[]{:S(2)}, u32[]{:S(2)}) %collective-permute-start.11) | collective-permute-done | bytes 131104 | tf_op jit(solution)/shard_map/ppermute | solution.py:625
  111.5 3.5 %collective-permute-done.12.refs_7_ = bf16[4,4,32,128]{3,2,1,0:T(8,128)(2,1)S(1)} collective-permute-done((bf16[4,4,32,128]{3,2,1,0:T(8,128)(2,1)S(1)}, bf16[4,4,32,128]{3,2,1,0:T(8,128)(2,1)S(1)}, u32[]{:S(2)}, u32[]{:S(2)}) %collective-permute-start.12) | collective-permute-done | bytes 131104 | tf_op jit(solution)/shard_map/ppermute | solution.py:625
  115.0 0.9 shard_map.119
  115.9 7.6 %collective-permute-start.14 = (bf16[32,32,128]{2,1,0:T(8,128)(2,1)}, bf16[32,32,128]{2,1,0:T(8,128)(2,1)S(1)}, u32[]{:S(2)}, u32[]{:S(2)}) collective-permute-start(bf16[32,32,128]{2,1,0:T(8,128)(2,1)} %get-tuple-element.34), channel_id=1, source_target_pairs={{0,16},{1,17},{2,18},{3,19},{4,20},{5,21},{6,22},{7,23},{8,24},{9,... | collective-permute-start | bytes 786440 | tf_op jit(solution)/shard_map/ppermute | solution.py:636
  123.7 1.3 collective-permute-start.1
  128.1 16.9 %collective-permute-done.13.refs_1_ = bf16[32,32,128]{2,1,0:T(8,128)(2,1)S(1)} collective-permute-done((bf16[32,32,128]{2,1,0:T(8,128)(2,1)}, bf16[32,32,128]{2,1,0:T(8,128)(2,1)S(1)}, u32[]{:S(2)}, u32[]{:S(2)}) %collective-permute-start.13) | collective-permute-done | bytes 262176 | tf_op jit(solution)/shard_map/ppermute | solution.py:636
  145.0 5.6 %collective-permute-done.14.refs_2_ = bf16[32,32,128]{2,1,0:T(8,128)(2,1)S(1)} collective-permute-done((bf16[32,32,128]{2,1,0:T(8,128)(2,1)}, bf16[32,32,128]{2,1,0:T(8,128)(2,1)S(1)}, u32[]{:S(2)}, u32[]{:S(2)}) %collective-permute-start.14) | collective-permute-done | bytes 262176 | tf_op jit(solution)/shard_map/ppermute | solution.py:636
  150.6 3.0 %collective-permute-done.15.refs_3_ = bf16[32,32,128]{2,1,0:T(8,128)(2,1)S(1)} collective-permute-done((bf16[32,32,128]{2,1,0:T(8,128)(2,1)}, bf16[32,32,128]{2,1,0:T(8,128)(2,1)S(1)}, u32[]{:S(2)}, u32[]{:S(2)}) %collective-permute-start.15) | collective-permute-done | bytes 262176 | tf_op jit(solution)/shard_map/ppermute | solution.py:636
  153.6 3.2 %shard_map.120 = f32[50,2,32,64]{3,2,1,0:T(8,128)} custom-call(s32[128]{0:T(128)S(1)} %reshape.61.label_ref, s32[128]{0:T(128)S(1)} %reshape.63.live_ref, f32[50]{0:T(128)S(1)} %maximum_convert_fusion.divisor_ref, bf16[32,32,128]{2,1,0:T(8,128)(2,1)S(1)} %get-tuple-element.32.refs_0_, bf16[32,32,128]{2,1,0:T(8,128)(2,1)S(1)} %collective-permute-done.13.refs_1_, ...), custom_call_target="tpu_custom_call" | custom-call | flops 33554432 | bytes 1869000 | tf_op jit(solution)/shard_map/pallas_call | solution.py:160
  156.8 1.5 shard_map.116
  (77 shorter events, 7.6 us)
Async XLA Ops:
  0.6 1.2 copy-start
  20.3 11.3 %copy-start.1 = (bf16[512,1024]{1,0:T(8,128)(2,1)S(1)}, bf16[512,1024]{1,0:T(8,128)(2,1)}, u32[]{:S(2)}) copy-start(bf16[512,1024]{1,0:T(8,128)(2,1)} %x_ref.3) | copy-start | bytes 3145732
  25.8 35.0 %copy-start.8 = (s32[8,4,4,2]{0,3,2,1:T(2,128)S(1)}, s32[8,4,4,2]{0,3,2,1:T(2,128)}, u32[]{:S(2)}) copy-start(s32[8,4,4,2]{0,3,2,1:T(2,128)} %param.11) | copy-start | bytes 3076
  25.9 35.2 %copy-start.9 = (s32[1,1,4,2]{2,3,1,0:T(2,128)S(1)}, s32[1,1,4,2]{2,3,1,0:T(2,128)}, u32[]{:S(2)}) copy-start(s32[1,1,4,2]{2,3,1,0:T(2,128)} %param.14) | copy-start | bytes 100
  25.9 74.2 %all-to-all-start.1 = ((bf16[32,4,32,128]{3,2,1,0:T(8,128)(2,1)}), bf16[32,4,32,128]{3,2,1,0:T(8,128)(2,1)S(1)}, u32[]{:S(2)}, u32[]{:S(2)}) async-start(bf16[32,4,32,128]{3,2,1,0:T(8,128)(2,1)} %shard_map.114), calls=%async_computation.1 | async-start | bytes 2097152 | tf_op jit(solution)/shard_map/all_to_all | solution.py:581
  31.6 36.2 %copy-start.6 = (s32[8,4,4]{0,2,1:T(4,128)S(1)}, s32[8,4,4]{0,2,1:T(4,128)}, u32[]{:S(2)}) copy-start(s32[8,4,4]{0,2,1:T(4,128)} %param.12) | copy-start | bytes 1540
  31.6 36.4 %copy-start.7 = (s32[8,4,4]{0,2,1:T(4,128)S(1)}, s32[8,4,4]{0,2,1:T(4,128)}, u32[]{:S(2)}) copy-start(s32[8,4,4]{0,2,1:T(4,128)} %param.13) | copy-start | bytes 1540
  32.5 27.4 %collective-permute-start.2 = (bf16[256,1024]{1,0:T(8,128)(2,1)}, bf16[256,1024]{1,0:T(8,128)(2,1)}, u32[]{:S(2)}, u32[]{:S(2)}) collective-permute-start(bf16[256,1024]{1,0:T(8,128)(2,1)} %slice.8), channel_id=1, source_target_pairs={{4,0},{8,4},{12,8},{16,12},{20,16},{24,20},{28,24},{5,1},{9,5},{13... | collective-permute-start | bytes 1572872 | tf_op jit(solution)/shard_map/ppermute | solution.py:25
  35.6 27.1 %collective-permute-start.3 = (bf16[512,1024]{1,0:T(8,128)(2,1)S(1)}, bf16[512,1024]{1,0:T(8,128)(2,1)S(1)}, u32[]{:S(2)}, u32[]{:S(2)}) collective-permute-start(bf16[512,1024]{1,0:T(8,128)(2,1)S(1)} %copy-done.1), channel_id=1, source_target_pairs={{0,1},{1,0},{2,3},{3,2},{4,5},{5,4},{6,7},{7,6},{8,9},{9,8},{10,11... | collective-permute-start | bytes 3145736 | tf_op jit(solution)/shard_map/ppermute | solution.py:530
  59.8 2.8 %collective-permute-start.4 = (bf16[256,1024]{1,0:T(8,128)(2,1)}, bf16[256,1024]{1,0:T(8,128)(2,1)}, u32[]{:S(2)}, u32[]{:S(2)}) collective-permute-start(bf16[256,1024]{1,0:T(8,128)(2,1)} %collective-permute-done.2.low_ref), channel_id=1, source_target_pairs={{0,1},{1,0},{2,3},{3,2},{4,5},{5,4},{6,7},{7,6},{8,9},{9,8},{10,11... | collective-permute-start | bytes 1572872 | tf_op jit(solution)/shard_map/ppermute | solution.py:530
  65.8 0.8 copy-start.2
  66.6 13.3 %collective-permute-start.5 = (bf16[4,256,256]{2,1,0:T(8,128)(2,1)}, bf16[4,256,256]{2,1,0:T(8,128)(2,1)S(1)}, u32[]{:S(2)}, u32[]{:S(2)}) collective-permute-start(bf16[4,256,256]{2,1,0:T(8,128)(2,1)} %get-tuple-element.23), channel_id=1, source_target_pairs={{0,2},{1,3},{2,0},{3,1},{4,6},{5,7},{6,4},{7,5},{8,10},{9,11},{10,... | collective-permute-start | bytes 1572872 | tf_op jit(solution)/shard_map/ppermute | solution.py:530
  79.9 1.0 copy-start.3
  87.7 0.7 copy-start.4
  88.3 16.9 %collective-permute-start.6 = (bf16[4,4,32,128]{3,2,1,0:T(8,128)(2,1)}, bf16[4,4,32,128]{3,2,1,0:T(8,128)(2,1)S(1)}, u32[]{:S(2)}, u32[]{:S(2)}) collective-permute-start(bf16[4,4,32,128]{3,2,1,0:T(8,128)(2,1)} %get-tuple-element.25), channel_id=1, source_target_pairs={{0,1},{1,0},{2,3},{3,2},{4,5},{5,4},{6,7},{7,6},{8,9},{9,8},{10,11... | collective-permute-start | bytes 393224 | tf_op jit(solution)/shard_map/ppermute | solution.py:625
  89.6 18.5 %collective-permute-start.7 = (bf16[4,4,32,128]{3,2,1,0:T(8,128)(2,1)}, bf16[4,4,32,128]{3,2,1,0:T(8,128)(2,1)S(1)}, u32[]{:S(2)}, u32[]{:S(2)}) collective-permute-start(bf16[4,4,32,128]{3,2,1,0:T(8,128)(2,1)} %get-tuple-element.26), channel_id=1, source_target_pairs={{0,2},{1,3},{2,0},{3,1},{4,6},{5,7},{6,4},{7,5},{8,10},{9,11},{10,... | collective-permute-start | bytes 393224 | tf_op jit(solution)/shard_map/ppermute | solution.py:625
  90.7 17.6 %collective-permute-start.8 = (bf16[4,4,32,128]{3,2,1,0:T(8,128)(2,1)}, bf16[4,4,32,128]{3,2,1,0:T(8,128)(2,1)S(1)}, u32[]{:S(2)}, u32[]{:S(2)}) collective-permute-start(bf16[4,4,32,128]{3,2,1,0:T(8,128)(2,1)} %get-tuple-element.27), channel_id=1, source_target_pairs={{0,3},{1,2},{2,1},{3,0},{4,7},{5,6},{6,5},{7,4},{8,11},{9,10},{10,... | collective-permute-start | bytes 393224 | tf_op jit(solution)/shard_map/ppermute | solution.py:625
  91.2 17.1 %collective-permute-start.9 = (bf16[4,4,32,128]{3,2,1,0:T(8,128)(2,1)}, bf16[4,4,32,128]{3,2,1,0:T(8,128)(2,1)S(1)}, u32[]{:S(2)}, u32[]{:S(2)}) collective-permute-start(bf16[4,4,32,128]{3,2,1,0:T(8,128)(2,1)} %get-tuple-element.28), channel_id=1, source_target_pairs={{0,4},{1,5},{2,6},{3,7},{4,0},{5,1},{6,2},{7,3},{8,12},{9,13},{10,... | collective-permute-start | bytes 393224 | tf_op jit(solution)/shard_map/ppermute | solution.py:625
  99.9 8.4 %collective-permute-start.10 = (bf16[4,4,32,128]{3,2,1,0:T(8,128)(2,1)}, bf16[4,4,32,128]{3,2,1,0:T(8,128)(2,1)S(1)}, u32[]{:S(2)}, u32[]{:S(2)}) collective-permute-start(bf16[4,4,32,128]{3,2,1,0:T(8,128)(2,1)} %get-tuple-element.29), channel_id=1, source_target_pairs={{0,5},{1,4},{2,7},{3,6},{4,1},{5,0},{6,3},{7,2},{8,13},{9,12},{10,... | collective-permute-start | bytes 393224 | tf_op jit(solution)/shard_map/ppermute | solution.py:625
  100.0 5.2 %copy-start.5 = (bf16[4,4,32,128]{3,2,1,0:T(8,128)(2,1)S(1)}, bf16[4,4,32,128]{3,2,1,0:T(8,128)(2,1)}, u32[]{:S(2)}) copy-start(bf16[4,4,32,128]{3,2,1,0:T(8,128)(2,1)} %copy-done.4) | copy-start | bytes 393220
  100.0 8.3 %copy-start.11 = (s32[50]{0:T(128)S(1)}, s32[50]{0:T(128)}, u32[]{:S(2)}) copy-start(s32[50]{0:T(128)} %select_reduce_fusion) | copy-start | bytes 604
  100.0 23.7 %copy-start.10 = (s32[4]{0:T(128)S(1)}, s32[4]{0:T(128)}, u32[]{:S(2)}) copy-start(s32[4]{0:T(128)} %compare_select_fusion.1) | copy-start | bytes 52
  105.3 6.2 %collective-permute-start.11 = (bf16[4,4,32,128]{3,2,1,0:T(8,128)(2,1)S(1)}, bf16[4,4,32,128]{3,2,1,0:T(8,128)(2,1)S(1)}, u32[]{:S(2)}, u32[]{:S(2)}) collective-permute-start(bf16[4,4,32,128]{3,2,1,0:T(8,128)(2,1)S(1)} %copy-done.5), channel_id=1, source_target_pairs={{0,6},{1,7},{2,4},{3,5},{4,2},{5,3},{6,0},{7,1},{8,14},{9,15},{10,... | collective-permute-start | bytes 393224 | tf_op jit(solution)/shard_map/ppermute | solution.py:625
  108.0 7.0 %collective-permute-start.12 = (bf16[4,4,32,128]{3,2,1,0:T(8,128)(2,1)S(1)}, bf16[4,4,32,128]{3,2,1,0:T(8,128)(2,1)S(1)}, u32[]{:S(2)}, u32[]{:S(2)}) collective-permute-start(bf16[4,4,32,128]{3,2,1,0:T(8,128)(2,1)S(1)} %get-tuple-element.31), channel_id=1, source_target_pairs={{0,7},{1,6},{2,5},{3,4},{4,3},{5,2},{6,1},{7,0},{8,15},{9,14},{10,... | collective-permute-start | bytes 393224 | tf_op jit(solution)/shard_map/ppermute | solution.py:625
  108.3 48.5 %collective-permute-start = (bf16[64,4096]{1,0:T(8,128)(2,1)S(1)}, bf16[64,4096]{1,0:T(8,128)(2,1)S(1)}, u32[]{:S(2)}, u32[]{:S(2)}) collective-permute-start(bf16[64,4096]{1,0:T(8,128)(2,1)S(1)} %get-tuple-element.20), channel_id=1, source_target_pairs={{0,31},{1,30},{2,29},{3,28},{4,27},{5,26},{6,25},{7,24},{8,23},{9,... | collective-permute-start | bytes 1572872 | tf_op jit(solution)/shard_map/ppermute | solution.py:655
  115.9 29.1 %collective-permute-start.13 = (bf16[32,32,128]{2,1,0:T(8,128)(2,1)}, bf16[32,32,128]{2,1,0:T(8,128)(2,1)S(1)}, u32[]{:S(2)}, u32[]{:S(2)}) collective-permute-start(bf16[32,32,128]{2,1,0:T(8,128)(2,1)} %get-tuple-element.33), channel_id=1, source_target_pairs={{0,8},{1,9},{2,10},{3,11},{4,12},{5,13},{6,14},{7,15},{8,16},{9,17... | collective-permute-start | bytes 786440 | tf_op jit(solution)/shard_map/ppermute | solution.py:636
  115.9 34.7 %collective-permute-start.14 = (bf16[32,32,128]{2,1,0:T(8,128)(2,1)}, bf16[32,32,128]{2,1,0:T(8,128)(2,1)S(1)}, u32[]{:S(2)}, u32[]{:S(2)}) collective-permute-start(bf16[32,32,128]{2,1,0:T(8,128)(2,1)} %get-tuple-element.34), channel_id=1, source_target_pairs={{0,16},{1,17},{2,18},{3,19},{4,20},{5,21},{6,22},{7,23},{8,24},{9,... | collective-permute-start | bytes 786440 | tf_op jit(solution)/shard_map/ppermute | solution.py:636
  123.5 30.1 %collective-permute-start.15 = (bf16[32,32,128]{2,1,0:T(8,128)(2,1)}, bf16[32,32,128]{2,1,0:T(8,128)(2,1)S(1)}, u32[]{:S(2)}, u32[]{:S(2)}) collective-permute-start(bf16[32,32,128]{2,1,0:T(8,128)(2,1)} %get-tuple-element.35), channel_id=1, source_target_pairs={{0,24},{1,25},{2,26},{3,27},{4,28},{5,29},{6,30},{7,31},{8,0},{9,1... | collective-permute-start | bytes 786440 | tf_op jit(solution)/shard_map/ppermute | solution.py:636
  123.7 33.1 %collective-permute-start.1 = (f32[32,128]{1,0:T(8,128)}, f32[32,128]{1,0:T(8,128)S(1)}, u32[]{:S(2)}, u32[]{:S(2)}) collective-permute-start(f32[32,128]{1,0:T(8,128)} %get-tuple-element.21), channel_id=1, source_target_pairs={{4,31},{8,27},{12,23},{16,19},{20,15},{24,11},{28,7},{1,3},{5,30},... | collective-permute-start | bytes 49160 | tf_op jit(solution)/shard_map/ppermute | solution.py:658

commit v4 on v3

--- a/solution.py
+++ b/solution.py
@@ -147,12 +147,12 @@
 
 
 GROUP = 4
+SUMS = 4
 f32 = jnp.float32
 bf16 = jnp.bfloat16
 VMEM = pl.BlockSpec(memory_space=pltpu.VMEM)
 SMEM = pl.BlockSpec(memory_space=pltpu.SMEM)
 HBM = pl.BlockSpec(memory_space=pltpu.HBM)
-
 
 def call(kernel, out, operands, specs, scratch=(), flops=0):
     made = out if isinstance(out, tuple) else (out,)
@@ -167,17 +167,14 @@
         cost_estimate=pl.CostEstimate(flops=flops, bytes_accessed=moved, transcendentals=0),
     )(*operands)
 
-
 def halves(table):
     high = table.astype(bf16)
     low = (table - high.astype(np.float64)).astype(bf16)
     return high, low
 
-
 def waves(left, right, length):
     angles = 2.0 * np.pi / length * np.mod(np.outer(left, right), length)
     return np.cos(angles), np.sin(angles)
-
 
 def dft4(re, im):
     sr, si = re[0] + re[2], im[0] + im[2]
@@ -185,7 +182,6 @@
     tr, ti = re[1] + re[3], im[1] + im[3]
     er, ei = re[1] - re[3], im[1] - im[3]
     return [sr + tr, dr + ei, sr - tr, dr - ei], [si + ti, di - er, si - ti, di + er]
-
 
 def turn(re, im, step):
     step = step % POINTS
@@ -201,7 +197,6 @@
         return (im - re) * s, (re + im) * -s
     return re * c + im * s, im * c - re * s
 
-
 def dft16(re, im):
     mid_re = [[None] * 4 for _ in range(4)]
     mid_im = [[None] * 4 for _ in range(4)]
@@ -216,56 +211,59 @@
             out_re[k + 4 * m], out_im[k + 4 * m] = yr[m], yi[m]
     return out_re, out_im
 
-
 def fetch(*pairs):
     copies = [pltpu.make_async_copy(source, target, sem) for source, target, sem in pairs]
     for copy in copies:
         copy.start()
     return copies
 
-
 def dot(a, b):
     return jnp.dot(a, b, preferred_element_type=f32)
 
+def one_hot(size, wanted):
+    place = lax.broadcasted_iota(jnp.int32, (size, size), 0)
+    source = lax.broadcasted_iota(jnp.int32, (size, size), 1)
+    return jnp.where(source == wanted(place), 1.0, 0.0).astype(bf16)
 
 def prepare_kernel(n_half, x_ref, y_ref):
     height, quarter = x_ref.shape
+    each = BOX // POINTS
+    share = height // n_half
     rows_each = height // POINTS
-    cols_each = quarter // POINTS
-    share = height // n_half
-    place = lax.broadcasted_iota(jnp.int32, (height, height), 0)
-    source = lax.broadcasted_iota(jnp.int32, (height, height), 1)
-    wanted = (place % rows_each) * POINTS + place // rows_each
-    pick_rows = jnp.where(source == wanted, 1.0, 0.0).astype(bf16)
-    ordered = dot(pick_rows, x_ref[...]).astype(bf16)
-    place = lax.broadcasted_iota(jnp.int32, (quarter, quarter), 0)
-    source = lax.broadcasted_iota(jnp.int32, (quarter, quarter), 1)
-    wanted = (place % cols_each) * POINTS + place // cols_each
-    pick_cols = jnp.where(source == wanted, 1.0, 0.0).astype(bf16)
-    turned = lax.dot_general(
-        pick_cols, ordered, (((1,), (1,)), ((), ())), preferred_element_type=f32
-    ).astype(bf16)
-    for j in range(n_half):
-        for c in range(POINTS):
-            y_ref[j, c] = turned[c * cols_each:(c + 1) * cols_each, j * share:(j + 1) * share]
-
-
-def rows_kernel(n_rows, n_half, y_ref, w_hbm, t_hbm, z_ref, re_ref, im_ref, w_ref, t_ref, sems):
+    pick_rows = one_hot(height, lambda p: (p % rows_each) * POINTS + p // rows_each)
+    pick_cols = one_hot(BOX, lambda p: (p % each) * POINTS + p // each)
+    for k in range(quarter // BOX):
+        ordered = dot(pick_rows, x_ref[:, k * BOX:(k + 1) * BOX]).astype(bf16)
+        turned = lax.dot_general(
+            pick_cols, ordered, (((1,), (1,)), ((), ())), preferred_element_type=f32
+        ).astype(bf16)
+        for j in range(n_half):
+            for c in range(POINTS):
+                y_ref[j, c, k * each:(k + 1) * each] = (
+                    turned[c * each:(c + 1) * each, j * share:(j + 1) * share]
+                )
+
+def rows_kernel(n_rows, n_half, y_ref, w_hbm, t_hbm, z_ref, re_ref, im_ref, turned_ref, w_ref, t_ref, sems):
     copies = fetch((w_hbm, w_ref, sems.at[0]), (t_hbm, t_ref, sems.at[1]))
     share = y_ref.shape[3]
     span = z_ref.shape[2]
     half = LANES // 2
     lane = lax.broadcasted_iota(jnp.int32, (16, LANES), 1)
 
-    for copy in copies:
-        copy.wait()
-
-    def first(g, carry):
+    def turn_blocks(g, carry):
         blocks = [
             jnp.concatenate([y_ref[j, g * GROUP + k] for j in range(n_half)], axis=0)
             for k in range(GROUP)
         ]
-        block = jnp.concatenate(blocks, axis=1).T
+        turned_ref[g] = jnp.concatenate(blocks, axis=1).T
+        return carry
+
+    lax.fori_loop(0, POINTS // GROUP, turn_blocks, 0)
+    for copy in copies:
+        copy.wait()
+
+    def first(g, carry):
+        block = turned_ref[g]
         both = dot(block, w_ref[0]) + dot(block, w_ref[1])
         for k in range(GROUP):
             c = g * GROUP + k
@@ -304,18 +302,14 @@
 
     lax.fori_loop(0, share // 16, second, 0)
 
-
 def columns_kernel(n_rows, n_half, place_ref, z_ref, w_hbm, t_hbm, own_ref, far_ref, edge_ref,
-                   re_ref, im_ref, mre_ref, mim_ref, mirror_ref, raw_ref, w_ref, t_ref, sems):
+                   re_ref, im_ref, mre_ref, mim_ref, mirror_ref, raw_ref, turned_ref, w_ref, t_ref, sems):
     copies = fetch((w_hbm, w_ref, sems.at[0]), (t_hbm, t_ref, sems.at[1]))
     kept = z_ref.shape[1]
     count = own_ref.shape[0]
     width = own_ref.shape[1]
 
-    for copy in copies:
-        copy.wait()
-
-    def first(g, carry):
+    def turn_blocks(g, carry):
         blocks = []
         for k in range(GROUP):
             r = g * GROUP + k
@@ -323,7 +317,15 @@
             blocks.append(
                 jnp.concatenate([z_ref[i * n_half + j, m] for i in range(n_rows)], axis=0)
             )
-        block = jnp.concatenate(blocks, axis=1).T
+        turned_ref[g] = jnp.concatenate(blocks, axis=1).T
+        return carry
+
+    lax.fori_loop(0, POINTS // GROUP, turn_blocks, 0)
+    for copy in copies:
+        copy.wait()
+
+    def first(g, carry):
+        block = turned_ref[g]
         product = dot(block, w_ref[0]) + dot(block, w_ref[1])
         for k in range(GROUP):
             r = g * GROUP + k
@@ -386,7 +388,6 @@
         to = pl.ds(k * BOX, BOX)
         far_ref[:, to] = dot(flip, mirror_ref[:, to].astype(bf16)).astype(bf16)
 
-
 def power_kernel(place_ref, own_ref, far_ref, edge_ref, o_ref):
     count, width = own_ref.shape
     upper = place_ref[0] != 0
@@ -396,7 +397,6 @@
         to = pl.ds(k * LANES, LANES)
         o_ref[0:1, to] = jnp.where(upper, edge_ref[k:k + 1, :], own_ref[0:1, to])
         o_ref[count:count + 1, to] = jnp.where(upper, own_ref[0:1, to], o_ref[count:count + 1, to])
-
 
 def pieces_kernel(at_ref, x_ref, low_ref, x2_ref, low2_ref, own_ref, sent_ref, ext_ref):
     height, quarter = x_ref.shape
@@ -442,7 +442,6 @@
         return carry
 
     lax.fori_loop(0, slots, both, 0)
-
 
 def spectra_kernel(n_planes, n_half, at_ref, p_ref, q_ref, w_hbm, c_hbm, *refs):
     members = len(refs) - 5
@@ -487,7 +486,6 @@
 
     lax.fori_loop(0, slots, one, 0, unroll=2)
 
-
 def gather_kernel(members, *refs):
     sides, outs = refs[:members], refs[members:]
     slots = sides[0].shape[1]
@@ -495,9 +493,8 @@
         for m, side_ref in enumerate(sides):
             out_ref[pl.ds(m * slots, slots)] = side_ref[k]
 
-
 def means_kernel(label_ref, live_ref, divisor_ref, *refs):
-    count = (len(refs) - 1) // 2
+    count = len(refs) - 1 - SUMS
     f_refs, o_ref, sum_refs = refs[:count], refs[count], refs[count + 1:]
     here = f_refs[0].shape[0]
     half = f_refs[0].shape[2] // 2
@@ -505,7 +502,8 @@
         sum_ref[...] = jnp.zeros_like(sum_ref)
 
     def add(g, carry):
-        for n, (f_ref, sum_ref) in enumerate(zip(f_refs, sum_refs)):
+        for n, f_ref in enumerate(f_refs):
+            sum_ref = sum_refs[n % SUMS]
             k = label_ref[n * here + g]
             live = live_ref[n * here + g].astype(f32)
             sum_ref[k] = sum_ref[k] + f_ref[g].astype(f32) * live
@@ -524,11 +522,9 @@
 
     lax.fori_loop(0, o_ref.shape[0], finish, 0, unroll=5)
 
-
 def swapped(block, axis, bit):
     route = [(i, i ^ bit) for i in range(lax.axis_size(axis))]
     return lax.ppermute(block, axis, route)
-
 
 def fast_device(micrograph, box_tops, box_live, box_class, box_shift):
     n_rows = lax.axis_size("rows")
@@ -575,7 +571,8 @@
         functools.partial(rows_kernel, n_rows, n_half),
         shape((total, kept, span, slab), bf16),
         [ready, table(first), table(turns)], [VMEM, HBM, HBM],
-        scratch=[pltpu.VMEM((POINTS, height // n_half, BOX), f32)] * 2 + fetched(first, turns),
+        scratch=[pltpu.VMEM((POINTS, height // n_half, BOX), f32)] * 2
+        + [pltpu.VMEM((POINTS // GROUP, GROUP * height // n_half, BOX), bf16)] + fetched(first, turns),
         flops=4 * height * quarter * 2 * BOX,
     )
     mixed = lax.all_to_all(mixed, everyone, 0, 0, tiled=True)
@@ -623,23 +620,30 @@
     for m in range(1, members):
         route = [(d, d - d % members + (d % members ^ m)) for d in range(total)]
         sides.append(lax.ppermute(spectra[m], everyone, route))
-    gathered = call(
-        functools.partial(gather_kernel, members),
-        (shape((members * slots, BOX // n_rows, 2 * part), bf16),) * n_planes,
-        sides, [VMEM] * members,
-        flops=total * slots * BOX * BOX // 8,
-    )
-
-    arrived = [gathered[0]]
-    for k in range(1, n_planes):
-        route = [(d, (d + k * members) % total) for d in range(total)]
-        arrived.append(lax.ppermute(gathered[k], everyone, route))
+
+    def across_planes(blocks):
+        count = len(blocks)
+        gathered = call(
+            functools.partial(gather_kernel, count),
+            (shape((count * slots, BOX // n_rows, 2 * part), bf16),) * n_planes,
+            blocks, [VMEM] * count,
+            flops=count * slots * BOX * BOX,
+        )
+        arrived = [gathered[0]]
+        for k in range(1, n_planes):
+            route = [(d, (d + k * members) % total) for d in range(total)]
+            arrived.append(lax.ppermute(gathered[k], everyone, route))
+        return arrived
+
+    early = members // 2
+    arrived = across_planes(sides[:early]) + across_planes(sides[early:])
 
     def source_order(values):
         values = values.reshape(n_planes, members, slots)
         ids = jnp.arange(max(n_planes, members), dtype=jnp.int32)
         values = values[jnp.mod(plane - ids[:n_planes], n_planes)]
-        return values[:, member ^ ids[:members]].reshape(-1)
+        values = values[:, member ^ ids[:members]].reshape(n_planes, members // early, early, slots)
+        return jnp.transpose(values, (1, 0, 2, 3)).reshape(-1)
 
     half = slab // 2
     place = half_index * n_rows + row_index
@@ -649,6 +653,7 @@
         [place.reshape(1), mixed, table(first), table(turns_both)], [SMEM, VMEM, HBM, HBM],
         scratch=[pltpu.VMEM((POINTS, half, BOX), f32)] * 4
         + [pltpu.VMEM((half, width), f32), pltpu.VMEM((4, 8, width), f32)]
+        + [pltpu.VMEM((POINTS // GROUP, GROUP * slab, BOX), bf16)]
         + fetched(first, turns_both),
         flops=8 * slab * width * 2 * BOX,
     )
@@ -671,11 +676,10 @@
         means_kernel,
         shape((CLASSES, 2, BOX // n_rows, part), f32),
         [labels_here, lives_here, divisor, *arrived], [SMEM] * 3 + [VMEM] * len(arrived),
-        scratch=[pltpu.VMEM((CLASSES, BOX // n_rows, 2 * part), f32)] * n_planes,
+        scratch=[pltpu.VMEM((CLASSES, BOX // n_rows, 2 * part), f32)] * SUMS,
         flops=4 * total * slots * BOX * BOX,
     )
     return (power, class_means)
-
 
 def fits(mesh, micrograph):
     height, quarter = micrograph.shape
@@ -693,7 +697,6 @@
         and n_rows == 8
     )
 
-
 def solution(mesh):
     in_specs = (P("rows", "half"), P(), P(), P(), P("rows", "half", None, None))
     out_specs = (P("half", "rows", None), P(None, None, "rows", "half"))

time: 159 us -> 135 us (0.85)
  the two profiles are of different devices: /device:TPU:9 before, /device:TPU:0 now
where the time goes in v4:
time: 135 us; the launch traced here: 132 us
  waiting for transfers between devices  56.3 us (42%)
  starting transfers between devices  36.3 us (27%)
  Pallas kernels  28.6 us (21%)
  local copies, waits for them, and re-layouts  9.42 us (7%)
    pallas_call x9, Pallas kernels, call(): pl.pallas_call(kernel, out_shape=out, in_specs=specs, out_specs=(VMEM,) *...  28.6 us
    ppermute x6, waiting for transfers between devices, across_planes(): arrived.append(lax.ppermute(gathered[k], everyone, route))  24.8 us
    ppermute x3, waiting for transfers between devices, swapped(): return lax.ppermute(block, axis, route)  19 us
    all_to_all x1, waiting for transfers between devices, fast_device(): ready = lax.all_to_all(ready, 'half', 0, 0, tiled=True)  11.6 us
    ppermute x6, starting transfers between devices, across_planes(): arrived.append(lax.ppermute(gathered[k], everyone, route))  11.4 us
    ppermute x7, starting transfers between devices, fast_device(): sides.append(lax.ppermute(spectra[m], everyone, route))  6.29 us
    all_to_all x1, starting transfers between devices, fast_device(): mixed = lax.all_to_all(mixed, everyone, 0, 0, tiled=True)  5.6 us
    all_to_all x1, starting transfers between devices, fast_device(): ready = lax.all_to_all(ready, 'half', 0, 0, tiled=True)  4.39 us
  transfers between devices with their start and end apart: 21, of which 8 were waited for; matrix products, arithmetic and copies ran while one was open for 6% of the time, Pallas kernels for 18%

profile of v4, /device:TPU:0, one launch (start us, length us, event | category | flops | bytes accessed | tf_op | source)
XLA Modules:
  0.0 132.5 jit_solution(2361039503385289673)
XLA Ops:
  0.6 1.2 copy-done
  1.9 3.0 %shard_map.113 = bf16[4,16,64,128]{3,2,1,0:T(8,128)(2,1)} custom-call(bf16[512,1024]{1,0:T(8,128)(2,1)S(1)} %copy-done), custom_call_target="tpu_custom_call" | custom-call | flops 1610612736 | bytes 2097152 | tf_op jit(solution)/shard_map/pallas_call | solution.py:160
  4.8 4.4 %all-to-all-start = ((bf16[4,16,64,128]{3,2,1,0:T(8,128)(2,1)}), bf16[4,16,64,128]{3,2,1,0:T(8,128)(2,1)S(1)}, u32[]{:S(2)}, u32[]{:S(2)}) async-start(bf16[4,16,64,128]{3,2,1,0:T(8,128)(2,1)} %shard_map.113), calls=%async_computation | async-start | bytes 2097152 | tf_op jit(solution)/shard_map/all_to_all | solution.py:568
  9.2 0.8 slice.8
  10.0 1.4 %collective-permute-start.2 = (bf16[256,1024]{1,0:T(8,128)(2,1)}, bf16[256,1024]{1,0:T(8,128)(2,1)}, u32[]{:S(2)}, u32[]{:S(2)}) collective-permute-start(bf16[256,1024]{1,0:T(8,128)(2,1)} %slice.8), channel_id=1, source_target_pairs={{4,0},{8,4},{12,8},{16,12},{20,16},{24,20},{28,24},{5,1},{9,5},{13... | collective-permute-start | bytes 1572872 | tf_op jit(solution)/shard_map/ppermute | solution.py:25
  12.0 11.6 %all-to-all-done.y_ref = bf16[4,16,64,128]{3,2,1,0:T(8,128)(2,1)S(1)} async-done(((bf16[4,16,64,128]{3,2,1,0:T(8,128)(2,1)}), bf16[4,16,64,128]{3,2,1,0:T(8,128)(2,1)S(1)}, u32[]{:S(2)}, u32[]{:S(2)}) %all-to-all-start) | async-done | bytes 1048608 | tf_op jit(solution)/shard_map/all_to_all | solution.py:568
  23.6 5.3 %shard_map.114 = bf16[32,4,32,128]{3,2,1,0:T(8,128)(2,1)} custom-call(bf16[4,16,64,128]{3,2,1,0:T(8,128)(2,1)S(1)} %all-to-all-done.y_ref, bf16[2,256,512]{2,1,0:T(8,128)(2,1)} %constant.135.clone.w_hbm, f32[2,16,1,256]{3,2,1,0:T(1,128)} %constant.136.clone.t_hbm), custom_call_target="tpu_custom_call" | custom-call | flops 1073741824 | bytes 2654208 | tf_op jit(solution)/shard_map/pallas_call | solution.py:160
  28.9 5.6 %all-to-all-start.1 = ((bf16[32,4,32,128]{3,2,1,0:T(8,128)(2,1)}), bf16[32,4,32,128]{3,2,1,0:T(8,128)(2,1)S(1)}, u32[]{:S(2)}, u32[]{:S(2)}) async-start(bf16[32,4,32,128]{3,2,1,0:T(8,128)(2,1)} %shard_map.114), calls=%async_computation.1 | async-start | bytes 2097152 | tf_op jit(solution)/shard_map/all_to_all | solution.py:578
  35.6 1.3 collective-permute-done.4.low2_ref
  36.9 3.1 %shard_map.117 = (bf16[4,256,256]{2,1,0:T(8,128)(2,1)S(1)}, bf16[4,256,256]{2,1,0:T(8,128)(2,1)}) custom-call(s32[17]{0:T(128)S(1)} %pad_add_fusion.2.at_ref, bf16[512,1024]{1,0:T(8,128)(2,1)S(1)} %copy-done.1, bf16[256,1024]{1,0:T(8,128)(2,1)} %collective-permute-done.2.low_ref, bf16[512,1024]{1,0:T(8,128)(2,1)S(1)} %collective-permute-done.3.x2_ref, ...), custom_call_target="tpu_custom_call" | custom-call | flops 5242880 | bytes 4194372 | tf_op jit(solution)/shard_map/pallas_call | solution.py:160
  40.0 0.8 copy-done.2
  40.8 1.8 %collective-permute-start.5 = (bf16[4,256,256]{2,1,0:T(8,128)(2,1)}, bf16[4,256,256]{2,1,0:T(8,128)(2,1)S(1)}, u32[]{:S(2)}, u32[]{:S(2)}) collective-permute-start(bf16[4,256,256]{2,1,0:T(8,128)(2,1)} %get-tuple-element.27), channel_id=1, source_target_pairs={{0,2},{1,3},{2,0},{3,1},{4,6},{5,7},{6,4},{7,5},{8,10},{9,11},{10,... | collective-permute-start | bytes 1572872 | tf_op jit(solution)/shard_map/ppermute | solution.py:527
  43.0 17.7 %collective-permute-done.5.q_ref = bf16[4,256,256]{2,1,0:T(8,128)(2,1)S(1)} collective-permute-done((bf16[4,256,256]{2,1,0:T(8,128)(2,1)}, bf16[4,256,256]{2,1,0:T(8,128)(2,1)S(1)}, u32[]{:S(2)}, u32[]{:S(2)}) %collective-permute-start.5) | collective-permute-done | bytes 524320 | tf_op jit(solution)/shard_map/ppermute | solution.py:527
  60.7 1.0 copy-done.3
  61.7 6.6 %shard_map.118 = (bf16[4,4,32,128]{3,2,1,0:T(8,128)(2,1)S(1)}, bf16[4,4,32,128]{3,2,1,0:T(8,128)(2,1)S(1)}, bf16[4,4,32,128]{3,2,1,0:T(8,128)(2,1)S(1)}, bf16[4,...) custom-call(s32[11]{0:T(128)S(1)} %pad_add_fusion.at_ref, ...), custom_call_target="tpu_custom_call" | custom-call | flops 2684354560 | bytes 3670060 | tf_op jit(solution)/shard_map/pallas_call | solution.py:160
  68.4 1.0 collective-permute-start.7
  69.4 0.9 collective-permute-start.8
  71.4 1.5 %collective-permute-start.12 = (bf16[4,4,32,128]{3,2,1,0:T(8,128)(2,1)}, bf16[4,4,32,128]{3,2,1,0:T(8,128)(2,1)S(1)}, u32[]{:S(2)}, u32[]{:S(2)}) collective-permute-start(bf16[4,4,32,128]{3,2,1,0:T(8,128)(2,1)} %get-tuple-element.36), channel_id=1, source_target_pairs={{0,4},{1,5},{2,6},{3,7},{4,0},{5,1},{6,2},{7,3},{8,12},{9,13},{10,... | collective-permute-start | bytes 393224 | tf_op jit(solution)/shard_map/ppermute | solution.py:622
  73.1 1.6 %collective-permute-start.14 = (bf16[4,4,32,128]{3,2,1,0:T(8,128)(2,1)}, bf16[4,4,32,128]{3,2,1,0:T(8,128)(2,1)S(1)}, u32[]{:S(2)}, u32[]{:S(2)}) collective-permute-start(bf16[4,4,32,128]{3,2,1,0:T(8,128)(2,1)} %get-tuple-element.38), channel_id=1, source_target_pairs={{0,6},{1,7},{2,4},{3,5},{4,2},{5,3},{6,0},{7,1},{8,14},{9,15},{10,... | collective-permute-start | bytes 393224 | tf_op jit(solution)/shard_map/ppermute | solution.py:622
  74.8 1.0 collective-permute-start.15
  77.3 2.0 %collective-permute-start.9 = (bf16[16,32,128]{2,1,0:T(8,128)(2,1)}, bf16[16,32,128]{2,1,0:T(8,128)(2,1)S(1)}, u32[]{:S(2)}, u32[]{:S(2)}) collective-permute-start(bf16[16,32,128]{2,1,0:T(8,128)(2,1)} %get-tuple-element.33), channel_id=1, source_target_pairs={{0,8},{1,9},{2,10},{3,11},{4,12},{5,13},{6,14},{7,15},{8,16},{9,17... | collective-permute-start | bytes 393224 | tf_op jit(solution)/shard_map/ppermute | solution.py:635
  79.3 4.5 %shard_map.115 = (f32[64,4096]{1,0:T(8,128)S(1)}, bf16[64,4096]{1,0:T(8,128)(2,1)S(1)}, f32[32,128]{1,0:T(8,128)S(1)}) custom-call(s32[1]{0:T(128)} %bitcast.1.place_ref, bf16[32,4,32,128]{3,2,1,0:T(8,128)(2,1)S(1)} %all-to-all-done.1.z_ref, bf16[2,256,512]{2,1,0:T(8,128)(2,1)} %constant.135.clone.w_hbm, f32[4,16,1,256]{3,2,1,0:T(1,128)} %constant.139.clone.t_hbm), custom_call_target="tpu_custom_call" | custom-call | flops 2147483648 | bytes 3227652 | tf_op jit(solution)/shard_map/pallas_call | solution.py:160
  83.9 2.2 %collective-permute-start.10 = (bf16[16,32,128]{2,1,0:T(8,128)(2,1)}, bf16[16,32,128]{2,1,0:T(8,128)(2,1)S(1)}, u32[]{:S(2)}, u32[]{:S(2)}) collective-permute-start(bf16[16,32,128]{2,1,0:T(8,128)(2,1)} %get-tuple-element.34), channel_id=1, source_target_pairs={{0,16},{1,17},{2,18},{3,19},{4,20},{5,21},{6,22},{7,23},{8,24},{9,... | collective-permute-start | bytes 393224 | tf_op jit(solution)/shard_map/ppermute | solution.py:635
  86.0 1.9 %collective-permute-start = (bf16[64,4096]{1,0:T(8,128)(2,1)S(1)}, bf16[64,4096]{1,0:T(8,128)(2,1)S(1)}, u32[]{:S(2)}, u32[]{:S(2)}) collective-permute-start(bf16[64,4096]{1,0:T(8,128)(2,1)S(1)} %get-tuple-element.24), channel_id=1, source_target_pairs={{0,31},{1,30},{2,29},{3,28},{4,27},{5,26},{6,25},{7,24},{8,23},{9,... | collective-permute-start | bytes 1572872 | tf_op jit(solution)/shard_map/ppermute | solution.py:660
  87.9 2.1 %collective-permute-start.11 = (bf16[16,32,128]{2,1,0:T(8,128)(2,1)}, bf16[16,32,128]{2,1,0:T(8,128)(2,1)S(1)}, u32[]{:S(2)}, u32[]{:S(2)}) collective-permute-start(bf16[16,32,128]{2,1,0:T(8,128)(2,1)} %get-tuple-element.35), channel_id=1, source_target_pairs={{0,24},{1,25},{2,26},{3,27},{4,28},{5,29},{6,30},{7,31},{8,0},{9,1... | collective-permute-start | bytes 393224 | tf_op jit(solution)/shard_map/ppermute | solution.py:635
  91.4 14.2 %collective-permute-done.10.refs_2_ = bf16[16,32,128]{2,1,0:T(8,128)(2,1)S(1)} collective-permute-done((bf16[16,32,128]{2,1,0:T(8,128)(2,1)}, bf16[16,32,128]{2,1,0:T(8,128)(2,1)S(1)}, u32[]{:S(2)}, u32[]{:S(2)}) %collective-permute-start.10) | collective-permute-done | bytes 131104 | tf_op jit(solution)/shard_map/ppermute | solution.py:635
  105.6 4.5 %collective-permute-start.18 = (bf16[16,32,128]{2,1,0:T(8,128)(2,1)S(1)}, bf16[16,32,128]{2,1,0:T(8,128)(2,1)S(1)}, u32[]{:S(2)}, u32[]{:S(2)}) collective-permute-start(bf16[16,32,128]{2,1,0:T(8,128)(2,1)S(1)} %get-tuple-element.43), channel_id=1, source_target_pairs={{0,24},{1,25},{2,26},{3,27},{4,28},{5,29},{6,30},{7,31},{8,0},{9,1... | collective-permute-start | bytes 393224 | tf_op jit(solution)/shard_map/ppermute | solution.py:635
  110.6 2.7 %collective-permute-start.1 = (f32[32,128]{1,0:T(8,128)}, f32[32,128]{1,0:T(8,128)S(1)}, u32[]{:S(2)}, u32[]{:S(2)}) collective-permute-start(f32[32,128]{1,0:T(8,128)} %copy-done.4), channel_id=1, source_target_pairs={{4,31},{8,27},{12,23},{16,19},{20,15},{24,11},{28,7},{1,3},{5,30},... | collective-permute-start | bytes 49160 | tf_op jit(solution)/shard_map/ppermute | solution.py:663
  113.4 0.8 copy.42
  117.7 10.2 %collective-permute-done.17.refs_6_ = bf16[16,32,128]{2,1,0:T(8,128)(2,1)S(1)} collective-permute-done((bf16[16,32,128]{2,1,0:T(8,128)(2,1)}, bf16[16,32,128]{2,1,0:T(8,128)(2,1)S(1)}, u32[]{:S(2)}, u32[]{:S(2)}) %collective-permute-start.17) | collective-permute-done | bytes 131104 | tf_op jit(solution)/shard_map/ppermute | solution.py:635
  127.8 3.2 %shard_map.121 = f32[50,2,32,64]{3,2,1,0:T(8,128)} custom-call(s32[128]{0:T(128)S(1)} %reshape.68.label_ref, s32[128]{0:T(128)S(1)} %reshape.71.live_ref, f32[50]{0:T(128)S(1)} %maximum_convert_fusion.divisor_ref, bf16[16,32,128]{2,1,0:T(8,128)(2,1)S(1)} %get-tuple-element.32.refs_0_, bf16[16,32,128]{2,1,0:T(8,128)(2,1)S(1)} %collective-permute-done.9.refs_1_, ...), custom_call_target="tpu_custom_call" | custom-call | flops 33554432 | bytes 1869000 | tf_op jit(solution)/shard_map/pallas_call | solution.py:160
  131.0 1.5 %shard_map.116 = f32[128,4096]{1,0:T(8,128)} custom-call(s32[1]{0:T(128)} %bitcast.place_ref, f32[64,4096]{1,0:T(8,128)S(1)} %get-tuple-element.23.own_ref, bf16[64,4096]{1,0:T(8,128)(2,1)S(1)} %collective-permute-done.far_ref, f32[32,128]{1,0:T(8,128)S(1)} %collective-permute-done.1.edge_ref), custom_call_target="tpu_custom_call" | custom-call | flops 524288 | bytes 3686404 | tf_op jit(solution)/shard_map/pallas_call | solution.py:160
  (83 shorter events, 10.4 us)
Async XLA Ops:
  0.6 1.2 copy-start
  4.8 4.4 %copy-start.1 = (bf16[512,1024]{1,0:T(8,128)(2,1)S(1)}, bf16[512,1024]{1,0:T(8,128)(2,1)}, u32[]{:S(2)}) copy-start(bf16[512,1024]{1,0:T(8,128)(2,1)} %x_ref.3) | copy-start | bytes 3145732
  4.8 18.8 %all-to-all-start = ((bf16[4,16,64,128]{3,2,1,0:T(8,128)(2,1)}), bf16[4,16,64,128]{3,2,1,0:T(8,128)(2,1)S(1)}, u32[]{:S(2)}, u32[]{:S(2)}) async-start(bf16[4,16,64,128]{3,2,1,0:T(8,128)(2,1)} %shard_map.113), calls=%async_computation | async-start | bytes 2097152 | tf_op jit(solution)/shard_map/all_to_all | solution.py:568
  10.0 24.9 %copy-start.7 = (s32[8,4,4,2]{0,3,2,1:T(2,128)S(1)}, s32[8,4,4,2]{0,3,2,1:T(2,128)}, u32[]{:S(2)}) copy-start(s32[8,4,4,2]{0,3,2,1:T(2,128)} %param.11) | copy-start | bytes 3076
  10.0 24.5 %collective-permute-start.2 = (bf16[256,1024]{1,0:T(8,128)(2,1)}, bf16[256,1024]{1,0:T(8,128)(2,1)}, u32[]{:S(2)}, u32[]{:S(2)}) collective-permute-start(bf16[256,1024]{1,0:T(8,128)(2,1)} %slice.8), channel_id=1, source_target_pairs={{4,0},{8,4},{12,8},{16,12},{20,16},{24,20},{28,24},{5,1},{9,5},{13... | collective-permute-start | bytes 1572872 | tf_op jit(solution)/shard_map/ppermute | solution.py:25
  11.5 25.5 %collective-permute-start.3 = (bf16[512,1024]{1,0:T(8,128)(2,1)S(1)}, bf16[512,1024]{1,0:T(8,128)(2,1)S(1)}, u32[]{:S(2)}, u32[]{:S(2)}) collective-permute-start(bf16[512,1024]{1,0:T(8,128)(2,1)S(1)} %copy-done.1), channel_id=1, source_target_pairs={{0,1},{1,0},{2,3},{3,2},{4,5},{5,4},{6,7},{7,6},{8,9},{9,8},{10,11... | collective-permute-start | bytes 3145736 | tf_op jit(solution)/shard_map/ppermute | solution.py:527
  28.9 50.4 %all-to-all-start.1 = ((bf16[32,4,32,128]{3,2,1,0:T(8,128)(2,1)}), bf16[32,4,32,128]{3,2,1,0:T(8,128)(2,1)S(1)}, u32[]{:S(2)}, u32[]{:S(2)}) async-start(bf16[32,4,32,128]{3,2,1,0:T(8,128)(2,1)} %shard_map.114), calls=%async_computation.1 | async-start | bytes 2097152 | tf_op jit(solution)/shard_map/all_to_all | solution.py:578
  34.5 8.2 %copy-start.8 = (s32[1,1,4,2]{2,3,1,0:T(2,128)S(1)}, s32[1,1,4,2]{2,3,1,0:T(2,128)}, u32[]{:S(2)}) copy-start(s32[1,1,4,2]{2,3,1,0:T(2,128)} %param.14) | copy-start | bytes 100
  34.6 2.3 %collective-permute-start.4 = (bf16[256,1024]{1,0:T(8,128)(2,1)}, bf16[256,1024]{1,0:T(8,128)(2,1)}, u32[]{:S(2)}, u32[]{:S(2)}) collective-permute-start(bf16[256,1024]{1,0:T(8,128)(2,1)} %collective-permute-done.2.low_ref), channel_id=1, source_target_pairs={{0,1},{1,0},{2,3},{3,2},{4,5},{5,4},{6,7},{7,6},{8,9},{9,8},{10,11... | collective-permute-start | bytes 1572872 | tf_op jit(solution)/shard_map/ppermute | solution.py:527
  40.0 0.8 copy-start.2
  40.8 19.8 %collective-permute-start.5 = (bf16[4,256,256]{2,1,0:T(8,128)(2,1)}, bf16[4,256,256]{2,1,0:T(8,128)(2,1)S(1)}, u32[]{:S(2)}, u32[]{:S(2)}) collective-permute-start(bf16[4,256,256]{2,1,0:T(8,128)(2,1)} %get-tuple-element.27), channel_id=1, source_target_pairs={{0,2},{1,3},{2,0},{3,1},{4,6},{5,7},{6,4},{7,5},{8,10},{9,11},{10,... | collective-permute-start | bytes 1572872 | tf_op jit(solution)/shard_map/ppermute | solution.py:527
  60.7 1.0 copy-start.3
  61.7 9.1 %copy-start.5 = (s32[8,4,4]{0,2,1:T(4,128)S(1)}, s32[8,4,4]{0,2,1:T(4,128)}, u32[]{:S(2)}) copy-start(s32[8,4,4]{0,2,1:T(4,128)} %param.12) | copy-start | bytes 1540
  61.7 9.3 %copy-start.6 = (s32[8,4,4]{0,2,1:T(4,128)S(1)}, s32[8,4,4]{0,2,1:T(4,128)}, u32[]{:S(2)}) copy-start(s32[8,4,4]{0,2,1:T(4,128)} %param.13) | copy-start | bytes 1540
  68.3 4.8 %collective-permute-start.6 = (bf16[4,4,32,128]{3,2,1,0:T(8,128)(2,1)S(1)}, bf16[4,4,32,128]{3,2,1,0:T(8,128)(2,1)S(1)}, u32[]{:S(2)}, u32[]{:S(2)}) collective-permute-start(bf16[4,4,32,128]{3,2,1,0:T(8,128)(2,1)S(1)} %get-tuple-element.29), channel_id=1, source_target_pairs={{0,1},{1,0},{2,3},{3,2},{4,5},{5,4},{6,7},{7,6},{8,9},{9,8},{10,11... | collective-permute-start | bytes 393224 | tf_op jit(solution)/shard_map/ppermute | solution.py:622
  68.4 6.4 %collective-permute-start.7 = (bf16[4,4,32,128]{3,2,1,0:T(8,128)(2,1)S(1)}, bf16[4,4,32,128]{3,2,1,0:T(8,128)(2,1)S(1)}, u32[]{:S(2)}, u32[]{:S(2)}) collective-permute-start(bf16[4,4,32,128]{3,2,1,0:T(8,128)(2,1)S(1)} %get-tuple-element.30), channel_id=1, source_target_pairs={{0,2},{1,3},{2,0},{3,1},{4,6},{5,7},{6,4},{7,5},{8,10},{9,11},{10,... | collective-permute-start | bytes 393224 | tf_op jit(solution)/shard_map/ppermute | solution.py:622
  69.4 7.2 %collective-permute-start.8 = (bf16[4,4,32,128]{3,2,1,0:T(8,128)(2,1)S(1)}, bf16[4,4,32,128]{3,2,1,0:T(8,128)(2,1)S(1)}, u32[]{:S(2)}, u32[]{:S(2)}) collective-permute-start(bf16[4,4,32,128]{3,2,1,0:T(8,128)(2,1)S(1)} %get-tuple-element.31), channel_id=1, source_target_pairs={{0,3},{1,2},{2,1},{3,0},{4,7},{5,6},{6,5},{7,4},{8,11},{9,10},{10,... | collective-permute-start | bytes 393224 | tf_op jit(solution)/shard_map/ppermute | solution.py:622
  71.4 12.5 %collective-permute-start.12 = (bf16[4,4,32,128]{3,2,1,0:T(8,128)(2,1)}, bf16[4,4,32,128]{3,2,1,0:T(8,128)(2,1)S(1)}, u32[]{:S(2)}, u32[]{:S(2)}) collective-permute-start(bf16[4,4,32,128]{3,2,1,0:T(8,128)(2,1)} %get-tuple-element.36), channel_id=1, source_target_pairs={{0,4},{1,5},{2,6},{3,7},{4,0},{5,1},{6,2},{7,3},{8,12},{9,13},{10,... | collective-permute-start | bytes 393224 | tf_op jit(solution)/shard_map/ppermute | solution.py:622
  72.8 13.2 %collective-permute-start.13 = (bf16[4,4,32,128]{3,2,1,0:T(8,128)(2,1)}, bf16[4,4,32,128]{3,2,1,0:T(8,128)(2,1)S(1)}, u32[]{:S(2)}, u32[]{:S(2)}) collective-permute-start(bf16[4,4,32,128]{3,2,1,0:T(8,128)(2,1)} %get-tuple-element.37), channel_id=1, source_target_pairs={{0,5},{1,4},{2,7},{3,6},{4,1},{5,0},{6,3},{7,2},{8,13},{9,12},{10,... | collective-permute-start | bytes 393224 | tf_op jit(solution)/shard_map/ppermute | solution.py:622
  73.1 14.8 %collective-permute-start.14 = (bf16[4,4,32,128]{3,2,1,0:T(8,128)(2,1)}, bf16[4,4,32,128]{3,2,1,0:T(8,128)(2,1)S(1)}, u32[]{:S(2)}, u32[]{:S(2)}) collective-permute-start(bf16[4,4,32,128]{3,2,1,0:T(8,128)(2,1)} %get-tuple-element.38), channel_id=1, source_target_pairs={{0,6},{1,7},{2,4},{3,5},{4,2},{5,3},{6,0},{7,1},{8,14},{9,15},{10,... | collective-permute-start | bytes 393224 | tf_op jit(solution)/shard_map/ppermute | solution.py:622
  74.8 15.2 %collective-permute-start.15 = (bf16[4,4,32,128]{3,2,1,0:T(8,128)(2,1)S(1)}, bf16[4,4,32,128]{3,2,1,0:T(8,128)(2,1)S(1)}, u32[]{:S(2)}, u32[]{:S(2)}) collective-permute-start(bf16[4,4,32,128]{3,2,1,0:T(8,128)(2,1)S(1)} %get-tuple-element.39), channel_id=1, source_target_pairs={{0,7},{1,6},{2,5},{3,4},{4,3},{5,2},{6,1},{7,0},{8,15},{9,14},{10,... | collective-permute-start | bytes 393224 | tf_op jit(solution)/shard_map/ppermute | solution.py:622
  77.3 13.5 %collective-permute-start.9 = (bf16[16,32,128]{2,1,0:T(8,128)(2,1)}, bf16[16,32,128]{2,1,0:T(8,128)(2,1)S(1)}, u32[]{:S(2)}, u32[]{:S(2)}) collective-permute-start(bf16[16,32,128]{2,1,0:T(8,128)(2,1)} %get-tuple-element.33), channel_id=1, source_target_pairs={{0,8},{1,9},{2,10},{3,11},{4,12},{5,13},{6,14},{7,15},{8,16},{9,17... | collective-permute-start | bytes 393224 | tf_op jit(solution)/shard_map/ppermute | solution.py:635
  79.3 10.7 %copy-start.9 = (s32[4]{0:T(128)S(1)}, s32[4]{0:T(128)}, u32[]{:S(2)}) copy-start(s32[4]{0:T(128)} %compare_select_fusion.1) | copy-start | bytes 52
  83.8 4.1 %copy-start.4 = (f32[32,128]{1,0:T(8,128)}, f32[32,128]{1,0:T(8,128)S(1)}, u32[]{:S(2)}) copy-start(f32[32,128]{1,0:T(8,128)S(1)} %get-tuple-element.25) | copy-start | bytes 49156
  83.9 21.8 %collective-permute-start.10 = (bf16[16,32,128]{2,1,0:T(8,128)(2,1)}, bf16[16,32,128]{2,1,0:T(8,128)(2,1)S(1)}, u32[]{:S(2)}, u32[]{:S(2)}) collective-permute-start(bf16[16,32,128]{2,1,0:T(8,128)(2,1)} %get-tuple-element.34), channel_id=1, source_target_pairs={{0,16},{1,17},{2,18},{3,19},{4,20},{5,21},{6,22},{7,23},{8,24},{9,... | collective-permute-start | bytes 393224 | tf_op jit(solution)/shard_map/ppermute | solution.py:635
  86.0 45.0 %collective-permute-start = (bf16[64,4096]{1,0:T(8,128)(2,1)S(1)}, bf16[64,4096]{1,0:T(8,128)(2,1)S(1)}, u32[]{:S(2)}, u32[]{:S(2)}) collective-permute-start(bf16[64,4096]{1,0:T(8,128)(2,1)S(1)} %get-tuple-element.24), channel_id=1, source_target_pairs={{0,31},{1,30},{2,29},{3,28},{4,27},{5,26},{6,25},{7,24},{8,23},{9,... | collective-permute-start | bytes 1572872 | tf_op jit(solution)/shard_map/ppermute | solution.py:660
  87.9 22.6 %collective-permute-start.11 = (bf16[16,32,128]{2,1,0:T(8,128)(2,1)}, bf16[16,32,128]{2,1,0:T(8,128)(2,1)S(1)}, u32[]{:S(2)}, u32[]{:S(2)}) collective-permute-start(bf16[16,32,128]{2,1,0:T(8,128)(2,1)} %get-tuple-element.35), channel_id=1, source_target_pairs={{0,24},{1,25},{2,26},{3,27},{4,28},{5,29},{6,30},{7,31},{8,0},{9,1... | collective-permute-start | bytes 393224 | tf_op jit(solution)/shard_map/ppermute | solution.py:635
  90.8 26.8 %collective-permute-start.16 = (bf16[16,32,128]{2,1,0:T(8,128)(2,1)}, bf16[16,32,128]{2,1,0:T(8,128)(2,1)S(1)}, u32[]{:S(2)}, u32[]{:S(2)}) collective-permute-start(bf16[16,32,128]{2,1,0:T(8,128)(2,1)} %get-tuple-element.41), channel_id=1, source_target_pairs={{0,8},{1,9},{2,10},{3,11},{4,12},{5,13},{6,14},{7,15},{8,16},{9,17... | collective-permute-start | bytes 393224 | tf_op jit(solution)/shard_map/ppermute | solution.py:635
  90.8 37.0 %collective-permute-start.17 = (bf16[16,32,128]{2,1,0:T(8,128)(2,1)}, bf16[16,32,128]{2,1,0:T(8,128)(2,1)S(1)}, u32[]{:S(2)}, u32[]{:S(2)}) collective-permute-start(bf16[16,32,128]{2,1,0:T(8,128)(2,1)} %get-tuple-element.42), channel_id=1, source_target_pairs={{0,16},{1,17},{2,18},{3,19},{4,20},{5,21},{6,22},{7,23},{8,24},{9,... | collective-permute-start | bytes 393224 | tf_op jit(solution)/shard_map/ppermute | solution.py:635
  105.6 22.2 %collective-permute-start.18 = (bf16[16,32,128]{2,1,0:T(8,128)(2,1)S(1)}, bf16[16,32,128]{2,1,0:T(8,128)(2,1)S(1)}, u32[]{:S(2)}, u32[]{:S(2)}) collective-permute-start(bf16[16,32,128]{2,1,0:T(8,128)(2,1)S(1)} %get-tuple-element.43), channel_id=1, source_target_pairs={{0,24},{1,25},{2,26},{3,27},{4,28},{5,29},{6,30},{7,31},{8,0},{9,1... | collective-permute-start | bytes 393224 | tf_op jit(solution)/shard_map/ppermute | solution.py:635
  110.6 20.4 %collective-permute-start.1 = (f32[32,128]{1,0:T(8,128)}, f32[32,128]{1,0:T(8,128)S(1)}, u32[]{:S(2)}, u32[]{:S(2)}) collective-permute-start(f32[32,128]{1,0:T(8,128)} %copy-done.4), channel_id=1, source_target_pairs={{4,31},{8,27},{12,23},{16,19},{20,15},{24,11},{28,7},{1,3},{5,30},... | collective-permute-start | bytes 49160 | tf_op jit(solution)/shard_map/ppermute | solution.py:663

commit v5 on v4

--- a/solution.py
+++ b/solution.py
@@ -258,7 +258,7 @@
         turned_ref[g] = jnp.concatenate(blocks, axis=1).T
         return carry
 
-    lax.fori_loop(0, POINTS // GROUP, turn_blocks, 0)
+    lax.fori_loop(0, POINTS // GROUP, turn_blocks, 0, unroll=2)
     for copy in copies:
         copy.wait()
 
@@ -274,7 +274,7 @@
             im_ref[c] = im * tc - re * ts
         return carry
 
-    lax.fori_loop(0, POINTS // GROUP, first, 0)
+    lax.fori_loop(0, POINTS // GROUP, first, 0, unroll=2)
     tiles = span // 16
 
     def second(t, carry):
@@ -300,7 +300,7 @@
                 z_ref[to, m, pl.ds(at, 16), :] = both.astype(bf16)
         return carry
 
-    lax.fori_loop(0, share // 16, second, 0)
+    lax.fori_loop(0, share // 16, second, 0, unroll=2)
 
 def columns_kernel(n_rows, n_half, place_ref, z_ref, w_hbm, t_hbm, own_ref, far_ref, edge_ref,
                    re_ref, im_ref, mre_ref, mim_ref, mirror_ref, raw_ref, turned_ref, w_ref, t_ref, sems):
@@ -320,7 +320,7 @@
         turned_ref[g] = jnp.concatenate(blocks, axis=1).T
         return carry
 
-    lax.fori_loop(0, POINTS // GROUP, turn_blocks, 0)
+    lax.fori_loop(0, POINTS // GROUP, turn_blocks, 0, unroll=2)
     for copy in copies:
         copy.wait()
 
@@ -342,7 +342,7 @@
             mim_ref[r] = im * tc - re * ts
         return carry
 
-    lax.fori_loop(0, POINTS // GROUP, first, 0)
+    lax.fori_loop(0, POINTS // GROUP, first, 0, unroll=2)
 
     def tile(t, raw):
         row = pl.multiple_of(t * 8, 8)
@@ -371,7 +371,7 @@
         tile(t, False)
         return carry
 
-    lax.fori_loop(0, count // 8, second, 0)
+    lax.fori_loop(0, count // 8, second, 0, unroll=2)
     tile(0, True)
     origin = place_ref[0] == 0
     for k in range(width // LANES):

time: 135 us -> 134 us (level)
  no operation moved by 1% of the time
where the time goes in v5:
time: 134 us; the launch traced here: 132 us
  waiting for transfers between devices  56.3 us (42%)
  starting transfers between devices  36.3 us (27%)
  Pallas kernels  27.7 us (21%)
  local copies, waits for them, and re-layouts  9.42 us (7%)
    pallas_call x9, Pallas kernels, call(): pl.pallas_call(kernel, out_shape=out, in_specs=specs, out_specs=(VMEM,) *...  27.7 us
    ppermute x6, waiting for transfers between devices, across_planes(): arrived.append(lax.ppermute(gathered[k], everyone, route))  24.8 us
    ppermute x3, waiting for transfers between devices, swapped(): return lax.ppermute(block, axis, route)  19 us
    all_to_all x1, waiting for transfers between devices, fast_device(): ready = lax.all_to_all(ready, 'half', 0, 0, tiled=True)  11.6 us
    ppermute x6, starting transfers between devices, across_planes(): arrived.append(lax.ppermute(gathered[k], everyone, route))  11.4 us
    ppermute x7, starting transfers between devices, fast_device(): sides.append(lax.ppermute(spectra[m], everyone, route))  6.29 us
    all_to_all x1, starting transfers between devices, fast_device(): mixed = lax.all_to_all(mixed, everyone, 0, 0, tiled=True)  5.6 us
    all_to_all x1, starting transfers between devices, fast_device(): ready = lax.all_to_all(ready, 'half', 0, 0, tiled=True)  4.39 us
  transfers between devices with their start and end apart: 21, of which 8 were waited for; matrix products, arithmetic and copies ran while one was open for 6% of the time, Pallas kernels for 18%

profile of v5, /device:TPU:0, one launch (start us, length us, event | category | flops | bytes accessed | tf_op | source)
XLA Modules:
  0.0 131.5 jit_solution(5869710779132445759)
XLA Ops:
  0.6 1.2 copy-done
  1.9 3.0 %shard_map.113 = bf16[4,16,64,128]{3,2,1,0:T(8,128)(2,1)} custom-call(bf16[512,1024]{1,0:T(8,128)(2,1)S(1)} %copy-done), custom_call_target="tpu_custom_call" | custom-call | flops 1610612736 | bytes 2097152 | tf_op jit(solution)/shard_map/pallas_call | solution.py:160
  4.8 4.4 %all-to-all-start = ((bf16[4,16,64,128]{3,2,1,0:T(8,128)(2,1)}), bf16[4,16,64,128]{3,2,1,0:T(8,128)(2,1)S(1)}, u32[]{:S(2)}, u32[]{:S(2)}) async-start(bf16[4,16,64,128]{3,2,1,0:T(8,128)(2,1)} %shard_map.113), calls=%async_computation | async-start | bytes 2097152 | tf_op jit(solution)/shard_map/all_to_all | solution.py:568
  9.2 0.8 slice.8
  10.0 1.4 %collective-permute-start.2 = (bf16[256,1024]{1,0:T(8,128)(2,1)}, bf16[256,1024]{1,0:T(8,128)(2,1)}, u32[]{:S(2)}, u32[]{:S(2)}) collective-permute-start(bf16[256,1024]{1,0:T(8,128)(2,1)} %slice.8), channel_id=1, source_target_pairs={{4,0},{8,4},{12,8},{16,12},{20,16},{24,20},{28,24},{5,1},{9,5},{13... | collective-permute-start | bytes 1572872 | tf_op jit(solution)/shard_map/ppermute | solution.py:25
  12.0 11.6 %all-to-all-done.y_ref = bf16[4,16,64,128]{3,2,1,0:T(8,128)(2,1)S(1)} async-done(((bf16[4,16,64,128]{3,2,1,0:T(8,128)(2,1)}), bf16[4,16,64,128]{3,2,1,0:T(8,128)(2,1)S(1)}, u32[]{:S(2)}, u32[]{:S(2)}) %all-to-all-start) | async-done | bytes 1048608 | tf_op jit(solution)/shard_map/all_to_all | solution.py:568
  23.6 4.8 %shard_map.114 = bf16[32,4,32,128]{3,2,1,0:T(8,128)(2,1)} custom-call(bf16[4,16,64,128]{3,2,1,0:T(8,128)(2,1)S(1)} %all-to-all-done.y_ref, bf16[2,256,512]{2,1,0:T(8,128)(2,1)} %constant.135.clone.w_hbm, f32[2,16,1,256]{3,2,1,0:T(1,128)} %constant.136.clone.t_hbm), custom_call_target="tpu_custom_call" | custom-call | flops 1073741824 | bytes 2654208 | tf_op jit(solution)/shard_map/pallas_call | solution.py:160
  28.4 5.6 %all-to-all-start.1 = ((bf16[32,4,32,128]{3,2,1,0:T(8,128)(2,1)}), bf16[32,4,32,128]{3,2,1,0:T(8,128)(2,1)S(1)}, u32[]{:S(2)}, u32[]{:S(2)}) async-start(bf16[32,4,32,128]{3,2,1,0:T(8,128)(2,1)} %shard_map.114), calls=%async_computation.1 | async-start | bytes 2097152 | tf_op jit(solution)/shard_map/all_to_all | solution.py:578
  35.1 1.3 collective-permute-done.4.low2_ref
  36.4 3.1 %shard_map.117 = (bf16[4,256,256]{2,1,0:T(8,128)(2,1)S(1)}, bf16[4,256,256]{2,1,0:T(8,128)(2,1)}) custom-call(s32[17]{0:T(128)S(1)} %pad_add_fusion.2.at_ref, bf16[512,1024]{1,0:T(8,128)(2,1)S(1)} %copy-done.1, bf16[256,1024]{1,0:T(8,128)(2,1)} %collective-permute-done.2.low_ref, bf16[512,1024]{1,0:T(8,128)(2,1)S(1)} %collective-permute-done.3.x2_ref, ...), custom_call_target="tpu_custom_call" | custom-call | flops 5242880 | bytes 4194372 | tf_op jit(solution)/shard_map/pallas_call | solution.py:160
  39.5 0.8 copy-done.2
  40.3 1.8 %collective-permute-start.5 = (bf16[4,256,256]{2,1,0:T(8,128)(2,1)}, bf16[4,256,256]{2,1,0:T(8,128)(2,1)S(1)}, u32[]{:S(2)}, u32[]{:S(2)}) collective-permute-start(bf16[4,256,256]{2,1,0:T(8,128)(2,1)} %get-tuple-element.27), channel_id=1, source_target_pairs={{0,2},{1,3},{2,0},{3,1},{4,6},{5,7},{6,4},{7,5},{8,10},{9,11},{10,... | collective-permute-start | bytes 1572872 | tf_op jit(solution)/shard_map/ppermute | solution.py:527
  42.5 17.7 %collective-permute-done.5.q_ref = bf16[4,256,256]{2,1,0:T(8,128)(2,1)S(1)} collective-permute-done((bf16[4,256,256]{2,1,0:T(8,128)(2,1)}, bf16[4,256,256]{2,1,0:T(8,128)(2,1)S(1)}, u32[]{:S(2)}, u32[]{:S(2)}) %collective-permute-start.5) | collective-permute-done | bytes 524320 | tf_op jit(solution)/shard_map/ppermute | solution.py:527
  60.1 1.0 copy-done.3
  61.2 6.6 %shard_map.118 = (bf16[4,4,32,128]{3,2,1,0:T(8,128)(2,1)S(1)}, bf16[4,4,32,128]{3,2,1,0:T(8,128)(2,1)S(1)}, bf16[4,4,32,128]{3,2,1,0:T(8,128)(2,1)S(1)}, bf16[4,...) custom-call(s32[11]{0:T(128)S(1)} %pad_add_fusion.at_ref, ...), custom_call_target="tpu_custom_call" | custom-call | flops 2684354560 | bytes 3670060 | tf_op jit(solution)/shard_map/pallas_call | solution.py:160
  67.9 1.0 collective-permute-start.7
  68.9 0.9 collective-permute-start.8
  70.8 1.5 %collective-permute-start.12 = (bf16[4,4,32,128]{3,2,1,0:T(8,128)(2,1)}, bf16[4,4,32,128]{3,2,1,0:T(8,128)(2,1)S(1)}, u32[]{:S(2)}, u32[]{:S(2)}) collective-permute-start(bf16[4,4,32,128]{3,2,1,0:T(8,128)(2,1)} %get-tuple-element.36), channel_id=1, source_target_pairs={{0,4},{1,5},{2,6},{3,7},{4,0},{5,1},{6,2},{7,3},{8,12},{9,13},{10,... | collective-permute-start | bytes 393224 | tf_op jit(solution)/shard_map/ppermute | solution.py:622
  72.6 1.6 %collective-permute-start.14 = (bf16[4,4,32,128]{3,2,1,0:T(8,128)(2,1)}, bf16[4,4,32,128]{3,2,1,0:T(8,128)(2,1)S(1)}, u32[]{:S(2)}, u32[]{:S(2)}) collective-permute-start(bf16[4,4,32,128]{3,2,1,0:T(8,128)(2,1)} %get-tuple-element.38), channel_id=1, source_target_pairs={{0,6},{1,7},{2,4},{3,5},{4,2},{5,3},{6,0},{7,1},{8,14},{9,15},{10,... | collective-permute-start | bytes 393224 | tf_op jit(solution)/shard_map/ppermute | solution.py:622
  74.3 1.0 collective-permute-start.15
  76.8 2.0 %collective-permute-start.9 = (bf16[16,32,128]{2,1,0:T(8,128)(2,1)}, bf16[16,32,128]{2,1,0:T(8,128)(2,1)S(1)}, u32[]{:S(2)}, u32[]{:S(2)}) collective-permute-start(bf16[16,32,128]{2,1,0:T(8,128)(2,1)} %get-tuple-element.33), channel_id=1, source_target_pairs={{0,8},{1,9},{2,10},{3,11},{4,12},{5,13},{6,14},{7,15},{8,16},{9,17... | collective-permute-start | bytes 393224 | tf_op jit(solution)/shard_map/ppermute | solution.py:635
  78.8 4.1 %shard_map.115 = (f32[64,4096]{1,0:T(8,128)S(1)}, bf16[64,4096]{1,0:T(8,128)(2,1)S(1)}, f32[32,128]{1,0:T(8,128)S(1)}) custom-call(s32[1]{0:T(128)} %bitcast.1.place_ref, bf16[32,4,32,128]{3,2,1,0:T(8,128)(2,1)S(1)} %all-to-all-done.1.z_ref, bf16[2,256,512]{2,1,0:T(8,128)(2,1)} %constant.135.clone.w_hbm, f32[4,16,1,256]{3,2,1,0:T(1,128)} %constant.139.clone.t_hbm), custom_call_target="tpu_custom_call" | custom-call | flops 2147483648 | bytes 3227652 | tf_op jit(solution)/shard_map/pallas_call | solution.py:160
  82.9 2.2 %collective-permute-start.10 = (bf16[16,32,128]{2,1,0:T(8,128)(2,1)}, bf16[16,32,128]{2,1,0:T(8,128)(2,1)S(1)}, u32[]{:S(2)}, u32[]{:S(2)}) collective-permute-start(bf16[16,32,128]{2,1,0:T(8,128)(2,1)} %get-tuple-element.34), channel_id=1, source_target_pairs={{0,16},{1,17},{2,18},{3,19},{4,20},{5,21},{6,22},{7,23},{8,24},{9,... | collective-permute-start | bytes 393224 | tf_op jit(solution)/shard_map/ppermute | solution.py:635
  85.1 1.9 %collective-permute-start = (bf16[64,4096]{1,0:T(8,128)(2,1)S(1)}, bf16[64,4096]{1,0:T(8,128)(2,1)S(1)}, u32[]{:S(2)}, u32[]{:S(2)}) collective-permute-start(bf16[64,4096]{1,0:T(8,128)(2,1)S(1)} %get-tuple-element.24), channel_id=1, source_target_pairs={{0,31},{1,30},{2,29},{3,28},{4,27},{5,26},{6,25},{7,24},{8,23},{9,... | collective-permute-start | bytes 1572872 | tf_op jit(solution)/shard_map/ppermute | solution.py:660
  87.0 2.1 %collective-permute-start.11 = (bf16[16,32,128]{2,1,0:T(8,128)(2,1)}, bf16[16,32,128]{2,1,0:T(8,128)(2,1)S(1)}, u32[]{:S(2)}, u32[]{:S(2)}) collective-permute-start(bf16[16,32,128]{2,1,0:T(8,128)(2,1)} %get-tuple-element.35), channel_id=1, source_target_pairs={{0,24},{1,25},{2,26},{3,27},{4,28},{5,29},{6,30},{7,31},{8,0},{9,1... | collective-permute-start | bytes 393224 | tf_op jit(solution)/shard_map/ppermute | solution.py:635
  90.5 14.2 %collective-permute-done.10.refs_2_ = bf16[16,32,128]{2,1,0:T(8,128)(2,1)S(1)} collective-permute-done((bf16[16,32,128]{2,1,0:T(8,128)(2,1)}, bf16[16,32,128]{2,1,0:T(8,128)(2,1)S(1)}, u32[]{:S(2)}, u32[]{:S(2)}) %collective-permute-start.10) | collective-permute-done | bytes 131104 | tf_op jit(solution)/shard_map/ppermute | solution.py:635
  104.7 4.5 %collective-permute-start.18 = (bf16[16,32,128]{2,1,0:T(8,128)(2,1)S(1)}, bf16[16,32,128]{2,1,0:T(8,128)(2,1)S(1)}, u32[]{:S(2)}, u32[]{:S(2)}) collective-permute-start(bf16[16,32,128]{2,1,0:T(8,128)(2,1)S(1)} %get-tuple-element.43), channel_id=1, source_target_pairs={{0,24},{1,25},{2,26},{3,27},{4,28},{5,29},{6,30},{7,31},{8,0},{9,1... | collective-permute-start | bytes 393224 | tf_op jit(solution)/shard_map/ppermute | solution.py:635
  109.6 2.7 %collective-permute-start.1 = (f32[32,128]{1,0:T(8,128)}, f32[32,128]{1,0:T(8,128)S(1)}, u32[]{:S(2)}, u32[]{:S(2)}) collective-permute-start(f32[32,128]{1,0:T(8,128)} %copy-done.4), channel_id=1, source_target_pairs={{4,31},{8,27},{12,23},{16,19},{20,15},{24,11},{28,7},{1,3},{5,30},... | collective-permute-start | bytes 49160 | tf_op jit(solution)/shard_map/ppermute | solution.py:663
  112.4 0.8 copy.42
  116.7 10.2 %collective-permute-done.17.refs_6_ = bf16[16,32,128]{2,1,0:T(8,128)(2,1)S(1)} collective-permute-done((bf16[16,32,128]{2,1,0:T(8,128)(2,1)}, bf16[16,32,128]{2,1,0:T(8,128)(2,1)S(1)}, u32[]{:S(2)}, u32[]{:S(2)}) %collective-permute-start.17) | collective-permute-done | bytes 131104 | tf_op jit(solution)/shard_map/ppermute | solution.py:635
  126.9 3.2 %shard_map.121 = f32[50,2,32,64]{3,2,1,0:T(8,128)} custom-call(s32[128]{0:T(128)S(1)} %reshape.68.label_ref, s32[128]{0:T(128)S(1)} %reshape.71.live_ref, f32[50]{0:T(128)S(1)} %maximum_convert_fusion.divisor_ref, bf16[16,32,128]{2,1,0:T(8,128)(2,1)S(1)} %get-tuple-element.32.refs_0_, bf16[16,32,128]{2,1,0:T(8,128)(2,1)S(1)} %collective-permute-done.9.refs_1_, ...), custom_call_target="tpu_custom_call" | custom-call | flops 33554432 | bytes 1869000 | tf_op jit(solution)/shard_map/pallas_call | solution.py:160
  130.1 1.5 %shard_map.116 = f32[128,4096]{1,0:T(8,128)} custom-call(s32[1]{0:T(128)} %bitcast.place_ref, f32[64,4096]{1,0:T(8,128)S(1)} %get-tuple-element.23.own_ref, bf16[64,4096]{1,0:T(8,128)(2,1)S(1)} %collective-permute-done.far_ref, f32[32,128]{1,0:T(8,128)S(1)} %collective-permute-done.1.edge_ref), custom_call_target="tpu_custom_call" | custom-call | flops 524288 | bytes 3686404 | tf_op jit(solution)/shard_map/pallas_call | solution.py:160
  (83 shorter events, 10.4 us)
Async XLA Ops:
  0.6 1.2 copy-start
  4.8 4.4 %copy-start.1 = (bf16[512,1024]{1,0:T(8,128)(2,1)S(1)}, bf16[512,1024]{1,0:T(8,128)(2,1)}, u32[]{:S(2)}) copy-start(bf16[512,1024]{1,0:T(8,128)(2,1)} %x_ref.3) | copy-start | bytes 3145732
  4.8 18.8 %all-to-all-start = ((bf16[4,16,64,128]{3,2,1,0:T(8,128)(2,1)}), bf16[4,16,64,128]{3,2,1,0:T(8,128)(2,1)S(1)}, u32[]{:S(2)}, u32[]{:S(2)}) async-start(bf16[4,16,64,128]{3,2,1,0:T(8,128)(2,1)} %shard_map.113), calls=%async_computation | async-start | bytes 2097152 | tf_op jit(solution)/shard_map/all_to_all | solution.py:568
  10.0 24.4 %copy-start.7 = (s32[8,4,4,2]{0,3,2,1:T(2,128)S(1)}, s32[8,4,4,2]{0,3,2,1:T(2,128)}, u32[]{:S(2)}) copy-start(s32[8,4,4,2]{0,3,2,1:T(2,128)} %param.11) | copy-start | bytes 3076
  10.0 24.0 %collective-permute-start.2 = (bf16[256,1024]{1,0:T(8,128)(2,1)}, bf16[256,1024]{1,0:T(8,128)(2,1)}, u32[]{:S(2)}, u32[]{:S(2)}) collective-permute-start(bf16[256,1024]{1,0:T(8,128)(2,1)} %slice.8), channel_id=1, source_target_pairs={{4,0},{8,4},{12,8},{16,12},{20,16},{24,20},{28,24},{5,1},{9,5},{13... | collective-permute-start | bytes 1572872 | tf_op jit(solution)/shard_map/ppermute | solution.py:25
  11.5 24.9 %collective-permute-start.3 = (bf16[512,1024]{1,0:T(8,128)(2,1)S(1)}, bf16[512,1024]{1,0:T(8,128)(2,1)S(1)}, u32[]{:S(2)}, u32[]{:S(2)}) collective-permute-start(bf16[512,1024]{1,0:T(8,128)(2,1)S(1)} %copy-done.1), channel_id=1, source_target_pairs={{0,1},{1,0},{2,3},{3,2},{4,5},{5,4},{6,7},{7,6},{8,9},{9,8},{10,11... | collective-permute-start | bytes 3145736 | tf_op jit(solution)/shard_map/ppermute | solution.py:527
  28.4 50.4 %all-to-all-start.1 = ((bf16[32,4,32,128]{3,2,1,0:T(8,128)(2,1)}), bf16[32,4,32,128]{3,2,1,0:T(8,128)(2,1)S(1)}, u32[]{:S(2)}, u32[]{:S(2)}) async-start(bf16[32,4,32,128]{3,2,1,0:T(8,128)(2,1)} %shard_map.114), calls=%async_computation.1 | async-start | bytes 2097152 | tf_op jit(solution)/shard_map/all_to_all | solution.py:578
  34.0 8.2 %copy-start.8 = (s32[1,1,4,2]{2,3,1,0:T(2,128)S(1)}, s32[1,1,4,2]{2,3,1,0:T(2,128)}, u32[]{:S(2)}) copy-start(s32[1,1,4,2]{2,3,1,0:T(2,128)} %param.14) | copy-start | bytes 100
  34.1 2.3 %collective-permute-start.4 = (bf16[256,1024]{1,0:T(8,128)(2,1)}, bf16[256,1024]{1,0:T(8,128)(2,1)}, u32[]{:S(2)}, u32[]{:S(2)}) collective-permute-start(bf16[256,1024]{1,0:T(8,128)(2,1)} %collective-permute-done.2.low_ref), channel_id=1, source_target_pairs={{0,1},{1,0},{2,3},{3,2},{4,5},{5,4},{6,7},{7,6},{8,9},{9,8},{10,11... | collective-permute-start | bytes 1572872 | tf_op jit(solution)/shard_map/ppermute | solution.py:527
  39.5 0.8 copy-start.2
  40.3 19.8 %collective-permute-start.5 = (bf16[4,256,256]{2,1,0:T(8,128)(2,1)}, bf16[4,256,256]{2,1,0:T(8,128)(2,1)S(1)}, u32[]{:S(2)}, u32[]{:S(2)}) collective-permute-start(bf16[4,256,256]{2,1,0:T(8,128)(2,1)} %get-tuple-element.27), channel_id=1, source_target_pairs={{0,2},{1,3},{2,0},{3,1},{4,6},{5,7},{6,4},{7,5},{8,10},{9,11},{10,... | collective-permute-start | bytes 1572872 | tf_op jit(solution)/shard_map/ppermute | solution.py:527
  60.1 1.0 copy-start.3
  61.2 9.1 %copy-start.5 = (s32[8,4,4]{0,2,1:T(4,128)S(1)}, s32[8,4,4]{0,2,1:T(4,128)}, u32[]{:S(2)}) copy-start(s32[8,4,4]{0,2,1:T(4,128)} %param.12) | copy-start | bytes 1540
  61.2 9.3 %copy-start.6 = (s32[8,4,4]{0,2,1:T(4,128)S(1)}, s32[8,4,4]{0,2,1:T(4,128)}, u32[]{:S(2)}) copy-start(s32[8,4,4]{0,2,1:T(4,128)} %param.13) | copy-start | bytes 1540
  67.8 4.8 %collective-permute-start.6 = (bf16[4,4,32,128]{3,2,1,0:T(8,128)(2,1)S(1)}, bf16[4,4,32,128]{3,2,1,0:T(8,128)(2,1)S(1)}, u32[]{:S(2)}, u32[]{:S(2)}) collective-permute-start(bf16[4,4,32,128]{3,2,1,0:T(8,128)(2,1)S(1)} %get-tuple-element.29), channel_id=1, source_target_pairs={{0,1},{1,0},{2,3},{3,2},{4,5},{5,4},{6,7},{7,6},{8,9},{9,8},{10,11... | collective-permute-start | bytes 393224 | tf_op jit(solution)/shard_map/ppermute | solution.py:622
  67.9 6.4 %collective-permute-start.7 = (bf16[4,4,32,128]{3,2,1,0:T(8,128)(2,1)S(1)}, bf16[4,4,32,128]{3,2,1,0:T(8,128)(2,1)S(1)}, u32[]{:S(2)}, u32[]{:S(2)}) collective-permute-start(bf16[4,4,32,128]{3,2,1,0:T(8,128)(2,1)S(1)} %get-tuple-element.30), channel_id=1, source_target_pairs={{0,2},{1,3},{2,0},{3,1},{4,6},{5,7},{6,4},{7,5},{8,10},{9,11},{10,... | collective-permute-start | bytes 393224 | tf_op jit(solution)/shard_map/ppermute | solution.py:622
  68.9 7.2 %collective-permute-start.8 = (bf16[4,4,32,128]{3,2,1,0:T(8,128)(2,1)S(1)}, bf16[4,4,32,128]{3,2,1,0:T(8,128)(2,1)S(1)}, u32[]{:S(2)}, u32[]{:S(2)}) collective-permute-start(bf16[4,4,32,128]{3,2,1,0:T(8,128)(2,1)S(1)} %get-tuple-element.31), channel_id=1, source_target_pairs={{0,3},{1,2},{2,1},{3,0},{4,7},{5,6},{6,5},{7,4},{8,11},{9,10},{10,... | collective-permute-start | bytes 393224 | tf_op jit(solution)/shard_map/ppermute | solution.py:622
  70.8 12.1 %collective-permute-start.12 = (bf16[4,4,32,128]{3,2,1,0:T(8,128)(2,1)}, bf16[4,4,32,128]{3,2,1,0:T(8,128)(2,1)S(1)}, u32[]{:S(2)}, u32[]{:S(2)}) collective-permute-start(bf16[4,4,32,128]{3,2,1,0:T(8,128)(2,1)} %get-tuple-element.36), channel_id=1, source_target_pairs={{0,4},{1,5},{2,6},{3,7},{4,0},{5,1},{6,2},{7,3},{8,12},{9,13},{10,... | collective-permute-start | bytes 393224 | tf_op jit(solution)/shard_map/ppermute | solution.py:622
  72.3 12.8 %collective-permute-start.13 = (bf16[4,4,32,128]{3,2,1,0:T(8,128)(2,1)}, bf16[4,4,32,128]{3,2,1,0:T(8,128)(2,1)S(1)}, u32[]{:S(2)}, u32[]{:S(2)}) collective-permute-start(bf16[4,4,32,128]{3,2,1,0:T(8,128)(2,1)} %get-tuple-element.37), channel_id=1, source_target_pairs={{0,5},{1,4},{2,7},{3,6},{4,1},{5,0},{6,3},{7,2},{8,13},{9,12},{10,... | collective-permute-start | bytes 393224 | tf_op jit(solution)/shard_map/ppermute | solution.py:622
  72.6 14.4 %collective-permute-start.14 = (bf16[4,4,32,128]{3,2,1,0:T(8,128)(2,1)}, bf16[4,4,32,128]{3,2,1,0:T(8,128)(2,1)S(1)}, u32[]{:S(2)}, u32[]{:S(2)}) collective-permute-start(bf16[4,4,32,128]{3,2,1,0:T(8,128)(2,1)} %get-tuple-element.38), channel_id=1, source_target_pairs={{0,6},{1,7},{2,4},{3,5},{4,2},{5,3},{6,0},{7,1},{8,14},{9,15},{10,... | collective-permute-start | bytes 393224 | tf_op jit(solution)/shard_map/ppermute | solution.py:622
  74.3 14.8 %collective-permute-start.15 = (bf16[4,4,32,128]{3,2,1,0:T(8,128)(2,1)S(1)}, bf16[4,4,32,128]{3,2,1,0:T(8,128)(2,1)S(1)}, u32[]{:S(2)}, u32[]{:S(2)}) collective-permute-start(bf16[4,4,32,128]{3,2,1,0:T(8,128)(2,1)S(1)} %get-tuple-element.39), channel_id=1, source_target_pairs={{0,7},{1,6},{2,5},{3,4},{4,3},{5,2},{6,1},{7,0},{8,15},{9,14},{10,... | collective-permute-start | bytes 393224 | tf_op jit(solution)/shard_map/ppermute | solution.py:622
  76.8 13.1 %collective-permute-start.9 = (bf16[16,32,128]{2,1,0:T(8,128)(2,1)}, bf16[16,32,128]{2,1,0:T(8,128)(2,1)S(1)}, u32[]{:S(2)}, u32[]{:S(2)}) collective-permute-start(bf16[16,32,128]{2,1,0:T(8,128)(2,1)} %get-tuple-element.33), channel_id=1, source_target_pairs={{0,8},{1,9},{2,10},{3,11},{4,12},{5,13},{6,14},{7,15},{8,16},{9,17... | collective-permute-start | bytes 393224 | tf_op jit(solution)/shard_map/ppermute | solution.py:635
  78.8 10.3 %copy-start.9 = (s32[4]{0:T(128)S(1)}, s32[4]{0:T(128)}, u32[]{:S(2)}) copy-start(s32[4]{0:T(128)} %compare_select_fusion.1) | copy-start | bytes 52
  82.9 4.1 %copy-start.4 = (f32[32,128]{1,0:T(8,128)}, f32[32,128]{1,0:T(8,128)S(1)}, u32[]{:S(2)}) copy-start(f32[32,128]{1,0:T(8,128)S(1)} %get-tuple-element.25) | copy-start | bytes 49156
  82.9 21.8 %collective-permute-start.10 = (bf16[16,32,128]{2,1,0:T(8,128)(2,1)}, bf16[16,32,128]{2,1,0:T(8,128)(2,1)S(1)}, u32[]{:S(2)}, u32[]{:S(2)}) collective-permute-start(bf16[16,32,128]{2,1,0:T(8,128)(2,1)} %get-tuple-element.34), channel_id=1, source_target_pairs={{0,16},{1,17},{2,18},{3,19},{4,20},{5,21},{6,22},{7,23},{8,24},{9,... | collective-permute-start | bytes 393224 | tf_op jit(solution)/shard_map/ppermute | solution.py:635
  85.1 45.0 %collective-permute-start = (bf16[64,4096]{1,0:T(8,128)(2,1)S(1)}, bf16[64,4096]{1,0:T(8,128)(2,1)S(1)}, u32[]{:S(2)}, u32[]{:S(2)}) collective-permute-start(bf16[64,4096]{1,0:T(8,128)(2,1)S(1)} %get-tuple-element.24), channel_id=1, source_target_pairs={{0,31},{1,30},{2,29},{3,28},{4,27},{5,26},{6,25},{7,24},{8,23},{9,... | collective-permute-start | bytes 1572872 | tf_op jit(solution)/shard_map/ppermute | solution.py:660
  87.0 22.6 %collective-permute-start.11 = (bf16[16,32,128]{2,1,0:T(8,128)(2,1)}, bf16[16,32,128]{2,1,0:T(8,128)(2,1)S(1)}, u32[]{:S(2)}, u32[]{:S(2)}) collective-permute-start(bf16[16,32,128]{2,1,0:T(8,128)(2,1)} %get-tuple-element.35), channel_id=1, source_target_pairs={{0,24},{1,25},{2,26},{3,27},{4,28},{5,29},{6,30},{7,31},{8,0},{9,1... | collective-permute-start | bytes 393224 | tf_op jit(solution)/shard_map/ppermute | solution.py:635
  89.9 26.8 %collective-permute-start.16 = (bf16[16,32,128]{2,1,0:T(8,128)(2,1)}, bf16[16,32,128]{2,1,0:T(8,128)(2,1)S(1)}, u32[]{:S(2)}, u32[]{:S(2)}) collective-permute-start(bf16[16,32,128]{2,1,0:T(8,128)(2,1)} %get-tuple-element.41), channel_id=1, source_target_pairs={{0,8},{1,9},{2,10},{3,11},{4,12},{5,13},{6,14},{7,15},{8,16},{9,17... | collective-permute-start | bytes 393224 | tf_op jit(solution)/shard_map/ppermute | solution.py:635
  89.9 37.0 %collective-permute-start.17 = (bf16[16,32,128]{2,1,0:T(8,128)(2,1)}, bf16[16,32,128]{2,1,0:T(8,128)(2,1)S(1)}, u32[]{:S(2)}, u32[]{:S(2)}) collective-permute-start(bf16[16,32,128]{2,1,0:T(8,128)(2,1)} %get-tuple-element.42), channel_id=1, source_target_pairs={{0,16},{1,17},{2,18},{3,19},{4,20},{5,21},{6,22},{7,23},{8,24},{9,... | collective-permute-start | bytes 393224 | tf_op jit(solution)/shard_map/ppermute | solution.py:635
  104.7 22.2 %collective-permute-start.18 = (bf16[16,32,128]{2,1,0:T(8,128)(2,1)S(1)}, bf16[16,32,128]{2,1,0:T(8,128)(2,1)S(1)}, u32[]{:S(2)}, u32[]{:S(2)}) collective-permute-start(bf16[16,32,128]{2,1,0:T(8,128)(2,1)S(1)} %get-tuple-element.43), channel_id=1, source_target_pairs={{0,24},{1,25},{2,26},{3,27},{4,28},{5,29},{6,30},{7,31},{8,0},{9,1... | collective-permute-start | bytes 393224 | tf_op jit(solution)/shard_map/ppermute | solution.py:635
  109.6 20.4 %collective-permute-start.1 = (f32[32,128]{1,0:T(8,128)}, f32[32,128]{1,0:T(8,128)S(1)}, u32[]{:S(2)}, u32[]{:S(2)}) collective-permute-start(f32[32,128]{1,0:T(8,128)} %copy-done.4), channel_id=1, source_target_pairs={{4,31},{8,27},{12,23},{16,19},{20,15},{24,11},{28,7},{1,3},{5,30},... | collective-permute-start | bytes 49160 | tf_op jit(solution)/shard_map/ppermute | solution.py:663
